TPU v7x, 32 devices: a whole 2x2x4 slice. The times are simulated.
32 devices in a mesh: qa: 16 (over z, x, core), qb: 2 (over y).
Axes of the slice: x: 2, y: 2, z: 4, core: 2. Of those that a mesh axis runs over, the one named last changes fastest.
Arguments:
- wave_parts: float32 [2, 256, 128, 128], P(None, ('qa', 'qb')), may hold values from -6 to 6
- level_table: float32 [256, 128, 128], P(('qa', 'qb')), may hold values from -2 to 2
- phase_angles: float32 [2, 128], replicated, may hold values from 0.3 to 1.2
Outputs:
- final_parts: float32 [2, 256, 128, 128], P(None, ('qa', 'qb'))
All inputs are finite; a program needn't handle non-finite values.
Results may differ from a plain program's by a relative error of at most 0.0003.
Values sent between devices are 32-bit elements; how exact they have to be, the bound alone decides.
No kernel may reach another device: no remote copies, remote signals or barrier semaphores. Data moves between devices by JAX's collectives and lax.ppermute only.
A program may use at most 64 MiB of HBM per device.

v0:
```python
import jax
import jax.numpy as jnp
from jax import lax
from jax.sharding import PartitionSpec as P

LAYERS = 2


def count_bits(values, count):
    places = jnp.arange(count.bit_length() - 1, dtype=jnp.int32)
    return jnp.sum(values[..., None] >> places & 1, axis=-1)


def sign_table(count):
    rank = jnp.arange(count, dtype=jnp.int32)
    parity = count_bits(rank[:, None] & rank[None, :], count) % 2
    real_part = jnp.where(parity == 1, -1.0, 1.0).astype(jnp.float32) * count ** (-0.5)
    return real_part


def turn_dim(values, dim):
    real_part = sign_table(values.shape[dim])
    moved = jnp.tensordot(values, real_part, axes=([dim], [0]), precision=lax.Precision.HIGHEST)
    return jnp.moveaxis(moved, -1, dim)


def turn_phase(values, levels, angle):
    turn = angle * levels
    return jnp.stack(
        [
            values[0] * jnp.cos(turn) + values[1] * jnp.sin(turn),
            values[1] * jnp.cos(turn) - values[0] * jnp.sin(turn),
        ]
    )


def body(wave_parts, level_table, phase_angles):
    values = wave_parts
    for layer in range(LAYERS):
        values = turn_phase(values, level_table, phase_angles[layer])
        values = turn_dim(values, 3)
        values = turn_dim(values, 2)
        moved = lax.all_to_all(values, "qa", split_axis=2, concat_axis=1, tiled=True)
        moved = turn_dim(moved, 1)
        values = lax.all_to_all(moved, "qa", split_axis=1, concat_axis=2, tiled=True)
        moved = lax.all_to_all(values, "qb", split_axis=3, concat_axis=1, tiled=True)
        spread = moved.reshape(2, lax.axis_size("qb"), -1, moved.shape[2], moved.shape[3])
        moved = turn_dim(spread, 1).reshape(moved.shape)
        values = lax.all_to_all(moved, "qb", split_axis=1, concat_axis=3, tiled=True)
    return values


def solution(mesh):
    in_specs = (P(None, ("qa", "qb"), None, None), P(("qa", "qb"), None, None), P())
    out_specs = P(None, ("qa", "qb"), None, None)
    return jax.shard_map(body, mesh=mesh, in_specs=in_specs, out_specs=out_specs, check_vma=False)
```

profile of v0, /device:TPU:0, one launch (start us, length us, event | category | flops | bytes accessed | tf_op | source)
XLA Modules:
  0.0 216.1 jit_solution(5427155283323233087)
XLA Ops:
  0.0 0.0 copy-start.1
  0.0 0.7 copy-done.1
  0.8 3.1 %fusion.15 = (f32[1,8,128,128]{3,2,1,0:T(8,128)S(1)}, f32[1,8,128,128]{3,2,1,0:T(8,128)S(1)}) fusion(f32[2,8,128,128]{3,2,1,0:T(8,128)} %param.3, f32[8,128,128]{2,1,0:T(8,128)} %param.4, f32[128]{0:T(128)S(1)} %get-tuple-element.12), kind=kLoop, calls=%fused_computation.25 | loop fusion | flops 917504 | bytes 2621952 | tf_op jit(solution)/shard_map/stack | solution.py:29
  3.9 1.1 fusion
  5.0 1.0 convolution_bitcast_fusion.5
  6.0 0.5 copy.64
  6.5 31.9 %all_to_all.135 = f32[2,8,128,128]{3,1,0,2:T(8,128)S(1)} all-to-all(f32[2,8,128,128]{3,1,0,2:T(8,128)S(1)} %copy.64), channel_id=1, replica_groups=mesh['qa'=16,'qb'=2] {'qa'}, dimensions={2} | all-to-all | bytes 2097152 | tf_op jit(solution)/shard_map/all_to_all | solution.py:43
  38.3 0.3 copy.66
  38.7 1.8 convolution_bitcast_fusion.4
  40.5 0.5 copy.68
  41.0 29.5 %all_to_all.136 = f32[2,128,8,128]{3,2,0,1:T(8,128)S(1)} all-to-all(f32[2,128,8,128]{3,2,0,1:T(8,128)S(1)} %copy.68), channel_id=1, replica_groups=mesh['qa'=16,'qb'=2] {'qa'}, dimensions={1} | all-to-all | bytes 2097152 | tf_op jit(solution)/shard_map/all_to_all | solution.py:45
  70.5 0.1 copy.129
  70.6 0.5 copy.71
  71.1 17.5 %all_to_all.137 = f32[2,8,128,128]{2,1,0,3:T(8,128)S(1)} all-to-all(f32[2,8,128,128]{2,1,0,3:T(8,128)S(1)} %copy.71), channel_id=1, replica_groups=mesh['qa'=16,'qb'=2] {'qb'}, dimensions={3} | all-to-all | bytes 2097152 | tf_op jit(solution)/shard_map/all_to_all | solution.py:46
  88.6 4.0 %convolution_bitcast_fusion.1 = f32[2,2,8,128,64]{3,1,4,2,0:T(2,128)S(1)} fusion(f32[2,8,128,2,64]{2,1,0,4,3:T(8,128)S(1)} %bitcast.112), kind=kOutput, calls=%fused_computation.1 | convolution fusion | flops 6291524 | bytes 2097152 | tf_op jit(solution)/shard_map/dot_general | solution.py:23
  92.6 0.1 copy.107
  92.7 16.5 %all_to_all.138 = f32[2,16,128,64]{2,3,0,1:T(8,128)S(1)} all-to-all(f32[2,16,128,64]{2,3,0,1:T(8,128)S(1)} %bitcast.113), channel_id=1, replica_groups=mesh['qa'=16,'qb'=2] {'qb'}, dimensions={1} | all-to-all | bytes 2097152 | tf_op jit(solution)/shard_map/all_to_all | solution.py:49
  109.2 0.1 copy.76
  109.3 0.1 fusion.87
  109.4 0.2 copy.80
  109.7 0.0 copy-start
  109.7 0.2 copy.78
  109.9 0.8 copy-done
  110.7 2.0 add_bitcast_fusion
  112.7 1.1 fusion.4
  113.9 1.0 convolution_bitcast_fusion.3
  114.8 0.5 copy.84
  115.3 28.4 %all_to_all.139 = f32[2,8,128,128]{3,1,0,2:T(8,128)S(1)} all-to-all(f32[2,8,128,128]{3,1,0,2:T(8,128)S(1)} %copy.84), channel_id=1, replica_groups=mesh['qa'=16,'qb'=2] {'qa'}, dimensions={2} | all-to-all | bytes 2097152 | tf_op jit(solution)/shard_map/all_to_all | solution.py:43
  143.7 0.3 copy.86
  144.1 1.8 convolution_bitcast_fusion.2
  145.9 0.5 copy.88
  146.4 29.5 %all_to_all.140 = f32[2,128,8,128]{3,2,0,1:T(8,128)S(1)} all-to-all(f32[2,128,8,128]{3,2,0,1:T(8,128)S(1)} %copy.88), channel_id=1, replica_groups=mesh['qa'=16,'qb'=2] {'qa'}, dimensions={1} | all-to-all | bytes 2097152 | tf_op jit(solution)/shard_map/all_to_all | solution.py:45
  175.9 0.1 copy.128
  176.0 0.5 copy.91
  176.5 17.5 %all_to_all.141 = f32[2,8,128,128]{2,1,0,3:T(8,128)S(1)} all-to-all(f32[2,8,128,128]{2,1,0,3:T(8,128)S(1)} %copy.91), channel_id=1, replica_groups=mesh['qa'=16,'qb'=2] {'qb'}, dimensions={3} | all-to-all | bytes 2097152 | tf_op jit(solution)/shard_map/all_to_all | solution.py:46
  194.0 4.0 %convolution_bitcast_fusion = f32[2,2,8,128,64]{3,1,4,2,0:T(2,128)S(1)} fusion(f32[2,8,128,2,64]{2,1,0,4,3:T(8,128)S(1)} %bitcast.117), kind=kOutput, calls=%fused_computation | convolution fusion | flops 6291524 | bytes 2097152 | tf_op jit(solution)/shard_map/dot_general | solution.py:23
  198.0 0.1 copy.112
  198.1 16.6 %all_to_all.142 = f32[2,16,128,64]{2,3,0,1:T(8,128)S(1)} all-to-all(f32[2,16,128,64]{2,3,0,1:T(8,128)S(1)} %bitcast.118), channel_id=1, replica_groups=mesh['qa'=16,'qb'=2] {'qb'}, dimensions={1} | all-to-all | bytes 2097152 | tf_op jit(solution)/shard_map/all_to_all | solution.py:49
  214.7 0.1 copy.97
  214.8 1.3 copy.98
  (6 shorter events, 0.2 us)
Async XLA Ops:
  0.0 0.7 copy-start.1
  109.7 1.0 copy-start
where the time goes:
time: 217 us; the launch traced here: 216 us
  blocking collectives  187 us (86%)
  matrix products  15.7 us (7%)
  local copies, waits for them, and re-layouts  7.69 us (4%)
  other arithmetic  5.19 us (2%)
    all_to_all x2, blocking collectives, body(): lax.all_to_all(values, 'qa', split_axis=2, concat_axis=1, tiled=True)  60.2 us
    all_to_all x2, blocking collectives, body(): lax.all_to_all(moved, 'qa', split_axis=1, concat_axis=2, tiled=True)  59 us
    all_to_all x2, blocking collectives, body(): lax.all_to_all(values, 'qb', split_axis=3, concat_axis=1, tiled=True)  34.9 us
    all_to_all x2, blocking collectives, body(): lax.all_to_all(moved, 'qb', split_axis=1, concat_axis=3, tiled=True)  33.1 us
    dot_general x8, matrix products, turn_dim(): jnp.tensordot(values, real_part, axes=([dim], [0]), precision=lax.Precisi...  15.7 us
    another operation x2, other arithmetic, turn_phase(): jnp.stack([values[0] * jnp.cos(turn) + values[1] * jnp.sin(turn), values[...  5.09 us

commit v1 on v0

v1 whole, which is shorter than its diff:
```python
import functools

import jax
import jax.numpy as jnp
from jax import lax
from jax.experimental import pallas as pl
from jax.experimental.pallas import tpu as pltpu
from jax.sharding import PartitionSpec as P

COS = (0.99999999952702, -0.49999999256864713, 0.04166664759095227, -0.0013888705067900038,
       2.4793136218611696e-05, -2.735711629719697e-07, 1.8502809653875554e-09)
SIN = (0.9999999999681006, -0.16666666616558576, 0.008333332047516205, -0.00019841145991402124,
       2.75516291724042e-06, -2.4917466240452868e-08, 1.446608995457697e-10)


def poly(coefs, t):
    total = jnp.full_like(t, coefs[-1])
    for c in coefs[-2::-1]:
        total = total * t + c
    return total


def turn(real, imag, levels, angle, scale):
    x = angle * levels
    t = x * x
    c = poly(COS, t) * scale
    s = x * poly(SIN, t) * scale
    return real * c + imag * s, imag * c - real * s


def butterflies(values):
    values = list(values)
    step = 1
    while step < len(values):
        for i in range(len(values)):
            if not i & step:
                u, v = values[i], values[i + step]
                values[i], values[i + step] = u + v, u - v
        step *= 2
    return values


def signs(count, dtype):
    rank = lax.broadcasted_iota(jnp.int32, (count, count), 0) & lax.broadcasted_iota(jnp.int32, (count, count), 1)
    parity = rank
    shift = 1
    while shift < count:
        parity = parity ^ (parity >> shift)
        shift *= 2
    return (1 - 2 * (parity & 1)).astype(dtype)


def split(x, axis):
    high = x.astype(jnp.bfloat16)
    low = (x - high.astype(jnp.float32)).astype(jnp.bfloat16)
    return jnp.concatenate([high, low], axis=axis)


def tile_turn(x, right, left):
    y = jnp.dot(split(x, 1), right, preferred_element_type=jnp.float32)
    return jnp.dot(left, split(y, 0), preferred_element_type=jnp.float32)


def first_kernel(devices, part, scale, wave_ref, level_ref, angle_ref, out_ref):
    tiles = part // 8
    angle = jnp.broadcast_to(angle_ref[0:1, :], (8, wave_ref.shape[2]))

    def step(tile, _):
        for d in range(devices):
            rows = pl.ds(pl.multiple_of(d * part + tile * 8, 8), 8)
            levels = level_ref[rows, :]
            real, imag = turn(wave_ref[0, rows, :], wave_ref[1, rows, :], levels, angle, scale)
            here = pl.ds(pl.multiple_of(tile * 8, 8), 8)
            out_ref[d, 0, here, :] = real
            out_ref[d, 1, here, :] = imag
            out_ref[d, 2, here, :] = levels
        for p in range(2):
            here = pl.ds(pl.multiple_of(tile * 8, 8), 8)
            values = butterflies([out_ref[d, p, here, :] for d in range(devices)])
            for d in range(devices):
                out_ref[d, p, here, :] = values[d]
        return 0

    lax.fori_loop(0, tiles, step, 0)


def middle_kernel(devices, part, scale, in_ref, angle_ref, right_ref, left_ref, out_ref, held):
    lanes = in_ref.shape[3]
    size = left_ref.shape[0]
    per = size // part
    groups = devices // per
    right, left = right_ref[...], left_ref[...]
    for p in range(2):
        for g in range(groups):
            x = in_ref[g * per:(g + 1) * per, p].reshape(size, lanes)
            held[p, g * size:(g + 1) * size] = tile_turn(x, right, left)
    angle = jnp.broadcast_to(angle_ref[1:2, :], (8, lanes))

    def step(tile, _):
        rows = [pl.ds(pl.multiple_of(g * size + tile * 8, 8), 8) for g in range(groups)]
        real = butterflies([held[0, r, :] for r in rows])
        imag = butterflies([held[1, r, :] for r in rows])
        for g in range(groups):
            first = (g * size + tile * 8) // part
            offset = pl.multiple_of((tile * 8) % part, 8)
            levels = in_ref[first, 2, pl.ds(offset, 8), :]
            real[g], imag[g] = turn(real[g], imag[g], levels, angle, scale)
        for p, values in enumerate((real, imag)):
            for r, value in zip(rows, butterflies(values)):
                held[p, r, :] = value
        return 0

    lax.fori_loop(0, size // 8, step, 0)
    for p in range(2):
        for g in range(groups):
            y = tile_turn(held[p, g * size:(g + 1) * size], right, left)
            out_ref[g * per:(g + 1) * per, p] = y.reshape(per, part, lanes)


def last_kernel(devices, part, in_ref, out_ref):
    def step(tile, _):
        for p in range(2):
            here = pl.ds(pl.multiple_of(tile * 8, 8), 8)
            values = butterflies([in_ref[d, p, here, :] for d in range(devices)])
            for d in range(devices):
                rows = pl.ds(pl.multiple_of(d * part + tile * 8, 8), 8)
                out_ref[p, rows, :] = values[d]
        return 0

    lax.fori_loop(0, part // 8, step, 0)


def call(kernel, shape, scratch=()):
    return pl.pallas_call(
        kernel,
        out_shape=jax.ShapeDtypeStruct(shape, jnp.float32),
        scratch_shapes=list(scratch),
    )


def body_fast(axes, devices, wave, levels, angles):
    blocks, rows, lanes = levels.shape
    total = blocks * rows
    part = total // devices
    scale = float(devices * total * lanes) ** -0.5
    wave = wave.reshape(2, total, lanes)
    levels = levels.reshape(total, lanes)
    sent = call(functools.partial(first_kernel, devices, part, scale), (devices, 3, part, lanes))(wave, levels, angles)
    seen = lax.all_to_all(sent, axes, 0, 0, tiled=True)
    sign = signs(lanes, jnp.bfloat16)
    right = jnp.concatenate([sign, sign], axis=0)
    sign = signs(128, jnp.bfloat16)
    left = jnp.concatenate([sign, sign], axis=1)
    back = call(
        functools.partial(middle_kernel, devices, part, scale), (devices, 2, part, lanes),
        [pltpu.VMEM((2, total, lanes), jnp.float32)],
    )(seen, angles, right, left)
    back = lax.all_to_all(back, axes, 0, 0, tiled=True)
    out = call(functools.partial(last_kernel, devices, part), (2, total, lanes))(back)
    return out.reshape(2, blocks, rows, lanes)


def walsh(values, dim):
    count = values.shape[dim]
    moved = jnp.tensordot(values, signs(count, jnp.float32), axes=([dim], [0]), precision=lax.Precision.HIGHEST)
    return jnp.moveaxis(moved, -1, dim) * count ** -0.5


def body_plain(axes, devices, wave, levels, angles):
    blocks, rows, lanes = levels.shape
    part = blocks * rows // devices
    values = wave.reshape(2, devices, part, lanes)
    levels = levels.reshape(devices, part, lanes)
    x = angles[0] * levels
    c, s = jnp.cos(x), jnp.sin(x)
    values = jnp.stack([values[0] * c + values[1] * s, values[1] * c - values[0] * s], axis=1)
    values = walsh(values, 0)
    values = lax.all_to_all(values, axes, 0, 0, tiled=True)
    levels = lax.all_to_all(levels, axes, 0, 0, tiled=True)
    for dim in (0, 2, 3):
        values = walsh(values, dim)
    x = angles[1] * levels
    c, s = jnp.cos(x), jnp.sin(x)
    values = jnp.stack([values[:, 0] * c + values[:, 1] * s, values[:, 1] * c - values[:, 0] * s], axis=1)
    for dim in (0, 2, 3):
        values = walsh(values, dim)
    values = lax.all_to_all(values, axes, 0, 0, tiled=True)
    values = walsh(values, 0)
    return jnp.moveaxis(values, 1, 0).reshape(wave.shape)


def solution(mesh):
    axes = ("qa", "qb")
    devices = mesh.shape["qa"] * mesh.shape["qb"]

    def body(wave, levels, angles):
        total = levels.shape[0] * levels.shape[1]
        part = total // devices
        fast = part % 8 == 0 and 128 % part == 0 and total % 128 == 0
        return (body_fast if fast else body_plain)(axes, devices, wave, levels, angles)

    in_specs = (P(None, axes, None, None), P(axes, None, None), P())
    return jax.shard_map(body, mesh=mesh, in_specs=in_specs, out_specs=in_specs[0], check_vma=False)
```

time: 217 us -> 87.5 us (0.40)
  blocking collectives: 187 us -> 29.9 us
  waiting for transfers between devices: 0 us -> 36.1 us
  matrix products: 15.7 us -> 0 us
  Pallas kernels: 0 us -> 11.2 us
  starting transfers between devices: 0 us -> 7.33 us
  local copies, waits for them, and re-layouts: 7.69 us -> 1.17 us
  other arithmetic: 5.19 us -> 1.3 us
    all_to_all x8 -> x1, blocking collectives: 187 us -> 29.9 us  [body_fast(): back = lax.all_to_all(back, axes, 0, 0, tiled=True)]
    all_to_all x0 -> x1, waiting for transfers between devices: none -> 36.1 us  [body_fast(): seen = lax.all_to_all(sent, axes, 0, 0, tiled=True)]
    dot_general x8 -> x0, matrix products: 15.7 us -> none  [turn_dim(): jnp.tensordot(values, real_part, axes=([dim], [0]), precision=lax.Precisi...]
    pallas_call x0 -> x3, Pallas kernels: none -> 11.2 us  [the longest x1 5.3 us: body_fast(): call(functools.partial(middle_kernel, devices, part, scale), (devices, 2,...]
    all_to_all x0 -> x1, starting transfers between devices: none -> 7.33 us  [body_fast(): seen = lax.all_to_all(sent, axes, 0, 0, tiled=True)]
    another operation x2 -> x0, other arithmetic: 5.09 us -> none  [turn_phase(): jnp.stack([values[0] * jnp.cos(turn) + values[1] * jnp.sin(turn), values[...]
    all_to_all x9 -> x0, local copies, waits for them, and re-layouts: 3.37 us -> none  [the longest x3 1.48 us: body(): lax.all_to_all(moved, 'qb', split_axis=1, concat_axis=3, tiled=True)]
  transfers between devices with their start and end apart: 0 -> 1, of which waited for: 0 -> 1; matrix products, arithmetic and copies ran while one was open for 0% -> 1% of each run, Pallas kernels for 0% -> 0%
where the time goes in v1:
time: 87.5 us; the launch traced here: 87.1 us
  waiting for transfers between devices  36.1 us (41%)
  blocking collectives  29.9 us (34%)
  Pallas kernels  11.2 us (13%)
  starting transfers between devices  7.33 us (8%)
  other arithmetic  1.3 us (1%)
  local copies, waits for them, and re-layouts  1.17 us (1%)
    all_to_all x1, waiting for transfers between devices, body_fast(): seen = lax.all_to_all(sent, axes, 0, 0, tiled=True)  36.1 us
    all_to_all x1, blocking collectives, body_fast(): back = lax.all_to_all(back, axes, 0, 0, tiled=True)  29.9 us
    all_to_all x1, starting transfers between devices, body_fast(): seen = lax.all_to_all(sent, axes, 0, 0, tiled=True)  7.33 us
    pallas_call x1, Pallas kernels, body_fast(): call(functools.partial(middle_kernel, devices, part, scale), (devices, 2,...  5.3 us
    pallas_call x1, Pallas kernels, body_fast(): call(functools.partial(first_kernel, devices, part, scale), (devices, 3,...  3.43 us
    pallas_call x1, Pallas kernels, body_fast(): call(functools.partial(last_kernel, devices, part), (2, total, lanes))(back)  2.51 us
  transfers between devices with their start and end apart: 1, of which 1 were waited for; matrix products, arithmetic and copies ran while one was open for 1% of the time, Pallas kernels for 0%

profile of v1, /device:TPU:0, one launch (start us, length us, event | category | flops | bytes accessed | tf_op | source)
XLA Modules:
  0.0 87.1 jit_solution(343468315644303710)
XLA Ops:
  0.0 3.4 %shard_map.37 = f32[32,3,32,128]{3,2,1,0:T(8,128)} custom-call(f32[2,1024,128]{2,1,0:T(8,128)} %bitcast.3, f32[1024,128]{1,0:T(8,128)} %bitcast.4, f32[2,128]{1,0:T(2,128)} %angle_ref.3), custom_call_target="tpu_custom_call" | custom-call | tf_op jit(solution)/shard_map/pallas_call | solution.py:148
  3.4 7.3 %all-to-all-start = ((f32[32,3,32,128]{3,2,1,0:T(8,128)}), f32[32,3,32,128]{3,2,1,0:T(8,128)S(1)}, u32[]{:S(2)}, u32[]{:S(2)}) async-start(f32[32,3,32,128]{3,2,1,0:T(8,128)} %shard_map.37), calls=%async_computation | async-start | bytes 3145728 | tf_op jit(solution)/shard_map/all_to_all | solution.py:149
  10.8 0.1 fusion.3
  10.8 0.6 pad_maximum_fusion.right_ref
  11.4 0.6 pad_maximum_fusion.1.left_ref
  12.1 36.1 %all-to-all-done.in_ref = f32[32,3,32,128]{3,2,1,0:T(8,128)S(1)} async-done(((f32[32,3,32,128]{3,2,1,0:T(8,128)}), f32[32,3,32,128]{3,2,1,0:T(8,128)S(1)}, u32[]{:S(2)}, u32[]{:S(2)}) %all-to-all-start) | async-done | bytes 1572896 | tf_op jit(solution)/shard_map/all_to_all | solution.py:149
  48.2 0.0 copy-start
  48.2 1.2 %copy-done = f32[32,3,32,128]{3,2,1,0:T(8,128)} copy-done((f32[32,3,32,128]{3,2,1,0:T(8,128)}, f32[32,3,32,128]{3,2,1,0:T(8,128)S(1)}, u32[]{:S(2)}) %copy-start) | copy-done | bytes 1572888
  49.4 5.3 %shard_map.38 = f32[32,2,32,128]{3,2,1,0:T(8,128)} custom-call(f32[32,3,32,128]{3,2,1,0:T(8,128)} %copy-done, f32[2,128]{1,0:T(2,128)} %angle_ref.3, bf16[256,128]{1,0:T(8,128)(2,1)} %pad_maximum_fusion.right_ref, bf16[128,256]{1,0:T(8,128)(2,1)} %pad_maximum_fusion.1.left_ref), custom_call_target="tpu_custom_call" | custom-call | tf_op jit(solution)/shard_map/pallas_call | solution.py:154
  54.7 29.9 %all_to_all.10.in_ref = f32[32,2,32,128]{3,2,1,0:T(8,128)} all-to-all(f32[32,2,32,128]{3,2,1,0:T(8,128)} %shard_map.38), channel_id=1, replica_groups=mesh['qa'=16,'qb'=2] {'qa','qb'}, dimensions={0} | all-to-all | bytes 2097152 | tf_op jit(solution)/shard_map/all_to_all | solution.py:158
  84.6 2.5 %shard_map.39 = f32[2,1024,128]{2,1,0:T(8,128)} custom-call(f32[32,2,32,128]{3,2,1,0:T(8,128)} %all_to_all.10.in_ref), custom_call_target="tpu_custom_call" | custom-call | tf_op jit(solution)/shard_map/pallas_call | solution.py:159
Async XLA Ops:
  3.4 44.8 %all-to-all-start = ((f32[32,3,32,128]{3,2,1,0:T(8,128)}), f32[32,3,32,128]{3,2,1,0:T(8,128)S(1)}, u32[]{:S(2)}, u32[]{:S(2)}) async-start(f32[32,3,32,128]{3,2,1,0:T(8,128)} %shard_map.37), calls=%async_computation | async-start | bytes 3145728 | tf_op jit(solution)/shard_map/all_to_all | solution.py:149
  48.2 1.2 %copy-start = (f32[32,3,32,128]{3,2,1,0:T(8,128)}, f32[32,3,32,128]{3,2,1,0:T(8,128)S(1)}, u32[]{:S(2)}) copy-start(f32[32,3,32,128]{3,2,1,0:T(8,128)S(1)} %all-to-all-done.in_ref) | copy-start | bytes 4718596

commit v2 on v1

--- a/solution.py
+++ b/solution.py
@@ -6,6 +6,7 @@
 from jax.experimental import pallas as pl
 from jax.experimental.pallas import tpu as pltpu
 from jax.sharding import PartitionSpec as P
+
 
 COS = (0.99999999952702, -0.49999999256864713, 0.04166664759095227, -0.0013888705067900038,
        2.4793136218611696e-05, -2.735711629719697e-07, 1.8502809653875554e-09)
@@ -61,59 +62,88 @@
     return jnp.dot(left, split(y, 0), preferred_element_type=jnp.float32)
 
 
-def first_kernel(devices, part, scale, wave_ref, level_ref, angle_ref, out_ref):
+def first_kernel(devices, group, scale, wave_ref, level_ref, angle_ref, out_ref):
+    part, lanes = wave_ref.shape[2:]
+    angle = jnp.broadcast_to(angle_ref[0:1, :], (8, lanes))
     tiles = part // 8
-    angle = jnp.broadcast_to(angle_ref[0:1, :], (8, wave_ref.shape[2]))
-
-    def step(tile, _):
-        for d in range(devices):
-            rows = pl.ds(pl.multiple_of(d * part + tile * 8, 8), 8)
-            levels = level_ref[rows, :]
-            real, imag = turn(wave_ref[0, rows, :], wave_ref[1, rows, :], levels, angle, scale)
-            here = pl.ds(pl.multiple_of(tile * 8, 8), 8)
-            out_ref[d, 0, here, :] = real
-            out_ref[d, 1, here, :] = imag
-            out_ref[d, 2, here, :] = levels
+
+    def inner(i, _):
+        base, rows = i // tiles * group, pl.ds(pl.multiple_of(i % tiles * 8, 8), 8)
+        pairs = [
+            turn(wave_ref[0, base + k, rows, :], wave_ref[1, base + k, rows, :], level_ref[base + k, rows, :], angle, scale)
+            for k in range(group)
+        ]
         for p in range(2):
-            here = pl.ds(pl.multiple_of(tile * 8, 8), 8)
-            values = butterflies([out_ref[d, p, here, :] for d in range(devices)])
-            for d in range(devices):
-                out_ref[d, p, here, :] = values[d]
-        return 0
-
-    lax.fori_loop(0, tiles, step, 0)
-
-
-def middle_kernel(devices, part, scale, in_ref, angle_ref, right_ref, left_ref, out_ref, held):
+            for k, value in enumerate(butterflies([pair[p] for pair in pairs])):
+                out_ref[base + k, p, rows, :] = value
+        return 0
+
+    lax.fori_loop(0, devices // group * tiles, inner, 0, unroll=True)
+
+    def outer(k, _):
+        for p in range(2):
+            for tile in range(tiles):
+                rows = slice(tile * 8, tile * 8 + 8)
+                values = butterflies([out_ref[g * group + k, p, rows, :] for g in range(devices // group)])
+                for g, value in enumerate(values):
+                    out_ref[g * group + k, p, rows, :] = value
+        return 0
+
+    lax.fori_loop(0, group, outer, 0, unroll=True)
+
+
+def pick_kernel(slabs, size, place_ref, wave_ref, level_ref, angle_ref, *refs):
+    outs, sems = refs[:-1], refs[-1]
+    mine = place_ref[0] // size
+    pairs = [(level_ref.at[pl.ds((mine ^ m) * size, size)], outs[m + 2]) for m in range(1, slabs)]
+    pairs += [(wave_ref, outs[0]), (level_ref, outs[1]), (angle_ref, outs[2])]
+    copies = [pltpu.make_async_copy(*pair, sems.at[k]) for k, pair in enumerate(pairs)]
+    for copy in copies:
+        copy.start()
+    for copy in copies:
+        copy.wait()
+
+
+def deal_kernel(slabs, size, place_ref, level_ref, *refs):
+    mine = place_ref[0] % size
+    for k in range(size):
+        refs[slabs - 1 + k][0] = level_ref[place_ref[0] ^ k]
+        for m in range(1, slabs):
+            refs[slabs - 1 + k][m] = refs[m - 1][mine ^ k]
+
+
+def middle_kernel(devices, part, scale, slabs, place_ref, in_ref, angle_ref, right_ref, left_ref, *refs):
+    size = devices // slabs
+    level_refs, out_ref, held, levels = refs[:size], refs[size], refs[size + 1], refs[size + 2]
     lanes = in_ref.shape[3]
-    size = left_ref.shape[0]
-    per = size // part
+    block = left_ref.shape[0]
+    per = block // part
     groups = devices // per
     right, left = right_ref[...], left_ref[...]
+    for k in range(size):
+        for m in range(slabs):
+            levels[pl.ds((place_ref[0] ^ (m * size + k)) * part, part), :] = level_refs[k][m]
     for p in range(2):
         for g in range(groups):
-            x = in_ref[g * per:(g + 1) * per, p].reshape(size, lanes)
-            held[p, g * size:(g + 1) * size] = tile_turn(x, right, left)
+            x = in_ref[g * per:(g + 1) * per, p].reshape(block, lanes)
+            held[p, g * block:(g + 1) * block] = tile_turn(x, right, left)
     angle = jnp.broadcast_to(angle_ref[1:2, :], (8, lanes))
 
     def step(tile, _):
-        rows = [pl.ds(pl.multiple_of(g * size + tile * 8, 8), 8) for g in range(groups)]
+        rows = [pl.ds(pl.multiple_of(g * block + tile * 8, 8), 8) for g in range(groups)]
         real = butterflies([held[0, r, :] for r in rows])
         imag = butterflies([held[1, r, :] for r in rows])
         for g in range(groups):
-            first = (g * size + tile * 8) // part
-            offset = pl.multiple_of((tile * 8) % part, 8)
-            levels = in_ref[first, 2, pl.ds(offset, 8), :]
-            real[g], imag[g] = turn(real[g], imag[g], levels, angle, scale)
+            real[g], imag[g] = turn(real[g], imag[g], levels[rows[g], :], angle, scale)
         for p, values in enumerate((real, imag)):
             for r, value in zip(rows, butterflies(values)):
                 held[p, r, :] = value
         return 0
 
-    lax.fori_loop(0, size // 8, step, 0)
+    lax.fori_loop(0, block // 8, step, 0)
     for p in range(2):
         for g in range(groups):
-            y = tile_turn(held[p, g * size:(g + 1) * size], right, left)
+            y = tile_turn(held[p, g * block:(g + 1) * block], right, left)
             out_ref[g * per:(g + 1) * per, p] = y.reshape(per, part, lanes)
 
 
@@ -130,33 +160,89 @@
     lax.fori_loop(0, part // 8, step, 0)
 
 
-def call(kernel, shape, scratch=()):
-    return pl.pallas_call(
-        kernel,
-        out_shape=jax.ShapeDtypeStruct(shape, jnp.float32),
-        scratch_shapes=list(scratch),
-    )
-
-
-def body_fast(axes, devices, wave, levels, angles):
+def near(x):
+    return pltpu.with_memory_space_constraint(x, pltpu.VMEM)
+
+
+def far(x):
+    return pltpu.with_memory_space_constraint(x, pltpu.HBM)
+
+
+def flat(*shape):
+    return jax.ShapeDtypeStruct(shape, jnp.float32)
+
+
+def swap(x, axes, devices, mask):
+    return lax.ppermute(x, axes, [(i, i ^ mask) for i in range(devices)])
+
+
+PARAMS = pltpu.CompilerParams(vmem_limit_bytes=16 * 2**20)
+SCALAR = pl.BlockSpec(memory_space=pltpu.SMEM)
+WHOLE = pl.BlockSpec(memory_space=pltpu.VMEM)
+
+
+def body_fast(axes, devices, slabs, wave, levels, angles):
     blocks, rows, lanes = levels.shape
     total = blocks * rows
     part = total // devices
+    size = devices // slabs
     scale = float(devices * total * lanes) ** -0.5
-    wave = wave.reshape(2, total, lanes)
-    levels = levels.reshape(total, lanes)
-    sent = call(functools.partial(first_kernel, devices, part, scale), (devices, 3, part, lanes))(wave, levels, angles)
+    place = lax.axis_index(axes).astype(jnp.int32).reshape(1)
+    wave = wave.reshape(2, devices, part, lanes)
+    levels = levels.reshape(devices, part, lanes)
+    wave, levels, angles, *picked = pl.pallas_call(
+        functools.partial(pick_kernel, slabs, size),
+        in_specs=[SCALAR] + [pl.BlockSpec(memory_space=pltpu.HBM)] * 3,
+        out_specs=[WHOLE] * (slabs + 2),
+        out_shape=[pltpu.VMEM(x.shape, jnp.float32) for x in (wave, levels, angles)]
+        + [pltpu.VMEM((size, part, lanes), jnp.float32)] * (slabs - 1),
+        scratch_shapes=[pltpu.SemaphoreType.DMA((slabs + 2,))],
+        name="pick",
+        compiler_params=PARAMS,
+    )(place, far(wave), far(levels), far(angles))
+    mine = []
+    for m in range(1, slabs):
+        mine.append(swap(picked[m - 1], axes, devices, m * size))
+    sent = pl.pallas_call(
+        functools.partial(first_kernel, devices, size, scale),
+        in_specs=[WHOLE] * 3,
+        out_specs=WHOLE,
+        out_shape=flat(devices, 2, part, lanes),
+        name="first",
+        compiler_params=PARAMS,
+    )(near(wave), near(levels), near(angles))
     seen = lax.all_to_all(sent, axes, 0, 0, tiled=True)
+    dealt = pl.pallas_call(
+        functools.partial(deal_kernel, slabs, size),
+        in_specs=[SCALAR] + [WHOLE] * slabs,
+        out_specs=[WHOLE] * size,
+        out_shape=[pltpu.VMEM((slabs, part, lanes), jnp.float32)] * size,
+        name="deal",
+        compiler_params=PARAMS,
+    )(place, near(levels), *map(near, mine))
+    dealt = [dealt[0]] + [swap(dealt[k], axes, devices, k) for k in range(1, size)]
     sign = signs(lanes, jnp.bfloat16)
     right = jnp.concatenate([sign, sign], axis=0)
     sign = signs(128, jnp.bfloat16)
     left = jnp.concatenate([sign, sign], axis=1)
-    back = call(
-        functools.partial(middle_kernel, devices, part, scale), (devices, 2, part, lanes),
-        [pltpu.VMEM((2, total, lanes), jnp.float32)],
-    )(seen, angles, right, left)
+    back = pl.pallas_call(
+        functools.partial(middle_kernel, devices, part, scale, slabs),
+        in_specs=[SCALAR] + [WHOLE] * (4 + size),
+        out_specs=WHOLE,
+        out_shape=pltpu.VMEM((devices, 2, part, lanes), jnp.float32),
+        scratch_shapes=[pltpu.VMEM((2, total, lanes), jnp.float32), pltpu.VMEM((total, lanes), jnp.float32)],
+        name="middle",
+        compiler_params=PARAMS,
+    )(place, near(seen), near(angles), right, left, *map(near, dealt))
     back = lax.all_to_all(back, axes, 0, 0, tiled=True)
-    out = call(functools.partial(last_kernel, devices, part), (2, total, lanes))(back)
+    out = pl.pallas_call(
+        functools.partial(last_kernel, devices, part),
+        in_specs=[WHOLE],
+        out_specs=WHOLE,
+        out_shape=flat(2, total, lanes),
+        name="last",
+        compiler_params=PARAMS,
+    )(near(back))
     return out.reshape(2, blocks, rows, lanes)
 
 
@@ -197,7 +283,10 @@
         total = levels.shape[0] * levels.shape[1]
         part = total // devices
         fast = part % 8 == 0 and 128 % part == 0 and total % 128 == 0
-        return (body_fast if fast else body_plain)(axes, devices, wave, levels, angles)
+        slabs = mesh.shape["qa"] // 4
+        if fast and slabs > 1:
+            return body_fast(axes, devices, slabs, wave, levels, angles)
+        return body_plain(axes, devices, wave, levels, angles)
 
     in_specs = (P(None, axes, None, None), P(axes, None, None), P())
     return jax.shard_map(body, mesh=mesh, in_specs=in_specs, out_specs=in_specs[0], check_vma=False)

time: 87.5 us -> 91.7 us (1.048)
  starting transfers between devices: 7.33 us -> 19.4 us
  Pallas kernels: 11.2 us -> 7.38 us
  waiting for transfers between devices: 36.1 us -> 34.2 us
  other arithmetic: 1.3 us -> 0.06 us
  local copies, waits for them, and re-layouts: 1.17 us -> 0 us
    all_to_all x1, waiting for transfers between devices: 36.1 us -> 0.01 us  [body_fast(): seen = lax.all_to_all(sent, axes, 0, 0, tiled=True)]
    ppermute x0 -> x10, waiting for transfers between devices: none -> 34.2 us  [swap(): return lax.ppermute(x, axes, [(i, i ^ mask) for i in range(devices)])]
    ppermute x0 -> x10, starting transfers between devices: none -> 12.1 us  [swap(): return lax.ppermute(x, axes, [(i, i ^ mask) for i in range(devices)])]
    pallas_call x3 -> x5, Pallas kernels: 11.2 us -> 7.38 us  [the longest x1 2.66 us: body_fast(): pl.pallas_call(functools.partial(middle_kernel, devices, part, scale, sla...]
    unnamed x2 -> x0, local copies, waits for them, and re-layouts: 1.17 us -> none
  transfers between devices with their start and end apart: 1 -> 11, of which waited for: 1 -> 5; matrix products, arithmetic and copies ran while one was open for 1% -> 0% of each run, Pallas kernels for 0% -> 0%
where the time goes in v2:
time: 91.7 us; the launch traced here: 91.5 us
  waiting for transfers between devices  34.2 us (37%)
  blocking collectives  30.4 us (33%)
  starting transfers between devices  19.4 us (21%)
  Pallas kernels  7.38 us (8%)
    ppermute x10, waiting for transfers between devices, swap(): return lax.ppermute(x, axes, [(i, i ^ mask) for i in range(devices)])  34.2 us
    all_to_all x1, blocking collectives, body_fast(): back = lax.all_to_all(back, axes, 0, 0, tiled=True)  30.4 us
    ppermute x10, starting transfers between devices, swap(): return lax.ppermute(x, axes, [(i, i ^ mask) for i in range(devices)])  12.1 us
    all_to_all x1, starting transfers between devices, body_fast(): seen = lax.all_to_all(sent, axes, 0, 0, tiled=True)  7.33 us
    pallas_call x1, Pallas kernels, body_fast(): pl.pallas_call(functools.partial(middle_kernel, devices, part, scale, sla...  2.66 us
  transfers between devices with their start and end apart: 11, of which 5 were waited for; matrix products, arithmetic and copies ran while one was open for 0% of the time, Pallas kernels for 0%

profile of v2, /device:TPU:0, one launch (start us, length us, event | category | flops | bytes accessed | tf_op | source)
XLA Modules:
  0.0 91.5 jit_solution(11986765414882386607)
XLA Ops:
  0.0 1.6 %pick.1 = (f32[2,32,32,128]{3,2,1,0:T(8,128)S(1)}, f32[32,32,128]{2,1,0:T(8,128)S(1)}, f32[2,128]{1,0:T(2,128)S(1)}, f32[8,32,128]{2,1,0:T(8,128)S(1)}, f32[8,32...) custom-call(s32[1]{0:T(128)} %bitcast.place_ref, f32[2,32,32,128]{3,2,1,0:T(8,128)} %bitcast.4, f32[32,32,128]{2,1,0:T(8,128)} %bitcast.5, ...), custom_call_target="tpu_custom_call" | custom-call | tf_op jit(solution)/shard_map/pick/pallas_call | solution.py:193
  1.6 1.8 %first.1 = f32[32,2,32,128]{3,2,1,0:T(8,128)} custom-call(f32[2,32,32,128]{3,2,1,0:T(8,128)S(1)} %get-tuple-element.19.wave_ref, f32[32,32,128]{2,1,0:T(8,128)S(1)} %get-tuple-element.20.level_ref, f32[2,128]{1,0:T(2,128)S(1)} %get-tuple-element.21.angle_ref), custom_call_target="tpu_custom_call" | custom-call | tf_op jit(solution)/shard_map/first/pallas_call | solution.py:206
  3.4 7.3 %all-to-all-start = ((f32[32,2,32,128]{3,2,1,0:T(8,128)}), f32[32,2,32,128]{3,2,1,0:T(8,128)S(1)}, u32[]{:S(2)}, u32[]{:S(2)}) async-start(f32[32,2,32,128]{3,2,1,0:T(8,128)} %first.1), calls=%async_computation | async-start | bytes 2097152 | tf_op jit(solution)/shard_map/all_to_all | solution.py:214
  10.7 1.8 %collective-permute-start = (f32[8,32,128]{2,1,0:T(8,128)S(1)}, f32[8,32,128]{2,1,0:T(8,128)S(1)}, u32[]{:S(2)}, u32[]{:S(2)}) collective-permute-start(f32[8,32,128]{2,1,0:T(8,128)S(1)} %get-tuple-element.22), channel_id=1, source_target_pairs={{0,8},{1,9},{2,10},{3,11},{4,12},{5,13},{6,14},{7,15},{8,0},{9,1},... | collective-permute-start | bytes 393224 | tf_op jit(solution)/shard_map/ppermute | solution.py:176
  12.6 2.4 %collective-permute-start.1 = (f32[8,32,128]{2,1,0:T(8,128)S(1)}, f32[8,32,128]{2,1,0:T(8,128)S(1)}, u32[]{:S(2)}, u32[]{:S(2)}) collective-permute-start(f32[8,32,128]{2,1,0:T(8,128)S(1)} %get-tuple-element.23), channel_id=1, source_target_pairs={{0,16},{1,17},{2,18},{3,19},{4,20},{5,21},{6,22},{7,23},{8,24},{9,... | collective-permute-start | bytes 393224 | tf_op jit(solution)/shard_map/ppermute | solution.py:176
  15.0 0.2 collective-permute-start.2
  15.3 16.3 %collective-permute-done.refs_0_ = f32[8,32,128]{2,1,0:T(8,128)S(1)} collective-permute-done((f32[8,32,128]{2,1,0:T(8,128)S(1)}, f32[8,32,128]{2,1,0:T(8,128)S(1)}, u32[]{:S(2)}, u32[]{:S(2)}) %collective-permute-start) | collective-permute-done | bytes 131104 | tf_op jit(solution)/shard_map/ppermute | solution.py:176
  31.5 14.4 %collective-permute-done.1.refs_1_ = f32[8,32,128]{2,1,0:T(8,128)S(1)} collective-permute-done((f32[8,32,128]{2,1,0:T(8,128)S(1)}, f32[8,32,128]{2,1,0:T(8,128)S(1)}, u32[]{:S(2)}, u32[]{:S(2)}) %collective-permute-start.1) | collective-permute-done | bytes 131104 | tf_op jit(solution)/shard_map/ppermute | solution.py:176
  45.9 0.0 collective-permute-done.2.refs_2_
  46.0 1.5 %collective-permute-start.3 = (f32[4,32,128]{2,1,0:T(8,128)S(1)}, f32[4,32,128]{2,1,0:T(8,128)S(1)}, u32[]{:S(2)}, u32[]{:S(2)}) collective-permute-start(f32[4,32,128]{2,1,0:T(8,128)S(1)} %get-tuple-element.26), channel_id=1, source_target_pairs={{0,1},{1,0},{2,3},{3,2},{4,5},{5,4},{6,7},{7,6},{8,9},{9,8},{10,11... | collective-permute-start | bytes 196616 | tf_op jit(solution)/shard_map/ppermute | solution.py:176
  47.5 0.0 collective-permute-start.4
  47.5 0.7 collective-permute-start.5
  48.2 1.5 %collective-permute-start.6 = (f32[4,32,128]{2,1,0:T(8,128)S(1)}, f32[4,32,128]{2,1,0:T(8,128)S(1)}, u32[]{:S(2)}, u32[]{:S(2)}) collective-permute-start(f32[4,32,128]{2,1,0:T(8,128)S(1)} %get-tuple-element.29), channel_id=1, source_target_pairs={{0,4},{1,5},{2,6},{3,7},{4,0},{5,1},{6,2},{7,3},{8,12},{9,13},{10,... | collective-permute-start | bytes 196616 | tf_op jit(solution)/shard_map/ppermute | solution.py:176
  49.7 1.5 %collective-permute-start.7 = (f32[4,32,128]{2,1,0:T(8,128)S(1)}, f32[4,32,128]{2,1,0:T(8,128)S(1)}, u32[]{:S(2)}, u32[]{:S(2)}) collective-permute-start(f32[4,32,128]{2,1,0:T(8,128)S(1)} %get-tuple-element.30), channel_id=1, source_target_pairs={{0,5},{1,4},{2,7},{3,6},{4,1},{5,0},{6,3},{7,2},{8,13},{9,12},{10,... | collective-permute-start | bytes 196616 | tf_op jit(solution)/shard_map/ppermute | solution.py:176
  51.1 0.0 collective-permute-done.3.refs_1_
  51.2 0.6 collective-permute-start.8
  51.8 0.0 collective-permute-done.4.refs_2_
  51.8 1.9 %collective-permute-start.9 = (f32[4,32,128]{2,1,0:T(8,128)S(1)}, f32[4,32,128]{2,1,0:T(8,128)S(1)}, u32[]{:S(2)}, u32[]{:S(2)}) collective-permute-start(f32[4,32,128]{2,1,0:T(8,128)S(1)} %get-tuple-element.32), channel_id=1, source_target_pairs={{0,7},{1,6},{2,5},{3,4},{4,3},{5,2},{6,1},{7,0},{8,15},{9,14},{10,... | collective-permute-start | bytes 196616 | tf_op jit(solution)/shard_map/ppermute | solution.py:176
  53.6 0.0 collective-permute-done.5.refs_3_
  53.6 0.0 collective-permute-done.6.refs_4_
  53.7 1.2 %collective-permute-done.7.refs_5_ = f32[4,32,128]{2,1,0:T(8,128)S(1)} collective-permute-done((f32[4,32,128]{2,1,0:T(8,128)S(1)}, f32[4,32,128]{2,1,0:T(8,128)S(1)}, u32[]{:S(2)}, u32[]{:S(2)}) %collective-permute-start.7) | collective-permute-done | bytes 65568 | tf_op jit(solution)/shard_map/ppermute | solution.py:176
  54.8 0.7 collective-permute-done.8.refs_6_
  55.5 1.6 %collective-permute-done.9.refs_7_ = f32[4,32,128]{2,1,0:T(8,128)S(1)} collective-permute-done((f32[4,32,128]{2,1,0:T(8,128)S(1)}, f32[4,32,128]{2,1,0:T(8,128)S(1)}, u32[]{:S(2)}, u32[]{:S(2)}) %collective-permute-start.9) | collective-permute-done | bytes 65568 | tf_op jit(solution)/shard_map/ppermute | solution.py:176
  57.1 0.0 all-to-all-done.in_ref
  57.1 2.7 %middle.1 = f32[32,2,32,128]{3,2,1,0:T(8,128)S(1)} custom-call(s32[1]{0:T(128)} %bitcast.place_ref, f32[32,2,32,128]{3,2,1,0:T(8,128)S(1)} %all-to-all-done.in_ref, f32[2,128]{1,0:T(2,128)S(1)} %get-tuple-element.21.angle_ref, bf16[256,128]{1,0:T(8,128)(2,1)S(1)} %pad_maximum_fusion.right_ref, bf16[128,256]{1,0:T(8,128)(2,1)S(1)} %pad_maximum_fusion.1.left_ref, ...), custom_call_target="tpu_custom_call" | custom-call | tf_op jit(solution)/shard_map/middle/pallas_call | solution.py:228
  59.8 30.4 %all_to_all.10.in_ref = f32[32,2,32,128]{3,2,1,0:T(8,128)S(1)} all-to-all(f32[32,2,32,128]{3,2,1,0:T(8,128)S(1)} %middle.1), channel_id=1, replica_groups=mesh['qa'=16,'qb'=2] {'qa','qb'}, dimensions={0} | all-to-all | bytes 2097152 | tf_op jit(solution)/shard_map/all_to_all | solution.py:237
  90.2 1.3 %last.1 = f32[2,1024,128]{2,1,0:T(8,128)} custom-call(f32[32,2,32,128]{3,2,1,0:T(8,128)S(1)} %all_to_all.10.in_ref), custom_call_target="tpu_custom_call" | custom-call | tf_op jit(solution)/shard_map/last/pallas_call | solution.py:238
  (4 shorter events, 0.1 us)
Async XLA Ops:
  3.4 53.7 %all-to-all-start = ((f32[32,2,32,128]{3,2,1,0:T(8,128)}), f32[32,2,32,128]{3,2,1,0:T(8,128)S(1)}, u32[]{:S(2)}, u32[]{:S(2)}) async-start(f32[32,2,32,128]{3,2,1,0:T(8,128)} %first.1), calls=%async_computation | async-start | bytes 2097152 | tf_op jit(solution)/shard_map/all_to_all | solution.py:214
  10.7 20.8 %collective-permute-start = (f32[8,32,128]{2,1,0:T(8,128)S(1)}, f32[8,32,128]{2,1,0:T(8,128)S(1)}, u32[]{:S(2)}, u32[]{:S(2)}) collective-permute-start(f32[8,32,128]{2,1,0:T(8,128)S(1)} %get-tuple-element.22), channel_id=1, source_target_pairs={{0,8},{1,9},{2,10},{3,11},{4,12},{5,13},{6,14},{7,15},{8,0},{9,1},... | collective-permute-start | bytes 393224 | tf_op jit(solution)/shard_map/ppermute | solution.py:176
  12.6 33.4 %collective-permute-start.1 = (f32[8,32,128]{2,1,0:T(8,128)S(1)}, f32[8,32,128]{2,1,0:T(8,128)S(1)}, u32[]{:S(2)}, u32[]{:S(2)}) collective-permute-start(f32[8,32,128]{2,1,0:T(8,128)S(1)} %get-tuple-element.23), channel_id=1, source_target_pairs={{0,16},{1,17},{2,18},{3,19},{4,20},{5,21},{6,22},{7,23},{8,24},{9,... | collective-permute-start | bytes 393224 | tf_op jit(solution)/shard_map/ppermute | solution.py:176
  15.0 31.0 %collective-permute-start.2 = (f32[8,32,128]{2,1,0:T(8,128)S(1)}, f32[8,32,128]{2,1,0:T(8,128)S(1)}, u32[]{:S(2)}, u32[]{:S(2)}) collective-permute-start(f32[8,32,128]{2,1,0:T(8,128)S(1)} %get-tuple-element.24), channel_id=1, source_target_pairs={{0,24},{1,25},{2,26},{3,27},{4,28},{5,29},{6,30},{7,31},{8,16},{9,... | collective-permute-start | bytes 393224 | tf_op jit(solution)/shard_map/ppermute | solution.py:176
  46.0 5.2 %collective-permute-start.3 = (f32[4,32,128]{2,1,0:T(8,128)S(1)}, f32[4,32,128]{2,1,0:T(8,128)S(1)}, u32[]{:S(2)}, u32[]{:S(2)}) collective-permute-start(f32[4,32,128]{2,1,0:T(8,128)S(1)} %get-tuple-element.26), channel_id=1, source_target_pairs={{0,1},{1,0},{2,3},{3,2},{4,5},{5,4},{6,7},{7,6},{8,9},{9,8},{10,11... | collective-permute-start | bytes 196616 | tf_op jit(solution)/shard_map/ppermute | solution.py:176
  47.5 4.2 %collective-permute-start.4 = (f32[4,32,128]{2,1,0:T(8,128)S(1)}, f32[4,32,128]{2,1,0:T(8,128)S(1)}, u32[]{:S(2)}, u32[]{:S(2)}) collective-permute-start(f32[4,32,128]{2,1,0:T(8,128)S(1)} %get-tuple-element.27), channel_id=1, source_target_pairs={{0,2},{1,3},{2,0},{3,1},{4,6},{5,7},{6,4},{7,5},{8,10},{9,11},{10,... | collective-permute-start | bytes 196616 | tf_op jit(solution)/shard_map/ppermute | solution.py:176
  47.5 6.1 %collective-permute-start.5 = (f32[4,32,128]{2,1,0:T(8,128)S(1)}, f32[4,32,128]{2,1,0:T(8,128)S(1)}, u32[]{:S(2)}, u32[]{:S(2)}) collective-permute-start(f32[4,32,128]{2,1,0:T(8,128)S(1)} %get-tuple-element.28), channel_id=1, source_target_pairs={{0,3},{1,2},{2,1},{3,0},{4,7},{5,6},{6,5},{7,4},{8,11},{9,10},{10,... | collective-permute-start | bytes 196616 | tf_op jit(solution)/shard_map/ppermute | solution.py:176
  48.2 5.4 %collective-permute-start.6 = (f32[4,32,128]{2,1,0:T(8,128)S(1)}, f32[4,32,128]{2,1,0:T(8,128)S(1)}, u32[]{:S(2)}, u32[]{:S(2)}) collective-permute-start(f32[4,32,128]{2,1,0:T(8,128)S(1)} %get-tuple-element.29), channel_id=1, source_target_pairs={{0,4},{1,5},{2,6},{3,7},{4,0},{5,1},{6,2},{7,3},{8,12},{9,13},{10,... | collective-permute-start | bytes 196616 | tf_op jit(solution)/shard_map/ppermute | solution.py:176
  49.7 5.2 %collective-permute-start.7 = (f32[4,32,128]{2,1,0:T(8,128)S(1)}, f32[4,32,128]{2,1,0:T(8,128)S(1)}, u32[]{:S(2)}, u32[]{:S(2)}) collective-permute-start(f32[4,32,128]{2,1,0:T(8,128)S(1)} %get-tuple-element.30), channel_id=1, source_target_pairs={{0,5},{1,4},{2,7},{3,6},{4,1},{5,0},{6,3},{7,2},{8,13},{9,12},{10,... | collective-permute-start | bytes 196616 | tf_op jit(solution)/shard_map/ppermute | solution.py:176
  51.2 4.4 %collective-permute-start.8 = (f32[4,32,128]{2,1,0:T(8,128)S(1)}, f32[4,32,128]{2,1,0:T(8,128)S(1)}, u32[]{:S(2)}, u32[]{:S(2)}) collective-permute-start(f32[4,32,128]{2,1,0:T(8,128)S(1)} %get-tuple-element.31), channel_id=1, source_target_pairs={{0,6},{1,7},{2,4},{3,5},{4,2},{5,3},{6,0},{7,1},{8,14},{9,15},{10,... | collective-permute-start | bytes 196616 | tf_op jit(solution)/shard_map/ppermute | solution.py:176
  51.8 5.4 %collective-permute-start.9 = (f32[4,32,128]{2,1,0:T(8,128)S(1)}, f32[4,32,128]{2,1,0:T(8,128)S(1)}, u32[]{:S(2)}, u32[]{:S(2)}) collective-permute-start(f32[4,32,128]{2,1,0:T(8,128)S(1)} %get-tuple-element.32), channel_id=1, source_target_pairs={{0,7},{1,6},{2,5},{3,4},{4,3},{5,2},{6,1},{7,0},{8,15},{9,14},{10,... | collective-permute-start | bytes 196616 | tf_op jit(solution)/shard_map/ppermute | solution.py:176

commit v3 on v1

v3 whole, which is shorter than its diff:
```python
import functools

import jax
import jax.numpy as jnp
from jax import lax
from jax.experimental import pallas as pl
from jax.experimental.pallas import tpu as pltpu
from jax.sharding import PartitionSpec as P


COS = (0.99999999952702, -0.49999999256864713, 0.04166664759095227, -0.0013888705067900038,
       2.4793136218611696e-05, -2.735711629719697e-07, 1.8502809653875554e-09)
SIN = (0.9999999999681006, -0.16666666616558576, 0.008333332047516205, -0.00019841145991402124,
       2.75516291724042e-06, -2.4917466240452868e-08, 1.446608995457697e-10)


def poly(coefs, t):
    total = jnp.full_like(t, coefs[-1])
    for c in coefs[-2::-1]:
        total = total * t + c
    return total


def butterflies(values):
    values = list(values)
    step = 1
    while step < len(values):
        for i in range(len(values)):
            if not i & step:
                u, v = values[i], values[i + step]
                values[i], values[i + step] = u + v, u - v
        step *= 2
    return values


def signs(count, dtype):
    rank = lax.broadcasted_iota(jnp.int32, (count, count), 0) & lax.broadcasted_iota(jnp.int32, (count, count), 1)
    parity = rank
    shift = 1
    while shift < count:
        parity = parity ^ (parity >> shift)
        shift *= 2
    return (1 - 2 * (parity & 1)).astype(dtype)


def split(x, axis):
    high = x.astype(jnp.bfloat16)
    low = (x - high.astype(jnp.float32)).astype(jnp.bfloat16)
    return jnp.concatenate([high, low], axis=axis)


def tile_turn(x, right, left):
    y = jnp.dot(split(x, 1), right, preferred_element_type=jnp.float32)
    return jnp.dot(left, split(y, 0), preferred_element_type=jnp.float32)


def trig(x, scale):
    t = x * x
    return poly(COS, t) * scale, x * poly(SIN, t) * scale


def rotate(real, imag, c, s):
    return real * c + imag * s, imag * c - real * s


def pick_kernel(slabs, size, place_ref, wave_ref, level_ref, angle_ref, *refs):
    outs, sems = refs[:-1], refs[-1]
    mine = place_ref[0] // size
    pairs = list(zip((wave_ref, level_ref, angle_ref), outs))
    pairs += [(level_ref.at[pl.ds((mine ^ m) * size, size)], outs[m + 2]) for m in range(1, slabs)]
    copies = [pltpu.make_async_copy(*pair, sems.at[k]) for k, pair in enumerate(pairs)]
    for copy in copies:
        copy.start()
    for copy in copies:
        copy.wait()


def first_kernel(devices, part, scale, wave_ref, level_ref, angle_ref, right_ref, left_ref, out_ref, held):
    lanes = wave_ref.shape[2]
    block = left_ref.shape[0]
    groups, per = devices * part // block, block // part
    right, left = right_ref[...], left_ref[...]
    angle = jnp.broadcast_to(angle_ref[0:1, :], (block, lanes))
    for g in range(groups):
        rows = slice(g * block, (g + 1) * block)
        c, s = trig(angle * level_ref[rows, :], scale)
        for p, x in enumerate(rotate(wave_ref[0, rows, :], wave_ref[1, rows, :], c, s)):
            held[p, rows, :] = tile_turn(x, right, left)
    for p in range(2):
        for tile in range(block // 8):
            values = butterflies([held[p, g * block + tile * 8:g * block + tile * 8 + 8, :] for g in range(groups)])
            k, row = tile * 8 // part, tile * 8 % part
            for g, value in enumerate(values):
                out_ref[g * per + k, p, row:row + 8, :] = value


def deal_kernel(slabs, size, place_ref, *refs):
    mine = place_ref[0] % size
    for k in range(size):
        for m in range(slabs):
            refs[slabs + k][m] = refs[m][mine ^ k]


def trig_kernel(slabs, size, scale, place_ref, angle_ref, *refs):
    level_refs, cos_ref, sin_ref = refs[:size], refs[size], refs[size + 1]
    angle = jnp.broadcast_to(angle_ref[1:2, :], cos_ref.shape[1:])
    for k in range(size):
        for m in range(slabs):
            whose = place_ref[0] ^ (m * size + k)
            cos_ref[whose], sin_ref[whose] = trig(angle * level_refs[k][m], scale)


def turn_devices(slabs, size, tiles, seen_ref, cos_ref, sin_ref, held):
    for tile in tiles:
        rows = slice(tile * 8, tile * 8 + 8)
        for z in range(slabs):
            for p in range(2):
                values = butterflies([seen_ref[z * size + q, p, rows, :] for q in range(size)])
                for q, value in enumerate(values):
                    held[z * size + q, p, rows, :] = value
        for q in range(size):
            real, imag = (butterflies([held[z * size + q, p, rows, :] for z in range(slabs)]) for p in range(2))
            for z in range(slabs):
                d = z * size + q
                real[z], imag[z] = rotate(real[z], imag[z], cos_ref[d, rows, :], sin_ref[d, rows, :])
            for p, values in enumerate((real, imag)):
                for z, value in enumerate(butterflies(values)):
                    held[z * size + q, p, rows, :] = value


def few_kernel(slabs, size, place_ref, seen_ref, cos_ref, sin_ref, *refs):
    outs, held = refs[:slabs], refs[slabs]
    count = outs[0].shape[2] // 8
    turn_devices(slabs, size, range(count), seen_ref, cos_ref, sin_ref, held)
    mine = place_ref[0] // size
    for m in range(slabs):
        for p in range(2):
            for tile in range(count):
                rows = slice(tile * 8, tile * 8 + 8)
                values = butterflies([held[(mine ^ m) * size + q, p, rows, :] for q in range(size)])
                for q, value in enumerate(values):
                    outs[m][q, p, rows, :] = value


def most_kernel(slabs, size, seen_ref, cos_ref, sin_ref, right_ref, left_ref, out_ref, held):
    part, lanes = seen_ref.shape[2:]
    devices = slabs * size
    start = (part - out_ref.shape[2]) // 8
    turn_devices(slabs, size, range(start, part // 8), seen_ref, cos_ref, sin_ref, held)
    right, left = right_ref[...], left_ref[...]
    step = left.shape[0] // 8
    for tile in range(start, part // 8):
        rows = slice(tile * 8, tile * 8 + 8)
        for p in range(2):
            for z in range(slabs):
                values = butterflies([held[z * size + q, p, rows, :] for q in range(size)])
                for q, value in enumerate(values):
                    held[z * size + q, p, rows, :] = value
            for d in range(0, devices, step):
                x = held[d:d + step, p, rows, :].reshape(step * 8, lanes)
                out_ref[d:d + step, p, (tile - start) * 8:(tile - start) * 8 + 8, :] = tile_turn(x, right, left).reshape(step, 8, lanes)


def gather_kernel(slabs, size, place_ref, right_ref, left_ref, *refs):
    parts, out_ref, held = refs[:size], refs[size], refs[size + 1]
    for k in range(size):
        for m in range(slabs):
            held[place_ref[0] ^ (m * size + k)] = parts[k][m]
    right, left = right_ref[...], left_ref[...]
    step = left.shape[0] // 8
    for p in range(2):
        for d in range(0, slabs * size, step):
            for row in range(0, held.shape[2], 8):
                x = held[d:d + step, p, row:row + 8, :].reshape(step * 8, held.shape[3])
                out_ref[d:d + step, p, row:row + 8, :] = tile_turn(x, right, left).reshape(step, 8, held.shape[3])


def last_kernel(devices, part, few_ref, most_ref, out_ref, held, done, sems):
    tiles = part // 8
    low = 4
    high = devices // low

    start = few_ref.shape[2] // 8

    def source(d, p, tile):
        ref, row = (few_ref, tile * 8) if tile < start else (most_ref, (tile - start) * 8)
        return ref[d, p, row:row + 8, :]

    copies = []
    for p in range(2):
        for k in range(low):
            for tile in range(tiles):
                values = butterflies([source(h * low + k, p, tile) for h in range(high)])
                for h, value in enumerate(values):
                    held[p, h, k * tiles + tile] = value
        for h in range(high):
            values = butterflies([held[p, h, i] for i in range(low * tiles)])
            for i, value in enumerate(values):
                done[p, (h * low * tiles + i) * 8:(h * low * tiles + i) * 8 + 8, :] = value
            rows = pl.ds(h * low * part, low * part)
            copies.append(pltpu.make_async_copy(done.at[p, rows], out_ref.at[p, rows], sems.at[p * high + h]))
            copies[-1].start()
    for copy in copies:
        copy.wait()


def near(x):
    return pltpu.with_memory_space_constraint(x, pltpu.VMEM)


def far(x):
    return pltpu.with_memory_space_constraint(x, pltpu.HBM)


def flat(*shape):
    return jax.ShapeDtypeStruct(shape, jnp.float32)


def held_shape(*shape):
    return pltpu.VMEM(shape, jnp.float32)


def swap(x, axes, devices, mask):
    return lax.ppermute(x, axes, [(i, i ^ mask) for i in range(devices)])


FEW = 16
PARAMS = pltpu.CompilerParams(vmem_limit_bytes=16 * 2**20)
SCALAR = pl.BlockSpec(memory_space=pltpu.SMEM)
WHOLE = pl.BlockSpec(memory_space=pltpu.VMEM)
FAR = pl.BlockSpec(memory_space=pltpu.HBM)


def kernel_call(kernel, in_specs, out_shape, scratch=(), out_specs=None):
    count = len(out_shape) if isinstance(out_shape, list) else 0
    return pl.pallas_call(
        kernel,
        in_specs=in_specs,
        out_specs=out_specs or ([WHOLE] * count if count else WHOLE),
        out_shape=out_shape,
        scratch_shapes=list(scratch),
        compiler_params=PARAMS,
    )


def body_fast(axes, devices, slabs, wave, levels, angles):
    blocks, rows, lanes = levels.shape
    total = blocks * rows
    part = total // devices
    size = devices // slabs
    count = FEW
    scale = float(devices * total * lanes) ** -0.5
    place = lax.axis_index(axes).astype(jnp.int32).reshape(1)
    wave = wave.reshape(2, total, lanes)
    levels = levels.reshape(devices, part, lanes)
    sign = signs(lanes, jnp.bfloat16)
    right = jnp.concatenate([sign, sign], axis=0)
    full = signs(128, jnp.bfloat16)
    rank = jnp.arange(128)
    small = jnp.where(rank[:, None] // 8 == rank[None, :] // 8, jnp.tile(signs(8, jnp.bfloat16), (16, 16)), 0)
    left = jnp.concatenate([full, full], axis=1)
    left_small = jnp.concatenate([small, small], axis=1)

    wave, levels, angles, *picked = kernel_call(
        functools.partial(pick_kernel, slabs, size), [SCALAR] + [FAR] * 3,
        [held_shape(*x.shape) for x in (wave, levels, angles)] + [held_shape(size, part, lanes)] * (slabs - 1),
        [pltpu.SemaphoreType.DMA((slabs + 2,))],
    )(place, far(wave), far(levels), far(angles))
    own = lax.dynamic_slice_in_dim(levels, place[0] // size * size, size, 0)
    mine = [own]
    for m in range(1, slabs):
        mine.append(swap(picked[m - 1], axes, devices, m * size))
    sent = kernel_call(
        functools.partial(first_kernel, devices, part, scale), [WHOLE] * 5,
        flat(devices, 2, part, lanes), [held_shape(2, total, lanes)],
    )(near(wave), near(levels.reshape(total, lanes)), near(angles), right, left)
    seen = lax.all_to_all(sent, axes, 0, 0, tiled=True)
    dealt = kernel_call(
        functools.partial(deal_kernel, slabs, size), [SCALAR] + [WHOLE] * slabs,
        [held_shape(slabs, part, lanes)] * size,
    )(place, *map(near, mine))
    dealt = [dealt[0]] + [swap(dealt[k], axes, devices, k) for k in range(1, size)]
    cos, sin = kernel_call(
        functools.partial(trig_kernel, slabs, size, scale), [SCALAR] + [WHOLE] * (1 + size),
        [held_shape(devices, part, lanes)] * 2,
    )(place, near(angles), *map(near, dealt))

    seen = near(seen)
    few = kernel_call(
        functools.partial(few_kernel, slabs, size), [SCALAR] + [WHOLE] * 3,
        [held_shape(size, 2, count, lanes)] * slabs, [held_shape(devices, 2, count, lanes)],
    )(place, seen, cos, sin)
    few = [few[0], *few[1:]]
    for m in range(1, slabs):
        few[m] = swap(few[m], axes, devices, m * size)
    most = kernel_call(
        functools.partial(most_kernel, slabs, size), [WHOLE] * 5,
        flat(devices, 2, part - count, lanes), [held_shape(devices, 2, part, lanes)],
    )(seen, cos, sin, right, left_small)
    most = lax.all_to_all(most, axes, 0, 0, tiled=True)
    few = kernel_call(
        functools.partial(deal_kernel, slabs, size), [SCALAR] + [WHOLE] * slabs,
        [held_shape(slabs, 2, count, lanes)] * size,
    )(place, *map(near, few))
    few = [few[0]] + [swap(few[k], axes, devices, k) for k in range(1, size)]
    few = kernel_call(
        functools.partial(gather_kernel, slabs, size), [SCALAR] + [WHOLE] * (2 + size),
        held_shape(devices, 2, count, lanes), [held_shape(devices, 2, count, lanes)],
    )(place, right, left_small, *map(near, few))
    out = kernel_call(
        functools.partial(last_kernel, devices, part), [WHOLE] * 2, flat(2, total, lanes),
        [held_shape(2, devices // 4, part // 2, 8, lanes), held_shape(2, total, lanes), pltpu.SemaphoreType.DMA((devices // 2,))],
        FAR,
    )(near(few), near(most))
    return out.reshape(2, blocks, rows, lanes)


def walsh(values, dim):
    count = values.shape[dim]
    moved = jnp.tensordot(values, signs(count, jnp.float32), axes=([dim], [0]), precision=lax.Precision.HIGHEST)
    return jnp.moveaxis(moved, -1, dim) * count ** -0.5


def body_plain(axes, devices, wave, levels, angles):
    blocks, rows, lanes = levels.shape
    part = blocks * rows // devices
    values = wave.reshape(2, devices, part, lanes)
    levels = levels.reshape(devices, part, lanes)
    x = angles[0] * levels
    c, s = jnp.cos(x), jnp.sin(x)
    values = jnp.stack([values[0] * c + values[1] * s, values[1] * c - values[0] * s], axis=1)
    values = walsh(values, 0)
    values = lax.all_to_all(values, axes, 0, 0, tiled=True)
    levels = lax.all_to_all(levels, axes, 0, 0, tiled=True)
    for dim in (0, 2, 3):
        values = walsh(values, dim)
    x = angles[1] * levels
    c, s = jnp.cos(x), jnp.sin(x)
    values = jnp.stack([values[:, 0] * c + values[:, 1] * s, values[:, 1] * c - values[:, 0] * s], axis=1)
    for dim in (0, 2, 3):
        values = walsh(values, dim)
    values = lax.all_to_all(values, axes, 0, 0, tiled=True)
    values = walsh(values, 0)
    return jnp.moveaxis(values, 1, 0).reshape(wave.shape)


def solution(mesh):
    axes = ("qa", "qb")
    devices = mesh.shape["qa"] * mesh.shape["qb"]

    def body(wave, levels, angles):
        total = levels.shape[0] * levels.shape[1]
        part = total // devices
        fast = part % 16 == 0 and 128 % part == 0 and total % 128 == 0 and devices % 16 == 0
        slabs = mesh.shape["qa"] // 4
        if fast and slabs > 1:
            return body_fast(axes, devices, slabs, wave, levels, angles)
        return body_plain(axes, devices, wave, levels, angles)

    in_specs = (P(None, axes, None, None), P(axes, None, None), P())
    return jax.shard_map(body, mesh=mesh, in_specs=in_specs, out_specs=in_specs[0], check_vma=False)
```

time: 87.5 us -> 102 us (1.17)
  blocking collectives: 29.9 us -> 0 us
  starting transfers between devices: 7.33 us -> 35.9 us
  waiting for transfers between devices: 36.1 us -> 56.5 us
  Pallas kernels: 11.2 us -> 7.9 us
  other arithmetic: 1.3 us -> 0.17 us
    ppermute x0 -> x20, waiting for transfers between devices: none -> 56.5 us  [swap(): return lax.ppermute(x, axes, [(i, i ^ mask) for i in range(devices)])]
    all_to_all x1, waiting for transfers between devices: 36.1 us -> 0.01 us  [body_fast(): seen = lax.all_to_all(sent, axes, 0, 0, tiled=True)]
    all_to_all x1 -> x0, blocking collectives: 29.9 us -> none  [body_fast(): back = lax.all_to_all(back, axes, 0, 0, tiled=True)]
    ppermute x0 -> x20, starting transfers between devices: none -> 24 us  [swap(): return lax.ppermute(x, axes, [(i, i ^ mask) for i in range(devices)])]
    all_to_all x0 -> x1, starting transfers between devices: none -> 4.5 us  [body_fast(): most = lax.all_to_all(most, axes, 0, 0, tiled=True)]
    pallas_call x3 -> x9, Pallas kernels: 11.2 us -> 7.9 us  [the longest x1 2.3 us: body_fast(): kernel_call(functools.partial(first_kernel, devices, part, scale), [WHOLE...]
    unnamed x2 -> x0, local copies, waits for them, and re-layouts: 1.17 us -> none
  transfers between devices with their start and end apart: 1 -> 22, of which waited for: 1 -> 10; matrix products, arithmetic and copies ran while one was open for 1% -> 1% of each run, Pallas kernels for 0% -> 1%
where the time goes in v3:
time: 102 us; the launch traced here: 101 us
  waiting for transfers between devices  56.5 us (55%)
  starting transfers between devices  35.9 us (35%)
  Pallas kernels  7.9 us (8%)
    ppermute x20, waiting for transfers between devices, swap(): return lax.ppermute(x, axes, [(i, i ^ mask) for i in range(devices)])  56.5 us
    ppermute x20, starting transfers between devices, swap(): return lax.ppermute(x, axes, [(i, i ^ mask) for i in range(devices)])  24 us
    all_to_all x1, starting transfers between devices, body_fast(): seen = lax.all_to_all(sent, axes, 0, 0, tiled=True)  7.33 us
    all_to_all x1, starting transfers between devices, body_fast(): most = lax.all_to_all(most, axes, 0, 0, tiled=True)  4.5 us
    pallas_call x1, Pallas kernels, body_fast(): kernel_call(functools.partial(first_kernel, devices, part, scale), [WHOLE...  2.3 us
  transfers between devices with their start and end apart: 22, of which 10 were waited for; matrix products, arithmetic and copies ran while one was open for 1% of the time, Pallas kernels for 1%

profile of v3, /device:TPU:0, one launch (start us, length us, event | category | flops | bytes accessed | tf_op | source)
XLA Modules:
  0.0 101.2 jit_solution(9327248459390597736)
XLA Ops:
  0.1 1.5 %shard_map.37 = (f32[2,1024,128]{2,1,0:T(8,128)S(1)}, f32[32,32,128]{2,1,0:T(8,128)S(1)}, f32[2,128]{1,0:T(2,128)S(1)}, f32[8,32,128]{2,1,0:T(8,128)S(1)}, f32[8...) custom-call(s32[1]{0:T(128)} %bitcast.place_ref, f32[2,1024,128]{2,1,0:T(8,128)} %bitcast.8, f32[32,32,128]{2,1,0:T(8,128)} %bitcast.9, ...), custom_call_target="tpu_custom_call" | custom-call | tf_op jit(solution)/shard_map/pallas_call | solution.py:264
  1.6 2.3 %shard_map.38 = f32[32,2,32,128]{3,2,1,0:T(8,128)} custom-call(f32[2,1024,128]{2,1,0:T(8,128)S(1)} %get-tuple-element.33.wave_ref, f32[1024,128]{1,0:T(8,128)S(1)} %bitcast.7, f32[2,128]{1,0:T(2,128)S(1)} %get-tuple-element.35.angle_ref, bf16[256,128]{1,0:T(8,128)(2,1)S(1)} %pad_maximum_fusion.right_ref, bf16[128,256]{1,0:T(8,128)(2,1)S(1)} %pad_maximum_fusion.2.left_ref), custom_call_target="tpu_custom_call" | custom-call | tf_op jit(solution)/shard_map/pallas_call | solution.py:273
  3.9 7.3 %all-to-all-start = ((f32[32,2,32,128]{3,2,1,0:T(8,128)}), f32[32,2,32,128]{3,2,1,0:T(8,128)S(1)}, u32[]{:S(2)}, u32[]{:S(2)}) async-start(f32[32,2,32,128]{3,2,1,0:T(8,128)} %shard_map.38), calls=%async_computation | async-start | bytes 2097152 | tf_op jit(solution)/shard_map/all_to_all | solution.py:277
  11.3 1.8 %collective-permute-start = (f32[8,32,128]{2,1,0:T(8,128)S(1)}, f32[8,32,128]{2,1,0:T(8,128)S(1)}, u32[]{:S(2)}, u32[]{:S(2)}) collective-permute-start(f32[8,32,128]{2,1,0:T(8,128)S(1)} %get-tuple-element.36), channel_id=1, source_target_pairs={{0,8},{1,9},{2,10},{3,11},{4,12},{5,13},{6,14},{7,15},{8,0},{9,1},... | collective-permute-start | bytes 393224 | tf_op jit(solution)/shard_map/ppermute | solution.py:224
  13.1 2.4 %collective-permute-start.1 = (f32[8,32,128]{2,1,0:T(8,128)S(1)}, f32[8,32,128]{2,1,0:T(8,128)S(1)}, u32[]{:S(2)}, u32[]{:S(2)}) collective-permute-start(f32[8,32,128]{2,1,0:T(8,128)S(1)} %get-tuple-element.37), channel_id=1, source_target_pairs={{0,16},{1,17},{2,18},{3,19},{4,20},{5,21},{6,22},{7,23},{8,24},{9,... | collective-permute-start | bytes 393224 | tf_op jit(solution)/shard_map/ppermute | solution.py:224
  15.5 0.2 collective-permute-start.2
  15.8 0.1 tile.13
  15.9 0.5 tile.14
  16.4 15.7 %collective-permute-done.refs_1_ = f32[8,32,128]{2,1,0:T(8,128)S(1)} collective-permute-done((f32[8,32,128]{2,1,0:T(8,128)S(1)}, f32[8,32,128]{2,1,0:T(8,128)S(1)}, u32[]{:S(2)}, u32[]{:S(2)}) %collective-permute-start) | collective-permute-done | bytes 131104 | tf_op jit(solution)/shard_map/ppermute | solution.py:224
  32.1 14.4 %collective-permute-done.1.refs_2_ = f32[8,32,128]{2,1,0:T(8,128)S(1)} collective-permute-done((f32[8,32,128]{2,1,0:T(8,128)S(1)}, f32[8,32,128]{2,1,0:T(8,128)S(1)}, u32[]{:S(2)}, u32[]{:S(2)}) %collective-permute-start.1) | collective-permute-done | bytes 131104 | tf_op jit(solution)/shard_map/ppermute | solution.py:224
  46.5 1.5 %collective-permute-start.3 = (f32[4,32,128]{2,1,0:T(8,128)S(1)}, f32[4,32,128]{2,1,0:T(8,128)S(1)}, u32[]{:S(2)}, u32[]{:S(2)}) collective-permute-start(f32[4,32,128]{2,1,0:T(8,128)S(1)} %get-tuple-element.40), channel_id=1, source_target_pairs={{0,1},{1,0},{2,3},{3,2},{4,5},{5,4},{6,7},{7,6},{8,9},{9,8},{10,11... | collective-permute-start | bytes 196616 | tf_op jit(solution)/shard_map/ppermute | solution.py:224
  48.1 0.0 collective-permute-start.4
  48.1 0.1 compare_select_fusion
  48.1 0.7 collective-permute-start.5
  48.9 1.5 %collective-permute-start.6 = (f32[4,32,128]{2,1,0:T(8,128)S(1)}, f32[4,32,128]{2,1,0:T(8,128)S(1)}, u32[]{:S(2)}, u32[]{:S(2)}) collective-permute-start(f32[4,32,128]{2,1,0:T(8,128)S(1)} %get-tuple-element.43), channel_id=1, source_target_pairs={{0,4},{1,5},{2,6},{3,7},{4,0},{5,1},{6,2},{7,3},{8,12},{9,13},{10,... | collective-permute-start | bytes 196616 | tf_op jit(solution)/shard_map/ppermute | solution.py:224
  50.3 1.5 %collective-permute-start.7 = (f32[4,32,128]{2,1,0:T(8,128)S(1)}, f32[4,32,128]{2,1,0:T(8,128)S(1)}, u32[]{:S(2)}, u32[]{:S(2)}) collective-permute-start(f32[4,32,128]{2,1,0:T(8,128)S(1)} %get-tuple-element.44), channel_id=1, source_target_pairs={{0,5},{1,4},{2,7},{3,6},{4,1},{5,0},{6,3},{7,2},{8,13},{9,12},{10,... | collective-permute-start | bytes 196616 | tf_op jit(solution)/shard_map/ppermute | solution.py:224
  51.8 0.0 collective-permute-done.3.refs_1_
  51.8 0.5 collective-permute-start.8
  52.4 0.0 collective-permute-done.4.refs_2_
  52.4 1.7 %collective-permute-start.9 = (f32[4,32,128]{2,1,0:T(8,128)S(1)}, f32[4,32,128]{2,1,0:T(8,128)S(1)}, u32[]{:S(2)}, u32[]{:S(2)}) collective-permute-start(f32[4,32,128]{2,1,0:T(8,128)S(1)} %get-tuple-element.46), channel_id=1, source_target_pairs={{0,7},{1,6},{2,5},{3,4},{4,3},{5,2},{6,1},{7,0},{8,15},{9,14},{10,... | collective-permute-start | bytes 196616 | tf_op jit(solution)/shard_map/ppermute | solution.py:224
  54.1 0.0 collective-permute-done.6.refs_4_
  54.1 1.6 %collective-permute-done.7.refs_5_ = f32[4,32,128]{2,1,0:T(8,128)S(1)} collective-permute-done((f32[4,32,128]{2,1,0:T(8,128)S(1)}, f32[4,32,128]{2,1,0:T(8,128)S(1)}, u32[]{:S(2)}, u32[]{:S(2)}) %collective-permute-start.7) | collective-permute-done | bytes 65568 | tf_op jit(solution)/shard_map/ppermute | solution.py:224
  55.7 0.5 collective-permute-done.8.refs_6_
  56.2 1.6 %collective-permute-done.9.refs_7_ = f32[4,32,128]{2,1,0:T(8,128)S(1)} collective-permute-done((f32[4,32,128]{2,1,0:T(8,128)S(1)}, f32[4,32,128]{2,1,0:T(8,128)S(1)}, u32[]{:S(2)}, u32[]{:S(2)}) %collective-permute-start.9) | collective-permute-done | bytes 65568 | tf_op jit(solution)/shard_map/ppermute | solution.py:224
  57.7 0.5 shard_map.40
  58.2 0.0 all-to-all-done.seen_ref
  58.2 1.5 %shard_map.44 = f32[32,2,16,128]{3,2,1,0:T(8,128)} custom-call(f32[32,2,32,128]{3,2,1,0:T(8,128)S(1)} %all-to-all-done.seen_ref, f32[32,32,128]{2,1,0:T(8,128)S(1)} %get-tuple-element.47.cos_ref, f32[32,32,128]{2,1,0:T(8,128)S(1)} %get-tuple-element.48.sin_ref, bf16[256,128]{1,0:T(8,128)(2,1)S(1)} %pad_maximum_fusion.right_ref, ...), custom_call_target="tpu_custom_call" | custom-call | tf_op jit(solution)/shard_map/pallas_call | solution.py:296
  59.7 4.5 %all-to-all-start.1 = ((f32[32,2,16,128]{3,2,1,0:T(8,128)}), f32[32,2,16,128]{3,2,1,0:T(8,128)S(1)}, u32[]{:S(2)}, u32[]{:S(2)}) async-start(f32[32,2,16,128]{3,2,1,0:T(8,128)} %shard_map.44), calls=%async_computation.1 | async-start | bytes 1048576 | tf_op jit(solution)/shard_map/all_to_all | solution.py:300
  64.2 0.3 shard_map.41
  64.5 1.8 %collective-permute-start.10 = (f32[8,2,16,128]{3,2,1,0:T(8,128)S(1)}, f32[8,2,16,128]{3,2,1,0:T(8,128)S(1)}, u32[]{:S(2)}, u32[]{:S(2)}) collective-permute-start(f32[8,2,16,128]{3,2,1,0:T(8,128)S(1)} %get-tuple-element.50), channel_id=1, source_target_pairs={{0,8},{1,9},{2,10},{3,11},{4,12},{5,13},{6,14},{7,15},{8,0},{9,1},... | collective-permute-start | bytes 393224 | tf_op jit(solution)/shard_map/ppermute | solution.py:224
  66.3 2.4 %collective-permute-start.11 = (f32[8,2,16,128]{3,2,1,0:T(8,128)S(1)}, f32[8,2,16,128]{3,2,1,0:T(8,128)S(1)}, u32[]{:S(2)}, u32[]{:S(2)}) collective-permute-start(f32[8,2,16,128]{3,2,1,0:T(8,128)S(1)} %get-tuple-element.51), channel_id=1, source_target_pairs={{0,16},{1,17},{2,18},{3,19},{4,20},{5,21},{6,22},{7,23},{8,24},{9,... | collective-permute-start | bytes 393224 | tf_op jit(solution)/shard_map/ppermute | solution.py:224
  68.7 0.2 collective-permute-start.12
  68.9 8.3 %collective-permute-done.10.refs_1_ = f32[8,2,16,128]{3,2,1,0:T(8,128)S(1)} collective-permute-done((f32[8,2,16,128]{3,2,1,0:T(8,128)S(1)}, f32[8,2,16,128]{3,2,1,0:T(8,128)S(1)}, u32[]{:S(2)}, u32[]{:S(2)}) %collective-permute-start.10) | collective-permute-done | bytes 131104 | tf_op jit(solution)/shard_map/ppermute | solution.py:224
  77.2 11.0 %collective-permute-done.11.refs_2_ = f32[8,2,16,128]{3,2,1,0:T(8,128)S(1)} collective-permute-done((f32[8,2,16,128]{3,2,1,0:T(8,128)S(1)}, f32[8,2,16,128]{3,2,1,0:T(8,128)S(1)}, u32[]{:S(2)}, u32[]{:S(2)}) %collective-permute-start.11) | collective-permute-done | bytes 131104 | tf_op jit(solution)/shard_map/ppermute | solution.py:224
  88.2 1.5 %collective-permute-start.13 = (f32[4,2,16,128]{3,2,1,0:T(8,128)S(1)}, f32[4,2,16,128]{3,2,1,0:T(8,128)S(1)}, u32[]{:S(2)}, u32[]{:S(2)}) collective-permute-start(f32[4,2,16,128]{3,2,1,0:T(8,128)S(1)} %get-tuple-element.54), channel_id=1, source_target_pairs={{0,1},{1,0},{2,3},{3,2},{4,5},{5,4},{6,7},{7,6},{8,9},{9,8},{10,11... | collective-permute-start | bytes 196616 | tf_op jit(solution)/shard_map/ppermute | solution.py:224
  89.8 0.7 collective-permute-start.15
  90.4 1.5 %collective-permute-start.16 = (f32[4,2,16,128]{3,2,1,0:T(8,128)S(1)}, f32[4,2,16,128]{3,2,1,0:T(8,128)S(1)}, u32[]{:S(2)}, u32[]{:S(2)}) collective-permute-start(f32[4,2,16,128]{3,2,1,0:T(8,128)S(1)} %get-tuple-element.57), channel_id=1, source_target_pairs={{0,4},{1,5},{2,6},{3,7},{4,0},{5,1},{6,2},{7,3},{8,12},{9,13},{10,... | collective-permute-start | bytes 196616 | tf_op jit(solution)/shard_map/ppermute | solution.py:224
  91.9 1.5 %collective-permute-start.17 = (f32[4,2,16,128]{3,2,1,0:T(8,128)S(1)}, f32[4,2,16,128]{3,2,1,0:T(8,128)S(1)}, u32[]{:S(2)}, u32[]{:S(2)}) collective-permute-start(f32[4,2,16,128]{3,2,1,0:T(8,128)S(1)} %get-tuple-element.58), channel_id=1, source_target_pairs={{0,5},{1,4},{2,7},{3,6},{4,1},{5,0},{6,3},{7,2},{8,13},{9,12},{10,... | collective-permute-start | bytes 196616 | tf_op jit(solution)/shard_map/ppermute | solution.py:224
  93.4 0.0 collective-permute-done.13.refs_1_
  93.4 0.5 collective-permute-start.18
  93.9 0.0 collective-permute-done.14.refs_2_
  93.9 2.0 %collective-permute-start.19 = (f32[4,2,16,128]{3,2,1,0:T(8,128)S(1)}, f32[4,2,16,128]{3,2,1,0:T(8,128)S(1)}, u32[]{:S(2)}, u32[]{:S(2)}) collective-permute-start(f32[4,2,16,128]{3,2,1,0:T(8,128)S(1)} %get-tuple-element.60), channel_id=1, source_target_pairs={{0,7},{1,6},{2,5},{3,4},{4,3},{5,2},{6,1},{7,0},{8,15},{9,14},{10,... | collective-permute-start | bytes 196616 | tf_op jit(solution)/shard_map/ppermute | solution.py:224
  95.9 0.0 collective-permute-done.16.refs_4_
  95.9 1.2 %collective-permute-done.17.refs_5_ = f32[4,2,16,128]{3,2,1,0:T(8,128)S(1)} collective-permute-done((f32[4,2,16,128]{3,2,1,0:T(8,128)S(1)}, f32[4,2,16,128]{3,2,1,0:T(8,128)S(1)}, u32[]{:S(2)}, u32[]{:S(2)}) %collective-permute-start.17) | collective-permute-done | bytes 65568 | tf_op jit(solution)/shard_map/ppermute | solution.py:224
  97.1 0.7 collective-permute-done.18.refs_6_
  97.7 1.7 %collective-permute-done.19.refs_7_ = f32[4,2,16,128]{3,2,1,0:T(8,128)S(1)} collective-permute-done((f32[4,2,16,128]{3,2,1,0:T(8,128)S(1)}, f32[4,2,16,128]{3,2,1,0:T(8,128)S(1)}, u32[]{:S(2)}, u32[]{:S(2)}) %collective-permute-start.19) | collective-permute-done | bytes 65568 | tf_op jit(solution)/shard_map/ppermute | solution.py:224
  99.4 0.6 shard_map.43.few_ref
  100.0 1.2 %shard_map.45 = f32[2,1024,128]{2,1,0:T(8,128)} custom-call(f32[32,2,16,128]{3,2,1,0:T(8,128)S(1)} %shard_map.43.few_ref, f32[32,2,16,128]{3,2,1,0:T(8,128)S(1)} %all-to-all-done.1.most_ref), custom_call_target="tpu_custom_call" | custom-call | tf_op jit(solution)/shard_map/pallas_call | solution.py:310
  (15 shorter events, 0.2 us)
Async XLA Ops:
  3.9 54.3 %all-to-all-start = ((f32[32,2,32,128]{3,2,1,0:T(8,128)}), f32[32,2,32,128]{3,2,1,0:T(8,128)S(1)}, u32[]{:S(2)}, u32[]{:S(2)}) async-start(f32[32,2,32,128]{3,2,1,0:T(8,128)} %shard_map.38), calls=%async_computation | async-start | bytes 2097152 | tf_op jit(solution)/shard_map/all_to_all | solution.py:277
  11.3 20.8 %collective-permute-start = (f32[8,32,128]{2,1,0:T(8,128)S(1)}, f32[8,32,128]{2,1,0:T(8,128)S(1)}, u32[]{:S(2)}, u32[]{:S(2)}) collective-permute-start(f32[8,32,128]{2,1,0:T(8,128)S(1)} %get-tuple-element.36), channel_id=1, source_target_pairs={{0,8},{1,9},{2,10},{3,11},{4,12},{5,13},{6,14},{7,15},{8,0},{9,1},... | collective-permute-start | bytes 393224 | tf_op jit(solution)/shard_map/ppermute | solution.py:224
  13.1 33.4 %collective-permute-start.1 = (f32[8,32,128]{2,1,0:T(8,128)S(1)}, f32[8,32,128]{2,1,0:T(8,128)S(1)}, u32[]{:S(2)}, u32[]{:S(2)}) collective-permute-start(f32[8,32,128]{2,1,0:T(8,128)S(1)} %get-tuple-element.37), channel_id=1, source_target_pairs={{0,16},{1,17},{2,18},{3,19},{4,20},{5,21},{6,22},{7,23},{8,24},{9,... | collective-permute-start | bytes 393224 | tf_op jit(solution)/shard_map/ppermute | solution.py:224
  15.5 31.0 %collective-permute-start.2 = (f32[8,32,128]{2,1,0:T(8,128)S(1)}, f32[8,32,128]{2,1,0:T(8,128)S(1)}, u32[]{:S(2)}, u32[]{:S(2)}) collective-permute-start(f32[8,32,128]{2,1,0:T(8,128)S(1)} %get-tuple-element.38), channel_id=1, source_target_pairs={{0,24},{1,25},{2,26},{3,27},{4,28},{5,29},{6,30},{7,31},{8,16},{9,... | collective-permute-start | bytes 393224 | tf_op jit(solution)/shard_map/ppermute | solution.py:224
  46.5 5.3 %collective-permute-start.3 = (f32[4,32,128]{2,1,0:T(8,128)S(1)}, f32[4,32,128]{2,1,0:T(8,128)S(1)}, u32[]{:S(2)}, u32[]{:S(2)}) collective-permute-start(f32[4,32,128]{2,1,0:T(8,128)S(1)} %get-tuple-element.40), channel_id=1, source_target_pairs={{0,1},{1,0},{2,3},{3,2},{4,5},{5,4},{6,7},{7,6},{8,9},{9,8},{10,11... | collective-permute-start | bytes 196616 | tf_op jit(solution)/shard_map/ppermute | solution.py:224
  48.1 4.3 %collective-permute-start.4 = (f32[4,32,128]{2,1,0:T(8,128)S(1)}, f32[4,32,128]{2,1,0:T(8,128)S(1)}, u32[]{:S(2)}, u32[]{:S(2)}) collective-permute-start(f32[4,32,128]{2,1,0:T(8,128)S(1)} %get-tuple-element.41), channel_id=1, source_target_pairs={{0,2},{1,3},{2,0},{3,1},{4,6},{5,7},{6,4},{7,5},{8,10},{9,11},{10,... | collective-permute-start | bytes 196616 | tf_op jit(solution)/shard_map/ppermute | solution.py:224
  48.1 5.9 %collective-permute-start.5 = (f32[4,32,128]{2,1,0:T(8,128)S(1)}, f32[4,32,128]{2,1,0:T(8,128)S(1)}, u32[]{:S(2)}, u32[]{:S(2)}) collective-permute-start(f32[4,32,128]{2,1,0:T(8,128)S(1)} %get-tuple-element.42), channel_id=1, source_target_pairs={{0,3},{1,2},{2,1},{3,0},{4,7},{5,6},{6,5},{7,4},{8,11},{9,10},{10,... | collective-permute-start | bytes 196616 | tf_op jit(solution)/shard_map/ppermute | solution.py:224
  48.9 5.2 %collective-permute-start.6 = (f32[4,32,128]{2,1,0:T(8,128)S(1)}, f32[4,32,128]{2,1,0:T(8,128)S(1)}, u32[]{:S(2)}, u32[]{:S(2)}) collective-permute-start(f32[4,32,128]{2,1,0:T(8,128)S(1)} %get-tuple-element.43), channel_id=1, source_target_pairs={{0,4},{1,5},{2,6},{3,7},{4,0},{5,1},{6,2},{7,3},{8,12},{9,13},{10,... | collective-permute-start | bytes 196616 | tf_op jit(solution)/shard_map/ppermute | solution.py:224
  50.3 5.4 %collective-permute-start.7 = (f32[4,32,128]{2,1,0:T(8,128)S(1)}, f32[4,32,128]{2,1,0:T(8,128)S(1)}, u32[]{:S(2)}, u32[]{:S(2)}) collective-permute-start(f32[4,32,128]{2,1,0:T(8,128)S(1)} %get-tuple-element.44), channel_id=1, source_target_pairs={{0,5},{1,4},{2,7},{3,6},{4,1},{5,0},{6,3},{7,2},{8,13},{9,12},{10,... | collective-permute-start | bytes 196616 | tf_op jit(solution)/shard_map/ppermute | solution.py:224
  51.8 4.4 %collective-permute-start.8 = (f32[4,32,128]{2,1,0:T(8,128)S(1)}, f32[4,32,128]{2,1,0:T(8,128)S(1)}, u32[]{:S(2)}, u32[]{:S(2)}) collective-permute-start(f32[4,32,128]{2,1,0:T(8,128)S(1)} %get-tuple-element.45), channel_id=1, source_target_pairs={{0,6},{1,7},{2,4},{3,5},{4,2},{5,3},{6,0},{7,1},{8,14},{9,15},{10,... | collective-permute-start | bytes 196616 | tf_op jit(solution)/shard_map/ppermute | solution.py:224
  52.4 5.4 %collective-permute-start.9 = (f32[4,32,128]{2,1,0:T(8,128)S(1)}, f32[4,32,128]{2,1,0:T(8,128)S(1)}, u32[]{:S(2)}, u32[]{:S(2)}) collective-permute-start(f32[4,32,128]{2,1,0:T(8,128)S(1)} %get-tuple-element.46), channel_id=1, source_target_pairs={{0,7},{1,6},{2,5},{3,4},{4,3},{5,2},{6,1},{7,0},{8,15},{9,14},{10,... | collective-permute-start | bytes 196616 | tf_op jit(solution)/shard_map/ppermute | solution.py:224
  59.7 40.3 %all-to-all-start.1 = ((f32[32,2,16,128]{3,2,1,0:T(8,128)}), f32[32,2,16,128]{3,2,1,0:T(8,128)S(1)}, u32[]{:S(2)}, u32[]{:S(2)}) async-start(f32[32,2,16,128]{3,2,1,0:T(8,128)} %shard_map.44), calls=%async_computation.1 | async-start | bytes 1048576 | tf_op jit(solution)/shard_map/all_to_all | solution.py:300
  64.5 12.7 %collective-permute-start.10 = (f32[8,2,16,128]{3,2,1,0:T(8,128)S(1)}, f32[8,2,16,128]{3,2,1,0:T(8,128)S(1)}, u32[]{:S(2)}, u32[]{:S(2)}) collective-permute-start(f32[8,2,16,128]{3,2,1,0:T(8,128)S(1)} %get-tuple-element.50), channel_id=1, source_target_pairs={{0,8},{1,9},{2,10},{3,11},{4,12},{5,13},{6,14},{7,15},{8,0},{9,1},... | collective-permute-start | bytes 393224 | tf_op jit(solution)/shard_map/ppermute | solution.py:224
  66.3 21.9 %collective-permute-start.11 = (f32[8,2,16,128]{3,2,1,0:T(8,128)S(1)}, f32[8,2,16,128]{3,2,1,0:T(8,128)S(1)}, u32[]{:S(2)}, u32[]{:S(2)}) collective-permute-start(f32[8,2,16,128]{3,2,1,0:T(8,128)S(1)} %get-tuple-element.51), channel_id=1, source_target_pairs={{0,16},{1,17},{2,18},{3,19},{4,20},{5,21},{6,22},{7,23},{8,24},{9,... | collective-permute-start | bytes 393224 | tf_op jit(solution)/shard_map/ppermute | solution.py:224
  68.7 19.5 %collective-permute-start.12 = (f32[8,2,16,128]{3,2,1,0:T(8,128)S(1)}, f32[8,2,16,128]{3,2,1,0:T(8,128)S(1)}, u32[]{:S(2)}, u32[]{:S(2)}) collective-permute-start(f32[8,2,16,128]{3,2,1,0:T(8,128)S(1)} %get-tuple-element.52), channel_id=1, source_target_pairs={{0,24},{1,25},{2,26},{3,27},{4,28},{5,29},{6,30},{7,31},{8,16},{9,... | collective-permute-start | bytes 393224 | tf_op jit(solution)/shard_map/ppermute | solution.py:224
  88.2 5.2 %collective-permute-start.13 = (f32[4,2,16,128]{3,2,1,0:T(8,128)S(1)}, f32[4,2,16,128]{3,2,1,0:T(8,128)S(1)}, u32[]{:S(2)}, u32[]{:S(2)}) collective-permute-start(f32[4,2,16,128]{3,2,1,0:T(8,128)S(1)} %get-tuple-element.54), channel_id=1, source_target_pairs={{0,1},{1,0},{2,3},{3,2},{4,5},{5,4},{6,7},{7,6},{8,9},{9,8},{10,11... | collective-permute-start | bytes 196616 | tf_op jit(solution)/shard_map/ppermute | solution.py:224
  89.8 4.1 %collective-permute-start.14 = (f32[4,2,16,128]{3,2,1,0:T(8,128)S(1)}, f32[4,2,16,128]{3,2,1,0:T(8,128)S(1)}, u32[]{:S(2)}, u32[]{:S(2)}) collective-permute-start(f32[4,2,16,128]{3,2,1,0:T(8,128)S(1)} %get-tuple-element.55), channel_id=1, source_target_pairs={{0,2},{1,3},{2,0},{3,1},{4,6},{5,7},{6,4},{7,5},{8,10},{9,11},{10,... | collective-permute-start | bytes 196616 | tf_op jit(solution)/shard_map/ppermute | solution.py:224
  89.8 6.1 %collective-permute-start.15 = (f32[4,2,16,128]{3,2,1,0:T(8,128)S(1)}, f32[4,2,16,128]{3,2,1,0:T(8,128)S(1)}, u32[]{:S(2)}, u32[]{:S(2)}) collective-permute-start(f32[4,2,16,128]{3,2,1,0:T(8,128)S(1)} %get-tuple-element.56), channel_id=1, source_target_pairs={{0,3},{1,2},{2,1},{3,0},{4,7},{5,6},{6,5},{7,4},{8,11},{9,10},{10,... | collective-permute-start | bytes 196616 | tf_op jit(solution)/shard_map/ppermute | solution.py:224
  90.4 5.5 %collective-permute-start.16 = (f32[4,2,16,128]{3,2,1,0:T(8,128)S(1)}, f32[4,2,16,128]{3,2,1,0:T(8,128)S(1)}, u32[]{:S(2)}, u32[]{:S(2)}) collective-permute-start(f32[4,2,16,128]{3,2,1,0:T(8,128)S(1)} %get-tuple-element.57), channel_id=1, source_target_pairs={{0,4},{1,5},{2,6},{3,7},{4,0},{5,1},{6,2},{7,3},{8,12},{9,13},{10,... | collective-permute-start | bytes 196616 | tf_op jit(solution)/shard_map/ppermute | solution.py:224
  91.9 5.2 %collective-permute-start.17 = (f32[4,2,16,128]{3,2,1,0:T(8,128)S(1)}, f32[4,2,16,128]{3,2,1,0:T(8,128)S(1)}, u32[]{:S(2)}, u32[]{:S(2)}) collective-permute-start(f32[4,2,16,128]{3,2,1,0:T(8,128)S(1)} %get-tuple-element.58), channel_id=1, source_target_pairs={{0,5},{1,4},{2,7},{3,6},{4,1},{5,0},{6,3},{7,2},{8,13},{9,12},{10,... | collective-permute-start | bytes 196616 | tf_op jit(solution)/shard_map/ppermute | solution.py:224
  93.4 4.4 %collective-permute-start.18 = (f32[4,2,16,128]{3,2,1,0:T(8,128)S(1)}, f32[4,2,16,128]{3,2,1,0:T(8,128)S(1)}, u32[]{:S(2)}, u32[]{:S(2)}) collective-permute-start(f32[4,2,16,128]{3,2,1,0:T(8,128)S(1)} %get-tuple-element.59), channel_id=1, source_target_pairs={{0,6},{1,7},{2,4},{3,5},{4,2},{5,3},{6,0},{7,1},{8,14},{9,15},{10,... | collective-permute-start | bytes 196616 | tf_op jit(solution)/shard_map/ppermute | solution.py:224
  93.9 5.5 %collective-permute-start.19 = (f32[4,2,16,128]{3,2,1,0:T(8,128)S(1)}, f32[4,2,16,128]{3,2,1,0:T(8,128)S(1)}, u32[]{:S(2)}, u32[]{:S(2)}) collective-permute-start(f32[4,2,16,128]{3,2,1,0:T(8,128)S(1)} %get-tuple-element.60), channel_id=1, source_target_pairs={{0,7},{1,6},{2,5},{3,4},{4,3},{5,2},{6,1},{7,0},{8,15},{9,14},{10,... | collective-permute-start | bytes 196616 | tf_op jit(solution)/shard_map/ppermute | solution.py:224

commit v4 on v3

--- a/solution.py
+++ b/solution.py
@@ -75,10 +75,10 @@
         copy.wait()
 
 
-def first_kernel(devices, part, scale, wave_ref, level_ref, angle_ref, right_ref, left_ref, out_ref, held):
+def first_kernel(slots, part, scale, wave_ref, level_ref, angle_ref, right_ref, left_ref, out_ref, held):
     lanes = wave_ref.shape[2]
     block = left_ref.shape[0]
-    groups, per = devices * part // block, block // part
+    groups, per = len(slots) * part // block, block // part
     right, left = right_ref[...], left_ref[...]
     angle = jnp.broadcast_to(angle_ref[0:1, :], (block, lanes))
     for g in range(groups):
@@ -91,7 +91,7 @@
             values = butterflies([held[p, g * block + tile * 8:g * block + tile * 8 + 8, :] for g in range(groups)])
             k, row = tile * 8 // part, tile * 8 % part
             for g, value in enumerate(values):
-                out_ref[g * per + k, p, row:row + 8, :] = value
+                out_ref[slots[g * per + k], p, row:row + 8, :] = value
 
 
 def deal_kernel(slabs, size, place_ref, *refs):
@@ -110,12 +110,12 @@
             cos_ref[whose], sin_ref[whose] = trig(angle * level_refs[k][m], scale)
 
 
-def turn_devices(slabs, size, tiles, seen_ref, cos_ref, sin_ref, held):
+def turn_devices(slabs, size, slots, tiles, seen_ref, cos_ref, sin_ref, held):
     for tile in tiles:
         rows = slice(tile * 8, tile * 8 + 8)
         for z in range(slabs):
             for p in range(2):
-                values = butterflies([seen_ref[z * size + q, p, rows, :] for q in range(size)])
+                values = butterflies([seen_ref[slots[z * size + q], p, rows, :] for q in range(size)])
                 for q, value in enumerate(values):
                     held[z * size + q, p, rows, :] = value
         for q in range(size):
@@ -128,10 +128,10 @@
                     held[z * size + q, p, rows, :] = value
 
 
-def few_kernel(slabs, size, place_ref, seen_ref, cos_ref, sin_ref, *refs):
+def few_kernel(slabs, size, slots, place_ref, seen_ref, cos_ref, sin_ref, *refs):
     outs, held = refs[:slabs], refs[slabs]
     count = outs[0].shape[2] // 8
-    turn_devices(slabs, size, range(count), seen_ref, cos_ref, sin_ref, held)
+    turn_devices(slabs, size, slots, range(count), seen_ref, cos_ref, sin_ref, held)
     mine = place_ref[0] // size
     for m in range(slabs):
         for p in range(2):
@@ -142,11 +142,11 @@
                     outs[m][q, p, rows, :] = value
 
 
-def most_kernel(slabs, size, seen_ref, cos_ref, sin_ref, right_ref, left_ref, out_ref, held):
+def most_kernel(slabs, size, slots, seen_ref, cos_ref, sin_ref, right_ref, left_ref, out_ref, held):
     part, lanes = seen_ref.shape[2:]
     devices = slabs * size
     start = (part - out_ref.shape[2]) // 8
-    turn_devices(slabs, size, range(start, part // 8), seen_ref, cos_ref, sin_ref, held)
+    turn_devices(slabs, size, slots, range(start, part // 8), seen_ref, cos_ref, sin_ref, held)
     right, left = right_ref[...], left_ref[...]
     step = left.shape[0] // 8
     for tile in range(start, part // 8):
@@ -231,6 +231,13 @@
 FAR = pl.BlockSpec(memory_space=pltpu.HBM)
 
 
+def device_order(devices, core):
+    low, high = core.bit_length() - 1, devices.bit_length() - 1
+    bits = [high - 1, *range(low - 1, -1, -1), low + 1, *range(high - 2, low + 1, -1), low]
+    order = [sum((rank >> (high - 1 - i) & 1) << bit for i, bit in enumerate(bits)) for rank in range(devices)]
+    return order, [order.index(d) for d in range(devices)]
+
+
 def kernel_call(kernel, in_specs, out_shape, scratch=(), out_specs=None):
     count = len(out_shape) if isinstance(out_shape, list) else 0
     return pl.pallas_call(
@@ -243,13 +250,14 @@
     )
 
 
-def body_fast(axes, devices, slabs, wave, levels, angles):
+def body_fast(axes, devices, slabs, core, wave, levels, angles):
     blocks, rows, lanes = levels.shape
     total = blocks * rows
     part = total // devices
     size = devices // slabs
     count = FEW
     scale = float(devices * total * lanes) ** -0.5
+    order, slots = device_order(devices, core)
     place = lax.axis_index(axes).astype(jnp.int32).reshape(1)
     wave = wave.reshape(2, total, lanes)
     levels = levels.reshape(devices, part, lanes)
@@ -271,10 +279,10 @@
     for m in range(1, slabs):
         mine.append(swap(picked[m - 1], axes, devices, m * size))
     sent = kernel_call(
-        functools.partial(first_kernel, devices, part, scale), [WHOLE] * 5,
+        functools.partial(first_kernel, slots, part, scale), [WHOLE] * 5,
         flat(devices, 2, part, lanes), [held_shape(2, total, lanes)],
     )(near(wave), near(levels.reshape(total, lanes)), near(angles), right, left)
-    seen = lax.all_to_all(sent, axes, 0, 0, tiled=True)
+    seen = lax.all_to_all(sent, axes, 0, 0, tiled=True, axis_index_groups=[order])
     dealt = kernel_call(
         functools.partial(deal_kernel, slabs, size), [SCALAR] + [WHOLE] * slabs,
         [held_shape(slabs, part, lanes)] * size,
@@ -287,14 +295,14 @@
 
     seen = near(seen)
     few = kernel_call(
-        functools.partial(few_kernel, slabs, size), [SCALAR] + [WHOLE] * 3,
+        functools.partial(few_kernel, slabs, size, slots), [SCALAR] + [WHOLE] * 3,
         [held_shape(size, 2, count, lanes)] * slabs, [held_shape(devices, 2, count, lanes)],
     )(place, seen, cos, sin)
     few = [few[0], *few[1:]]
     for m in range(1, slabs):
         few[m] = swap(few[m], axes, devices, m * size)
     most = kernel_call(
-        functools.partial(most_kernel, slabs, size), [WHOLE] * 5,
+        functools.partial(most_kernel, slabs, size, slots), [WHOLE] * 5,
         flat(devices, 2, part - count, lanes), [held_shape(devices, 2, part, lanes)],
     )(seen, cos, sin, right, left_small)
     most = lax.all_to_all(most, axes, 0, 0, tiled=True)
@@ -354,7 +362,7 @@
         fast = part % 16 == 0 and 128 % part == 0 and total % 128 == 0 and devices % 16 == 0
         slabs = mesh.shape["qa"] // 4
         if fast and slabs > 1:
-            return body_fast(axes, devices, slabs, wave, levels, angles)
+            return body_fast(axes, devices, slabs, mesh.shape["qb"], wave, levels, angles)
         return body_plain(axes, devices, wave, levels, angles)
 
     in_specs = (P(None, axes, None, None), P(axes, None, None), P())

time: 102 us -> 102 us (level)
  no operation moved by 1% of the time
where the time goes in v4:
time: 102 us; the launch traced here: 101 us
  waiting for transfers between devices  56.6 us (55%)
  starting transfers between devices  35.8 us (35%)
  Pallas kernels  7.9 us (8%)
    ppermute x20, waiting for transfers between devices, swap(): return lax.ppermute(x, axes, [(i, i ^ mask) for i in range(devices)])  56.6 us
    ppermute x20, starting transfers between devices, swap(): return lax.ppermute(x, axes, [(i, i ^ mask) for i in range(devices)])  24 us
    all_to_all x1, starting transfers between devices, body_fast(): lax.all_to_all(sent, axes, 0, 0, tiled=True, axis_index_groups=[order])  7.33 us
    all_to_all x1, starting transfers between devices, body_fast(): most = lax.all_to_all(most, axes, 0, 0, tiled=True)  4.4 us
    pallas_call x1, Pallas kernels, body_fast(): kernel_call(functools.partial(first_kernel, slots, part, scale), [WHOLE]...  2.3 us
  transfers between devices with their start and end apart: 22, of which 10 were waited for; matrix products, arithmetic and copies ran while one was open for 1% of the time, Pallas kernels for 1%

profile of v4, /device:TPU:0, one launch (start us, length us, event | category | flops | bytes accessed | tf_op | source)
XLA Modules:
  0.0 101.2 jit_solution(13099707248639605690)
XLA Ops:
  0.1 1.5 %shard_map.37 = (f32[2,1024,128]{2,1,0:T(8,128)S(1)}, f32[32,32,128]{2,1,0:T(8,128)S(1)}, f32[2,128]{1,0:T(2,128)S(1)}, f32[8,32,128]{2,1,0:T(8,128)S(1)}, f32[8...) custom-call(s32[1]{0:T(128)} %bitcast.place_ref, f32[2,1024,128]{2,1,0:T(8,128)} %bitcast.8, f32[32,32,128]{2,1,0:T(8,128)} %bitcast.9, ...), custom_call_target="tpu_custom_call" | custom-call | tf_op jit(solution)/shard_map/pallas_call | solution.py:272
  1.6 2.3 %shard_map.38 = f32[32,2,32,128]{3,2,1,0:T(8,128)} custom-call(f32[2,1024,128]{2,1,0:T(8,128)S(1)} %get-tuple-element.33.wave_ref, f32[1024,128]{1,0:T(8,128)S(1)} %bitcast.7, f32[2,128]{1,0:T(2,128)S(1)} %get-tuple-element.35.angle_ref, bf16[256,128]{1,0:T(8,128)(2,1)S(1)} %pad_maximum_fusion.right_ref, bf16[128,256]{1,0:T(8,128)(2,1)S(1)} %pad_maximum_fusion.2.left_ref), custom_call_target="tpu_custom_call" | custom-call | tf_op jit(solution)/shard_map/pallas_call | solution.py:281
  3.9 7.3 %all-to-all-start = ((f32[32,2,32,128]{3,2,1,0:T(8,128)}), f32[32,2,32,128]{3,2,1,0:T(8,128)S(1)}, u32[]{:S(2)}, u32[]{:S(2)}) async-start(f32[32,2,32,128]{3,2,1,0:T(8,128)} %shard_map.38), calls=%async_computation | async-start | bytes 2097152 | tf_op jit(solution)/shard_map/all_to_all | solution.py:285
  11.3 1.8 %collective-permute-start = (f32[8,32,128]{2,1,0:T(8,128)S(1)}, f32[8,32,128]{2,1,0:T(8,128)S(1)}, u32[]{:S(2)}, u32[]{:S(2)}) collective-permute-start(f32[8,32,128]{2,1,0:T(8,128)S(1)} %get-tuple-element.36), channel_id=1, source_target_pairs={{0,8},{1,9},{2,10},{3,11},{4,12},{5,13},{6,14},{7,15},{8,0},{9,1},... | collective-permute-start | bytes 393224 | tf_op jit(solution)/shard_map/ppermute | solution.py:224
  13.1 2.4 %collective-permute-start.1 = (f32[8,32,128]{2,1,0:T(8,128)S(1)}, f32[8,32,128]{2,1,0:T(8,128)S(1)}, u32[]{:S(2)}, u32[]{:S(2)}) collective-permute-start(f32[8,32,128]{2,1,0:T(8,128)S(1)} %get-tuple-element.37), channel_id=1, source_target_pairs={{0,16},{1,17},{2,18},{3,19},{4,20},{5,21},{6,22},{7,23},{8,24},{9,... | collective-permute-start | bytes 393224 | tf_op jit(solution)/shard_map/ppermute | solution.py:224
  15.5 0.2 collective-permute-start.2
  15.8 0.1 tile.13
  15.9 0.5 tile.14
  16.4 15.6 %collective-permute-done.refs_1_ = f32[8,32,128]{2,1,0:T(8,128)S(1)} collective-permute-done((f32[8,32,128]{2,1,0:T(8,128)S(1)}, f32[8,32,128]{2,1,0:T(8,128)S(1)}, u32[]{:S(2)}, u32[]{:S(2)}) %collective-permute-start) | collective-permute-done | bytes 131104 | tf_op jit(solution)/shard_map/ppermute | solution.py:224
  32.0 14.5 %collective-permute-done.1.refs_2_ = f32[8,32,128]{2,1,0:T(8,128)S(1)} collective-permute-done((f32[8,32,128]{2,1,0:T(8,128)S(1)}, f32[8,32,128]{2,1,0:T(8,128)S(1)}, u32[]{:S(2)}, u32[]{:S(2)}) %collective-permute-start.1) | collective-permute-done | bytes 131104 | tf_op jit(solution)/shard_map/ppermute | solution.py:224
  46.5 0.0 collective-permute-done.2.refs_3_
  46.5 1.5 %collective-permute-start.3 = (f32[4,32,128]{2,1,0:T(8,128)S(1)}, f32[4,32,128]{2,1,0:T(8,128)S(1)}, u32[]{:S(2)}, u32[]{:S(2)}) collective-permute-start(f32[4,32,128]{2,1,0:T(8,128)S(1)} %get-tuple-element.40), channel_id=1, source_target_pairs={{0,1},{1,0},{2,3},{3,2},{4,5},{5,4},{6,7},{7,6},{8,9},{9,8},{10,11... | collective-permute-start | bytes 196616 | tf_op jit(solution)/shard_map/ppermute | solution.py:224
  48.0 0.0 collective-permute-start.4
  48.1 0.1 compare_select_fusion
  48.1 0.7 collective-permute-start.5
  48.9 1.5 %collective-permute-start.6 = (f32[4,32,128]{2,1,0:T(8,128)S(1)}, f32[4,32,128]{2,1,0:T(8,128)S(1)}, u32[]{:S(2)}, u32[]{:S(2)}) collective-permute-start(f32[4,32,128]{2,1,0:T(8,128)S(1)} %get-tuple-element.43), channel_id=1, source_target_pairs={{0,4},{1,5},{2,6},{3,7},{4,0},{5,1},{6,2},{7,3},{8,12},{9,13},{10,... | collective-permute-start | bytes 196616 | tf_op jit(solution)/shard_map/ppermute | solution.py:224
  50.4 1.4 %collective-permute-start.7 = (f32[4,32,128]{2,1,0:T(8,128)S(1)}, f32[4,32,128]{2,1,0:T(8,128)S(1)}, u32[]{:S(2)}, u32[]{:S(2)}) collective-permute-start(f32[4,32,128]{2,1,0:T(8,128)S(1)} %get-tuple-element.44), channel_id=1, source_target_pairs={{0,5},{1,4},{2,7},{3,6},{4,1},{5,0},{6,3},{7,2},{8,13},{9,12},{10,... | collective-permute-start | bytes 196616 | tf_op jit(solution)/shard_map/ppermute | solution.py:224
  51.8 0.0 collective-permute-done.3.refs_1_
  51.8 0.5 collective-permute-start.8
  52.3 0.0 collective-permute-done.4.refs_2_
  52.3 1.7 %collective-permute-start.9 = (f32[4,32,128]{2,1,0:T(8,128)S(1)}, f32[4,32,128]{2,1,0:T(8,128)S(1)}, u32[]{:S(2)}, u32[]{:S(2)}) collective-permute-start(f32[4,32,128]{2,1,0:T(8,128)S(1)} %get-tuple-element.46), channel_id=1, source_target_pairs={{0,7},{1,6},{2,5},{3,4},{4,3},{5,2},{6,1},{7,0},{8,15},{9,14},{10,... | collective-permute-start | bytes 196616 | tf_op jit(solution)/shard_map/ppermute | solution.py:224
  54.1 0.0 collective-permute-done.6.refs_4_
  54.1 1.7 %collective-permute-done.7.refs_5_ = f32[4,32,128]{2,1,0:T(8,128)S(1)} collective-permute-done((f32[4,32,128]{2,1,0:T(8,128)S(1)}, f32[4,32,128]{2,1,0:T(8,128)S(1)}, u32[]{:S(2)}, u32[]{:S(2)}) %collective-permute-start.7) | collective-permute-done | bytes 65568 | tf_op jit(solution)/shard_map/ppermute | solution.py:224
  55.8 0.4 collective-permute-done.8.refs_6_
  56.2 1.6 %collective-permute-done.9.refs_7_ = f32[4,32,128]{2,1,0:T(8,128)S(1)} collective-permute-done((f32[4,32,128]{2,1,0:T(8,128)S(1)}, f32[4,32,128]{2,1,0:T(8,128)S(1)}, u32[]{:S(2)}, u32[]{:S(2)}) %collective-permute-start.9) | collective-permute-done | bytes 65568 | tf_op jit(solution)/shard_map/ppermute | solution.py:224
  57.8 0.5 shard_map.40
  58.3 0.0 all-to-all-done.seen_ref
  58.3 1.5 %shard_map.44 = f32[32,2,16,128]{3,2,1,0:T(8,128)} custom-call(f32[32,2,32,128]{3,2,1,0:T(8,128)S(1)} %all-to-all-done.seen_ref, f32[32,32,128]{2,1,0:T(8,128)S(1)} %get-tuple-element.47.cos_ref, f32[32,32,128]{2,1,0:T(8,128)S(1)} %get-tuple-element.48.sin_ref, bf16[256,128]{1,0:T(8,128)(2,1)S(1)} %pad_maximum_fusion.right_ref, ...), custom_call_target="tpu_custom_call" | custom-call | tf_op jit(solution)/shard_map/pallas_call | solution.py:304
  59.8 4.4 %all-to-all-start.1 = ((f32[32,2,16,128]{3,2,1,0:T(8,128)}), f32[32,2,16,128]{3,2,1,0:T(8,128)S(1)}, u32[]{:S(2)}, u32[]{:S(2)}) async-start(f32[32,2,16,128]{3,2,1,0:T(8,128)} %shard_map.44), calls=%async_computation.1 | async-start | bytes 1048576 | tf_op jit(solution)/shard_map/all_to_all | solution.py:308
  64.2 0.3 shard_map.41
  64.5 1.8 %collective-permute-start.10 = (f32[8,2,16,128]{3,2,1,0:T(8,128)S(1)}, f32[8,2,16,128]{3,2,1,0:T(8,128)S(1)}, u32[]{:S(2)}, u32[]{:S(2)}) collective-permute-start(f32[8,2,16,128]{3,2,1,0:T(8,128)S(1)} %get-tuple-element.50), channel_id=1, source_target_pairs={{0,8},{1,9},{2,10},{3,11},{4,12},{5,13},{6,14},{7,15},{8,0},{9,1},... | collective-permute-start | bytes 393224 | tf_op jit(solution)/shard_map/ppermute | solution.py:224
  66.3 2.4 %collective-permute-start.11 = (f32[8,2,16,128]{3,2,1,0:T(8,128)S(1)}, f32[8,2,16,128]{3,2,1,0:T(8,128)S(1)}, u32[]{:S(2)}, u32[]{:S(2)}) collective-permute-start(f32[8,2,16,128]{3,2,1,0:T(8,128)S(1)} %get-tuple-element.51), channel_id=1, source_target_pairs={{0,16},{1,17},{2,18},{3,19},{4,20},{5,21},{6,22},{7,23},{8,24},{9,... | collective-permute-start | bytes 393224 | tf_op jit(solution)/shard_map/ppermute | solution.py:224
  68.7 0.2 collective-permute-start.12
  68.9 8.3 %collective-permute-done.10.refs_1_ = f32[8,2,16,128]{3,2,1,0:T(8,128)S(1)} collective-permute-done((f32[8,2,16,128]{3,2,1,0:T(8,128)S(1)}, f32[8,2,16,128]{3,2,1,0:T(8,128)S(1)}, u32[]{:S(2)}, u32[]{:S(2)}) %collective-permute-start.10) | collective-permute-done | bytes 131104 | tf_op jit(solution)/shard_map/ppermute | solution.py:224
  77.2 11.0 %collective-permute-done.11.refs_2_ = f32[8,2,16,128]{3,2,1,0:T(8,128)S(1)} collective-permute-done((f32[8,2,16,128]{3,2,1,0:T(8,128)S(1)}, f32[8,2,16,128]{3,2,1,0:T(8,128)S(1)}, u32[]{:S(2)}, u32[]{:S(2)}) %collective-permute-start.11) | collective-permute-done | bytes 131104 | tf_op jit(solution)/shard_map/ppermute | solution.py:224
  88.2 0.0 collective-permute-done.12.refs_3_
  88.2 1.5 %collective-permute-start.13 = (f32[4,2,16,128]{3,2,1,0:T(8,128)S(1)}, f32[4,2,16,128]{3,2,1,0:T(8,128)S(1)}, u32[]{:S(2)}, u32[]{:S(2)}) collective-permute-start(f32[4,2,16,128]{3,2,1,0:T(8,128)S(1)} %get-tuple-element.54), channel_id=1, source_target_pairs={{0,1},{1,0},{2,3},{3,2},{4,5},{5,4},{6,7},{7,6},{8,9},{9,8},{10,11... | collective-permute-start | bytes 196616 | tf_op jit(solution)/shard_map/ppermute | solution.py:224
  89.8 0.7 collective-permute-start.15
  90.4 1.5 %collective-permute-start.16 = (f32[4,2,16,128]{3,2,1,0:T(8,128)S(1)}, f32[4,2,16,128]{3,2,1,0:T(8,128)S(1)}, u32[]{:S(2)}, u32[]{:S(2)}) collective-permute-start(f32[4,2,16,128]{3,2,1,0:T(8,128)S(1)} %get-tuple-element.57), channel_id=1, source_target_pairs={{0,4},{1,5},{2,6},{3,7},{4,0},{5,1},{6,2},{7,3},{8,12},{9,13},{10,... | collective-permute-start | bytes 196616 | tf_op jit(solution)/shard_map/ppermute | solution.py:224
  91.9 1.5 %collective-permute-start.17 = (f32[4,2,16,128]{3,2,1,0:T(8,128)S(1)}, f32[4,2,16,128]{3,2,1,0:T(8,128)S(1)}, u32[]{:S(2)}, u32[]{:S(2)}) collective-permute-start(f32[4,2,16,128]{3,2,1,0:T(8,128)S(1)} %get-tuple-element.58), channel_id=1, source_target_pairs={{0,5},{1,4},{2,7},{3,6},{4,1},{5,0},{6,3},{7,2},{8,13},{9,12},{10,... | collective-permute-start | bytes 196616 | tf_op jit(solution)/shard_map/ppermute | solution.py:224
  93.4 0.5 collective-permute-start.18
  93.9 0.0 collective-permute-done.14.refs_2_
  93.9 2.0 %collective-permute-start.19 = (f32[4,2,16,128]{3,2,1,0:T(8,128)S(1)}, f32[4,2,16,128]{3,2,1,0:T(8,128)S(1)}, u32[]{:S(2)}, u32[]{:S(2)}) collective-permute-start(f32[4,2,16,128]{3,2,1,0:T(8,128)S(1)} %get-tuple-element.60), channel_id=1, source_target_pairs={{0,7},{1,6},{2,5},{3,4},{4,3},{5,2},{6,1},{7,0},{8,15},{9,14},{10,... | collective-permute-start | bytes 196616 | tf_op jit(solution)/shard_map/ppermute | solution.py:224
  95.9 1.2 %collective-permute-done.17.refs_5_ = f32[4,2,16,128]{3,2,1,0:T(8,128)S(1)} collective-permute-done((f32[4,2,16,128]{3,2,1,0:T(8,128)S(1)}, f32[4,2,16,128]{3,2,1,0:T(8,128)S(1)}, u32[]{:S(2)}, u32[]{:S(2)}) %collective-permute-start.17) | collective-permute-done | bytes 65568 | tf_op jit(solution)/shard_map/ppermute | solution.py:224
  97.1 0.7 collective-permute-done.18.refs_6_
  97.7 1.7 %collective-permute-done.19.refs_7_ = f32[4,2,16,128]{3,2,1,0:T(8,128)S(1)} collective-permute-done((f32[4,2,16,128]{3,2,1,0:T(8,128)S(1)}, f32[4,2,16,128]{3,2,1,0:T(8,128)S(1)}, u32[]{:S(2)}, u32[]{:S(2)}) %collective-permute-start.19) | collective-permute-done | bytes 65568 | tf_op jit(solution)/shard_map/ppermute | solution.py:224
  99.4 0.6 shard_map.43.few_ref
  100.0 1.2 %shard_map.45 = f32[2,1024,128]{2,1,0:T(8,128)} custom-call(f32[32,2,16,128]{3,2,1,0:T(8,128)S(1)} %shard_map.43.few_ref, f32[32,2,16,128]{3,2,1,0:T(8,128)S(1)} %all-to-all-done.1.most_ref), custom_call_target="tpu_custom_call" | custom-call | tf_op jit(solution)/shard_map/pallas_call | solution.py:318
  (15 shorter events, 0.2 us)
Async XLA Ops:
  3.9 54.4 %all-to-all-start = ((f32[32,2,32,128]{3,2,1,0:T(8,128)}), f32[32,2,32,128]{3,2,1,0:T(8,128)S(1)}, u32[]{:S(2)}, u32[]{:S(2)}) async-start(f32[32,2,32,128]{3,2,1,0:T(8,128)} %shard_map.38), calls=%async_computation | async-start | bytes 2097152 | tf_op jit(solution)/shard_map/all_to_all | solution.py:285
  11.3 20.7 %collective-permute-start = (f32[8,32,128]{2,1,0:T(8,128)S(1)}, f32[8,32,128]{2,1,0:T(8,128)S(1)}, u32[]{:S(2)}, u32[]{:S(2)}) collective-permute-start(f32[8,32,128]{2,1,0:T(8,128)S(1)} %get-tuple-element.36), channel_id=1, source_target_pairs={{0,8},{1,9},{2,10},{3,11},{4,12},{5,13},{6,14},{7,15},{8,0},{9,1},... | collective-permute-start | bytes 393224 | tf_op jit(solution)/shard_map/ppermute | solution.py:224
  13.1 33.4 %collective-permute-start.1 = (f32[8,32,128]{2,1,0:T(8,128)S(1)}, f32[8,32,128]{2,1,0:T(8,128)S(1)}, u32[]{:S(2)}, u32[]{:S(2)}) collective-permute-start(f32[8,32,128]{2,1,0:T(8,128)S(1)} %get-tuple-element.37), channel_id=1, source_target_pairs={{0,16},{1,17},{2,18},{3,19},{4,20},{5,21},{6,22},{7,23},{8,24},{9,... | collective-permute-start | bytes 393224 | tf_op jit(solution)/shard_map/ppermute | solution.py:224
  15.5 31.0 %collective-permute-start.2 = (f32[8,32,128]{2,1,0:T(8,128)S(1)}, f32[8,32,128]{2,1,0:T(8,128)S(1)}, u32[]{:S(2)}, u32[]{:S(2)}) collective-permute-start(f32[8,32,128]{2,1,0:T(8,128)S(1)} %get-tuple-element.38), channel_id=1, source_target_pairs={{0,24},{1,25},{2,26},{3,27},{4,28},{5,29},{6,30},{7,31},{8,16},{9,... | collective-permute-start | bytes 393224 | tf_op jit(solution)/shard_map/ppermute | solution.py:224
  46.5 5.3 %collective-permute-start.3 = (f32[4,32,128]{2,1,0:T(8,128)S(1)}, f32[4,32,128]{2,1,0:T(8,128)S(1)}, u32[]{:S(2)}, u32[]{:S(2)}) collective-permute-start(f32[4,32,128]{2,1,0:T(8,128)S(1)} %get-tuple-element.40), channel_id=1, source_target_pairs={{0,1},{1,0},{2,3},{3,2},{4,5},{5,4},{6,7},{7,6},{8,9},{9,8},{10,11... | collective-permute-start | bytes 196616 | tf_op jit(solution)/shard_map/ppermute | solution.py:224
  48.0 4.3 %collective-permute-start.4 = (f32[4,32,128]{2,1,0:T(8,128)S(1)}, f32[4,32,128]{2,1,0:T(8,128)S(1)}, u32[]{:S(2)}, u32[]{:S(2)}) collective-permute-start(f32[4,32,128]{2,1,0:T(8,128)S(1)} %get-tuple-element.41), channel_id=1, source_target_pairs={{0,2},{1,3},{2,0},{3,1},{4,6},{5,7},{6,4},{7,5},{8,10},{9,11},{10,... | collective-permute-start | bytes 196616 | tf_op jit(solution)/shard_map/ppermute | solution.py:224
  48.1 5.9 %collective-permute-start.5 = (f32[4,32,128]{2,1,0:T(8,128)S(1)}, f32[4,32,128]{2,1,0:T(8,128)S(1)}, u32[]{:S(2)}, u32[]{:S(2)}) collective-permute-start(f32[4,32,128]{2,1,0:T(8,128)S(1)} %get-tuple-element.42), channel_id=1, source_target_pairs={{0,3},{1,2},{2,1},{3,0},{4,7},{5,6},{6,5},{7,4},{8,11},{9,10},{10,... | collective-permute-start | bytes 196616 | tf_op jit(solution)/shard_map/ppermute | solution.py:224
  48.9 5.2 %collective-permute-start.6 = (f32[4,32,128]{2,1,0:T(8,128)S(1)}, f32[4,32,128]{2,1,0:T(8,128)S(1)}, u32[]{:S(2)}, u32[]{:S(2)}) collective-permute-start(f32[4,32,128]{2,1,0:T(8,128)S(1)} %get-tuple-element.43), channel_id=1, source_target_pairs={{0,4},{1,5},{2,6},{3,7},{4,0},{5,1},{6,2},{7,3},{8,12},{9,13},{10,... | collective-permute-start | bytes 196616 | tf_op jit(solution)/shard_map/ppermute | solution.py:224
  50.4 5.4 %collective-permute-start.7 = (f32[4,32,128]{2,1,0:T(8,128)S(1)}, f32[4,32,128]{2,1,0:T(8,128)S(1)}, u32[]{:S(2)}, u32[]{:S(2)}) collective-permute-start(f32[4,32,128]{2,1,0:T(8,128)S(1)} %get-tuple-element.44), channel_id=1, source_target_pairs={{0,5},{1,4},{2,7},{3,6},{4,1},{5,0},{6,3},{7,2},{8,13},{9,12},{10,... | collective-permute-start | bytes 196616 | tf_op jit(solution)/shard_map/ppermute | solution.py:224
  51.8 4.4 %collective-permute-start.8 = (f32[4,32,128]{2,1,0:T(8,128)S(1)}, f32[4,32,128]{2,1,0:T(8,128)S(1)}, u32[]{:S(2)}, u32[]{:S(2)}) collective-permute-start(f32[4,32,128]{2,1,0:T(8,128)S(1)} %get-tuple-element.45), channel_id=1, source_target_pairs={{0,6},{1,7},{2,4},{3,5},{4,2},{5,3},{6,0},{7,1},{8,14},{9,15},{10,... | collective-permute-start | bytes 196616 | tf_op jit(solution)/shard_map/ppermute | solution.py:224
  52.3 5.5 %collective-permute-start.9 = (f32[4,32,128]{2,1,0:T(8,128)S(1)}, f32[4,32,128]{2,1,0:T(8,128)S(1)}, u32[]{:S(2)}, u32[]{:S(2)}) collective-permute-start(f32[4,32,128]{2,1,0:T(8,128)S(1)} %get-tuple-element.46), channel_id=1, source_target_pairs={{0,7},{1,6},{2,5},{3,4},{4,3},{5,2},{6,1},{7,0},{8,15},{9,14},{10,... | collective-permute-start | bytes 196616 | tf_op jit(solution)/shard_map/ppermute | solution.py:224
  59.8 40.2 %all-to-all-start.1 = ((f32[32,2,16,128]{3,2,1,0:T(8,128)}), f32[32,2,16,128]{3,2,1,0:T(8,128)S(1)}, u32[]{:S(2)}, u32[]{:S(2)}) async-start(f32[32,2,16,128]{3,2,1,0:T(8,128)} %shard_map.44), calls=%async_computation.1 | async-start | bytes 1048576 | tf_op jit(solution)/shard_map/all_to_all | solution.py:308
  64.5 12.7 %collective-permute-start.10 = (f32[8,2,16,128]{3,2,1,0:T(8,128)S(1)}, f32[8,2,16,128]{3,2,1,0:T(8,128)S(1)}, u32[]{:S(2)}, u32[]{:S(2)}) collective-permute-start(f32[8,2,16,128]{3,2,1,0:T(8,128)S(1)} %get-tuple-element.50), channel_id=1, source_target_pairs={{0,8},{1,9},{2,10},{3,11},{4,12},{5,13},{6,14},{7,15},{8,0},{9,1},... | collective-permute-start | bytes 393224 | tf_op jit(solution)/shard_map/ppermute | solution.py:224
  66.3 21.9 %collective-permute-start.11 = (f32[8,2,16,128]{3,2,1,0:T(8,128)S(1)}, f32[8,2,16,128]{3,2,1,0:T(8,128)S(1)}, u32[]{:S(2)}, u32[]{:S(2)}) collective-permute-start(f32[8,2,16,128]{3,2,1,0:T(8,128)S(1)} %get-tuple-element.51), channel_id=1, source_target_pairs={{0,16},{1,17},{2,18},{3,19},{4,20},{5,21},{6,22},{7,23},{8,24},{9,... | collective-permute-start | bytes 393224 | tf_op jit(solution)/shard_map/ppermute | solution.py:224
  68.7 19.5 %collective-permute-start.12 = (f32[8,2,16,128]{3,2,1,0:T(8,128)S(1)}, f32[8,2,16,128]{3,2,1,0:T(8,128)S(1)}, u32[]{:S(2)}, u32[]{:S(2)}) collective-permute-start(f32[8,2,16,128]{3,2,1,0:T(8,128)S(1)} %get-tuple-element.52), channel_id=1, source_target_pairs={{0,24},{1,25},{2,26},{3,27},{4,28},{5,29},{6,30},{7,31},{8,16},{9,... | collective-permute-start | bytes 393224 | tf_op jit(solution)/shard_map/ppermute | solution.py:224
  88.2 5.2 %collective-permute-start.13 = (f32[4,2,16,128]{3,2,1,0:T(8,128)S(1)}, f32[4,2,16,128]{3,2,1,0:T(8,128)S(1)}, u32[]{:S(2)}, u32[]{:S(2)}) collective-permute-start(f32[4,2,16,128]{3,2,1,0:T(8,128)S(1)} %get-tuple-element.54), channel_id=1, source_target_pairs={{0,1},{1,0},{2,3},{3,2},{4,5},{5,4},{6,7},{7,6},{8,9},{9,8},{10,11... | collective-permute-start | bytes 196616 | tf_op jit(solution)/shard_map/ppermute | solution.py:224
  89.8 4.1 %collective-permute-start.14 = (f32[4,2,16,128]{3,2,1,0:T(8,128)S(1)}, f32[4,2,16,128]{3,2,1,0:T(8,128)S(1)}, u32[]{:S(2)}, u32[]{:S(2)}) collective-permute-start(f32[4,2,16,128]{3,2,1,0:T(8,128)S(1)} %get-tuple-element.55), channel_id=1, source_target_pairs={{0,2},{1,3},{2,0},{3,1},{4,6},{5,7},{6,4},{7,5},{8,10},{9,11},{10,... | collective-permute-start | bytes 196616 | tf_op jit(solution)/shard_map/ppermute | solution.py:224
  89.8 6.1 %collective-permute-start.15 = (f32[4,2,16,128]{3,2,1,0:T(8,128)S(1)}, f32[4,2,16,128]{3,2,1,0:T(8,128)S(1)}, u32[]{:S(2)}, u32[]{:S(2)}) collective-permute-start(f32[4,2,16,128]{3,2,1,0:T(8,128)S(1)} %get-tuple-element.56), channel_id=1, source_target_pairs={{0,3},{1,2},{2,1},{3,0},{4,7},{5,6},{6,5},{7,4},{8,11},{9,10},{10,... | collective-permute-start | bytes 196616 | tf_op jit(solution)/shard_map/ppermute | solution.py:224
  90.4 5.5 %collective-permute-start.16 = (f32[4,2,16,128]{3,2,1,0:T(8,128)S(1)}, f32[4,2,16,128]{3,2,1,0:T(8,128)S(1)}, u32[]{:S(2)}, u32[]{:S(2)}) collective-permute-start(f32[4,2,16,128]{3,2,1,0:T(8,128)S(1)} %get-tuple-element.57), channel_id=1, source_target_pairs={{0,4},{1,5},{2,6},{3,7},{4,0},{5,1},{6,2},{7,3},{8,12},{9,13},{10,... | collective-permute-start | bytes 196616 | tf_op jit(solution)/shard_map/ppermute | solution.py:224
  91.9 5.2 %collective-permute-start.17 = (f32[4,2,16,128]{3,2,1,0:T(8,128)S(1)}, f32[4,2,16,128]{3,2,1,0:T(8,128)S(1)}, u32[]{:S(2)}, u32[]{:S(2)}) collective-permute-start(f32[4,2,16,128]{3,2,1,0:T(8,128)S(1)} %get-tuple-element.58), channel_id=1, source_target_pairs={{0,5},{1,4},{2,7},{3,6},{4,1},{5,0},{6,3},{7,2},{8,13},{9,12},{10,... | collective-permute-start | bytes 196616 | tf_op jit(solution)/shard_map/ppermute | solution.py:224
  93.4 4.4 %collective-permute-start.18 = (f32[4,2,16,128]{3,2,1,0:T(8,128)S(1)}, f32[4,2,16,128]{3,2,1,0:T(8,128)S(1)}, u32[]{:S(2)}, u32[]{:S(2)}) collective-permute-start(f32[4,2,16,128]{3,2,1,0:T(8,128)S(1)} %get-tuple-element.59), channel_id=1, source_target_pairs={{0,6},{1,7},{2,4},{3,5},{4,2},{5,3},{6,0},{7,1},{8,14},{9,15},{10,... | collective-permute-start | bytes 196616 | tf_op jit(solution)/shard_map/ppermute | solution.py:224
  93.9 5.5 %collective-permute-start.19 = (f32[4,2,16,128]{3,2,1,0:T(8,128)S(1)}, f32[4,2,16,128]{3,2,1,0:T(8,128)S(1)}, u32[]{:S(2)}, u32[]{:S(2)}) collective-permute-start(f32[4,2,16,128]{3,2,1,0:T(8,128)S(1)} %get-tuple-element.60), channel_id=1, source_target_pairs={{0,7},{1,6},{2,5},{3,4},{4,3},{5,2},{6,1},{7,0},{8,15},{9,14},{10,... | collective-permute-start | bytes 196616 | tf_op jit(solution)/shard_map/ppermute | solution.py:224

commit v5 on v4

--- a/solution.py
+++ b/solution.py
@@ -229,6 +229,11 @@
 SCALAR = pl.BlockSpec(memory_space=pltpu.SMEM)
 WHOLE = pl.BlockSpec(memory_space=pltpu.VMEM)
 FAR = pl.BlockSpec(memory_space=pltpu.HBM)
+
+
+def low_masks(size, core):
+    far = sorted((k for k in range(1, size) if not k & core), key=lambda k: (k.bit_count(), -k))
+    return [*far, *(k | core for k in far), core]
 
 
 def device_order(devices, core):
@@ -310,7 +315,9 @@
         functools.partial(deal_kernel, slabs, size), [SCALAR] + [WHOLE] * slabs,
         [held_shape(slabs, 2, count, lanes)] * size,
     )(place, *map(near, few))
-    few = [few[0]] + [swap(few[k], axes, devices, k) for k in range(1, size)]
+    few = list(few)
+    for k in low_masks(size, core):
+        few[k] = swap(few[k], axes, devices, k)
     few = kernel_call(
         functools.partial(gather_kernel, slabs, size), [SCALAR] + [WHOLE] * (2 + size),
         held_shape(devices, 2, count, lanes), [held_shape(devices, 2, count, lanes)],

time: 102 us -> 102 us (level)
  no operation moved by 1% of the time
where the time goes in v5:
time: 102 us; the launch traced here: 101 us
  waiting for transfers between devices  56.6 us (55%)
  starting transfers between devices  35.8 us (35%)
  Pallas kernels  7.9 us (8%)
    ppermute x20, waiting for transfers between devices, swap(): return lax.ppermute(x, axes, [(i, i ^ mask) for i in range(devices)])  56.6 us
    ppermute x20, starting transfers between devices, swap(): return lax.ppermute(x, axes, [(i, i ^ mask) for i in range(devices)])  24 us
    all_to_all x1, starting transfers between devices, body_fast(): lax.all_to_all(sent, axes, 0, 0, tiled=True, axis_index_groups=[order])  7.33 us
    all_to_all x1, starting transfers between devices, body_fast(): most = lax.all_to_all(most, axes, 0, 0, tiled=True)  4.4 us
    pallas_call x1, Pallas kernels, body_fast(): kernel_call(functools.partial(first_kernel, slots, part, scale), [WHOLE]...  2.3 us
  transfers between devices with their start and end apart: 22, of which 10 were waited for; matrix products, arithmetic and copies ran while one was open for 1% of the time, Pallas kernels for 1%

profile of v5, /device:TPU:0, one launch (start us, length us, event | category | flops | bytes accessed | tf_op | source)
XLA Modules:
  0.0 101.2 jit_solution(13099707248639605690)
XLA Ops:
  0.1 1.5 %shard_map.37 = (f32[2,1024,128]{2,1,0:T(8,128)S(1)}, f32[32,32,128]{2,1,0:T(8,128)S(1)}, f32[2,128]{1,0:T(2,128)S(1)}, f32[8,32,128]{2,1,0:T(8,128)S(1)}, f32[8...) custom-call(s32[1]{0:T(128)} %bitcast.place_ref, f32[2,1024,128]{2,1,0:T(8,128)} %bitcast.8, f32[32,32,128]{2,1,0:T(8,128)} %bitcast.9, ...), custom_call_target="tpu_custom_call" | custom-call | tf_op jit(solution)/shard_map/pallas_call | solution.py:277
  1.6 2.3 %shard_map.38 = f32[32,2,32,128]{3,2,1,0:T(8,128)} custom-call(f32[2,1024,128]{2,1,0:T(8,128)S(1)} %get-tuple-element.33.wave_ref, f32[1024,128]{1,0:T(8,128)S(1)} %bitcast.7, f32[2,128]{1,0:T(2,128)S(1)} %get-tuple-element.35.angle_ref, bf16[256,128]{1,0:T(8,128)(2,1)S(1)} %pad_maximum_fusion.right_ref, bf16[128,256]{1,0:T(8,128)(2,1)S(1)} %pad_maximum_fusion.2.left_ref), custom_call_target="tpu_custom_call" | custom-call | tf_op jit(solution)/shard_map/pallas_call | solution.py:286
  3.9 7.3 %all-to-all-start = ((f32[32,2,32,128]{3,2,1,0:T(8,128)}), f32[32,2,32,128]{3,2,1,0:T(8,128)S(1)}, u32[]{:S(2)}, u32[]{:S(2)}) async-start(f32[32,2,32,128]{3,2,1,0:T(8,128)} %shard_map.38), calls=%async_computation | async-start | bytes 2097152 | tf_op jit(solution)/shard_map/all_to_all | solution.py:290
  11.3 1.8 %collective-permute-start = (f32[8,32,128]{2,1,0:T(8,128)S(1)}, f32[8,32,128]{2,1,0:T(8,128)S(1)}, u32[]{:S(2)}, u32[]{:S(2)}) collective-permute-start(f32[8,32,128]{2,1,0:T(8,128)S(1)} %get-tuple-element.36), channel_id=1, source_target_pairs={{0,8},{1,9},{2,10},{3,11},{4,12},{5,13},{6,14},{7,15},{8,0},{9,1},... | collective-permute-start | bytes 393224 | tf_op jit(solution)/shard_map/ppermute | solution.py:224
  13.1 2.4 %collective-permute-start.1 = (f32[8,32,128]{2,1,0:T(8,128)S(1)}, f32[8,32,128]{2,1,0:T(8,128)S(1)}, u32[]{:S(2)}, u32[]{:S(2)}) collective-permute-start(f32[8,32,128]{2,1,0:T(8,128)S(1)} %get-tuple-element.37), channel_id=1, source_target_pairs={{0,16},{1,17},{2,18},{3,19},{4,20},{5,21},{6,22},{7,23},{8,24},{9,... | collective-permute-start | bytes 393224 | tf_op jit(solution)/shard_map/ppermute | solution.py:224
  15.5 0.2 collective-permute-start.2
  15.8 0.1 tile.13
  15.9 0.5 tile.14
  16.4 15.6 %collective-permute-done.refs_1_ = f32[8,32,128]{2,1,0:T(8,128)S(1)} collective-permute-done((f32[8,32,128]{2,1,0:T(8,128)S(1)}, f32[8,32,128]{2,1,0:T(8,128)S(1)}, u32[]{:S(2)}, u32[]{:S(2)}) %collective-permute-start) | collective-permute-done | bytes 131104 | tf_op jit(solution)/shard_map/ppermute | solution.py:224
  32.0 14.5 %collective-permute-done.1.refs_2_ = f32[8,32,128]{2,1,0:T(8,128)S(1)} collective-permute-done((f32[8,32,128]{2,1,0:T(8,128)S(1)}, f32[8,32,128]{2,1,0:T(8,128)S(1)}, u32[]{:S(2)}, u32[]{:S(2)}) %collective-permute-start.1) | collective-permute-done | bytes 131104 | tf_op jit(solution)/shard_map/ppermute | solution.py:224
  46.5 0.0 collective-permute-done.2.refs_3_
  46.5 1.5 %collective-permute-start.3 = (f32[4,32,128]{2,1,0:T(8,128)S(1)}, f32[4,32,128]{2,1,0:T(8,128)S(1)}, u32[]{:S(2)}, u32[]{:S(2)}) collective-permute-start(f32[4,32,128]{2,1,0:T(8,128)S(1)} %get-tuple-element.40), channel_id=1, source_target_pairs={{0,1},{1,0},{2,3},{3,2},{4,5},{5,4},{6,7},{7,6},{8,9},{9,8},{10,11... | collective-permute-start | bytes 196616 | tf_op jit(solution)/shard_map/ppermute | solution.py:224
  48.0 0.0 collective-permute-start.4
  48.1 0.1 compare_select_fusion
  48.1 0.7 collective-permute-start.5
  48.9 1.5 %collective-permute-start.6 = (f32[4,32,128]{2,1,0:T(8,128)S(1)}, f32[4,32,128]{2,1,0:T(8,128)S(1)}, u32[]{:S(2)}, u32[]{:S(2)}) collective-permute-start(f32[4,32,128]{2,1,0:T(8,128)S(1)} %get-tuple-element.43), channel_id=1, source_target_pairs={{0,4},{1,5},{2,6},{3,7},{4,0},{5,1},{6,2},{7,3},{8,12},{9,13},{10,... | collective-permute-start | bytes 196616 | tf_op jit(solution)/shard_map/ppermute | solution.py:224
  50.4 1.4 %collective-permute-start.7 = (f32[4,32,128]{2,1,0:T(8,128)S(1)}, f32[4,32,128]{2,1,0:T(8,128)S(1)}, u32[]{:S(2)}, u32[]{:S(2)}) collective-permute-start(f32[4,32,128]{2,1,0:T(8,128)S(1)} %get-tuple-element.44), channel_id=1, source_target_pairs={{0,5},{1,4},{2,7},{3,6},{4,1},{5,0},{6,3},{7,2},{8,13},{9,12},{10,... | collective-permute-start | bytes 196616 | tf_op jit(solution)/shard_map/ppermute | solution.py:224
  51.8 0.0 collective-permute-done.3.refs_1_
  51.8 0.5 collective-permute-start.8
  52.3 0.0 collective-permute-done.4.refs_2_
  52.3 1.7 %collective-permute-start.9 = (f32[4,32,128]{2,1,0:T(8,128)S(1)}, f32[4,32,128]{2,1,0:T(8,128)S(1)}, u32[]{:S(2)}, u32[]{:S(2)}) collective-permute-start(f32[4,32,128]{2,1,0:T(8,128)S(1)} %get-tuple-element.46), channel_id=1, source_target_pairs={{0,7},{1,6},{2,5},{3,4},{4,3},{5,2},{6,1},{7,0},{8,15},{9,14},{10,... | collective-permute-start | bytes 196616 | tf_op jit(solution)/shard_map/ppermute | solution.py:224
  54.1 0.0 collective-permute-done.6.refs_4_
  54.1 1.7 %collective-permute-done.7.refs_5_ = f32[4,32,128]{2,1,0:T(8,128)S(1)} collective-permute-done((f32[4,32,128]{2,1,0:T(8,128)S(1)}, f32[4,32,128]{2,1,0:T(8,128)S(1)}, u32[]{:S(2)}, u32[]{:S(2)}) %collective-permute-start.7) | collective-permute-done | bytes 65568 | tf_op jit(solution)/shard_map/ppermute | solution.py:224
  55.8 0.4 collective-permute-done.8.refs_6_
  56.2 1.6 %collective-permute-done.9.refs_7_ = f32[4,32,128]{2,1,0:T(8,128)S(1)} collective-permute-done((f32[4,32,128]{2,1,0:T(8,128)S(1)}, f32[4,32,128]{2,1,0:T(8,128)S(1)}, u32[]{:S(2)}, u32[]{:S(2)}) %collective-permute-start.9) | collective-permute-done | bytes 65568 | tf_op jit(solution)/shard_map/ppermute | solution.py:224
  57.8 0.5 shard_map.40
  58.3 0.0 all-to-all-done.seen_ref
  58.3 1.5 %shard_map.44 = f32[32,2,16,128]{3,2,1,0:T(8,128)} custom-call(f32[32,2,32,128]{3,2,1,0:T(8,128)S(1)} %all-to-all-done.seen_ref, f32[32,32,128]{2,1,0:T(8,128)S(1)} %get-tuple-element.47.cos_ref, f32[32,32,128]{2,1,0:T(8,128)S(1)} %get-tuple-element.48.sin_ref, bf16[256,128]{1,0:T(8,128)(2,1)S(1)} %pad_maximum_fusion.right_ref, ...), custom_call_target="tpu_custom_call" | custom-call | tf_op jit(solution)/shard_map/pallas_call | solution.py:309
  59.8 4.4 %all-to-all-start.1 = ((f32[32,2,16,128]{3,2,1,0:T(8,128)}), f32[32,2,16,128]{3,2,1,0:T(8,128)S(1)}, u32[]{:S(2)}, u32[]{:S(2)}) async-start(f32[32,2,16,128]{3,2,1,0:T(8,128)} %shard_map.44), calls=%async_computation.1 | async-start | bytes 1048576 | tf_op jit(solution)/shard_map/all_to_all | solution.py:313
  64.2 0.3 shard_map.41
  64.5 1.8 %collective-permute-start.10 = (f32[8,2,16,128]{3,2,1,0:T(8,128)S(1)}, f32[8,2,16,128]{3,2,1,0:T(8,128)S(1)}, u32[]{:S(2)}, u32[]{:S(2)}) collective-permute-start(f32[8,2,16,128]{3,2,1,0:T(8,128)S(1)} %get-tuple-element.50), channel_id=1, source_target_pairs={{0,8},{1,9},{2,10},{3,11},{4,12},{5,13},{6,14},{7,15},{8,0},{9,1},... | collective-permute-start | bytes 393224 | tf_op jit(solution)/shard_map/ppermute | solution.py:224
  66.3 2.4 %collective-permute-start.11 = (f32[8,2,16,128]{3,2,1,0:T(8,128)S(1)}, f32[8,2,16,128]{3,2,1,0:T(8,128)S(1)}, u32[]{:S(2)}, u32[]{:S(2)}) collective-permute-start(f32[8,2,16,128]{3,2,1,0:T(8,128)S(1)} %get-tuple-element.51), channel_id=1, source_target_pairs={{0,16},{1,17},{2,18},{3,19},{4,20},{5,21},{6,22},{7,23},{8,24},{9,... | collective-permute-start | bytes 393224 | tf_op jit(solution)/shard_map/ppermute | solution.py:224
  68.7 0.2 collective-permute-start.12
  68.9 8.3 %collective-permute-done.10.refs_1_ = f32[8,2,16,128]{3,2,1,0:T(8,128)S(1)} collective-permute-done((f32[8,2,16,128]{3,2,1,0:T(8,128)S(1)}, f32[8,2,16,128]{3,2,1,0:T(8,128)S(1)}, u32[]{:S(2)}, u32[]{:S(2)}) %collective-permute-start.10) | collective-permute-done | bytes 131104 | tf_op jit(solution)/shard_map/ppermute | solution.py:224
  77.2 11.0 %collective-permute-done.11.refs_2_ = f32[8,2,16,128]{3,2,1,0:T(8,128)S(1)} collective-permute-done((f32[8,2,16,128]{3,2,1,0:T(8,128)S(1)}, f32[8,2,16,128]{3,2,1,0:T(8,128)S(1)}, u32[]{:S(2)}, u32[]{:S(2)}) %collective-permute-start.11) | collective-permute-done | bytes 131104 | tf_op jit(solution)/shard_map/ppermute | solution.py:224
  88.2 0.0 collective-permute-done.12.refs_3_
  88.2 1.5 %collective-permute-start.13 = (f32[4,2,16,128]{3,2,1,0:T(8,128)S(1)}, f32[4,2,16,128]{3,2,1,0:T(8,128)S(1)}, u32[]{:S(2)}, u32[]{:S(2)}) collective-permute-start(f32[4,2,16,128]{3,2,1,0:T(8,128)S(1)} %get-tuple-element.54), channel_id=1, source_target_pairs={{0,1},{1,0},{2,3},{3,2},{4,5},{5,4},{6,7},{7,6},{8,9},{9,8},{10,11... | collective-permute-start | bytes 196616 | tf_op jit(solution)/shard_map/ppermute | solution.py:224
  89.8 0.7 collective-permute-start.15
  90.4 1.5 %collective-permute-start.16 = (f32[4,2,16,128]{3,2,1,0:T(8,128)S(1)}, f32[4,2,16,128]{3,2,1,0:T(8,128)S(1)}, u32[]{:S(2)}, u32[]{:S(2)}) collective-permute-start(f32[4,2,16,128]{3,2,1,0:T(8,128)S(1)} %get-tuple-element.57), channel_id=1, source_target_pairs={{0,4},{1,5},{2,6},{3,7},{4,0},{5,1},{6,2},{7,3},{8,12},{9,13},{10,... | collective-permute-start | bytes 196616 | tf_op jit(solution)/shard_map/ppermute | solution.py:224
  91.9 1.5 %collective-permute-start.17 = (f32[4,2,16,128]{3,2,1,0:T(8,128)S(1)}, f32[4,2,16,128]{3,2,1,0:T(8,128)S(1)}, u32[]{:S(2)}, u32[]{:S(2)}) collective-permute-start(f32[4,2,16,128]{3,2,1,0:T(8,128)S(1)} %get-tuple-element.58), channel_id=1, source_target_pairs={{0,5},{1,4},{2,7},{3,6},{4,1},{5,0},{6,3},{7,2},{8,13},{9,12},{10,... | collective-permute-start | bytes 196616 | tf_op jit(solution)/shard_map/ppermute | solution.py:224
  93.4 0.5 collective-permute-start.18
  93.9 0.0 collective-permute-done.14.refs_2_
  93.9 2.0 %collective-permute-start.19 = (f32[4,2,16,128]{3,2,1,0:T(8,128)S(1)}, f32[4,2,16,128]{3,2,1,0:T(8,128)S(1)}, u32[]{:S(2)}, u32[]{:S(2)}) collective-permute-start(f32[4,2,16,128]{3,2,1,0:T(8,128)S(1)} %get-tuple-element.60), channel_id=1, source_target_pairs={{0,7},{1,6},{2,5},{3,4},{4,3},{5,2},{6,1},{7,0},{8,15},{9,14},{10,... | collective-permute-start | bytes 196616 | tf_op jit(solution)/shard_map/ppermute | solution.py:224
  95.9 1.2 %collective-permute-done.17.refs_5_ = f32[4,2,16,128]{3,2,1,0:T(8,128)S(1)} collective-permute-done((f32[4,2,16,128]{3,2,1,0:T(8,128)S(1)}, f32[4,2,16,128]{3,2,1,0:T(8,128)S(1)}, u32[]{:S(2)}, u32[]{:S(2)}) %collective-permute-start.17) | collective-permute-done | bytes 65568 | tf_op jit(solution)/shard_map/ppermute | solution.py:224
  97.1 0.7 collective-permute-done.18.refs_6_
  97.7 1.7 %collective-permute-done.19.refs_7_ = f32[4,2,16,128]{3,2,1,0:T(8,128)S(1)} collective-permute-done((f32[4,2,16,128]{3,2,1,0:T(8,128)S(1)}, f32[4,2,16,128]{3,2,1,0:T(8,128)S(1)}, u32[]{:S(2)}, u32[]{:S(2)}) %collective-permute-start.19) | collective-permute-done | bytes 65568 | tf_op jit(solution)/shard_map/ppermute | solution.py:224
  99.4 0.6 shard_map.43.few_ref
  100.0 1.2 %shard_map.45 = f32[2,1024,128]{2,1,0:T(8,128)} custom-call(f32[32,2,16,128]{3,2,1,0:T(8,128)S(1)} %shard_map.43.few_ref, f32[32,2,16,128]{3,2,1,0:T(8,128)S(1)} %all-to-all-done.1.most_ref), custom_call_target="tpu_custom_call" | custom-call | tf_op jit(solution)/shard_map/pallas_call | solution.py:325
  (15 shorter events, 0.2 us)
Async XLA Ops:
  3.9 54.4 %all-to-all-start = ((f32[32,2,32,128]{3,2,1,0:T(8,128)}), f32[32,2,32,128]{3,2,1,0:T(8,128)S(1)}, u32[]{:S(2)}, u32[]{:S(2)}) async-start(f32[32,2,32,128]{3,2,1,0:T(8,128)} %shard_map.38), calls=%async_computation | async-start | bytes 2097152 | tf_op jit(solution)/shard_map/all_to_all | solution.py:290
  11.3 20.7 %collective-permute-start = (f32[8,32,128]{2,1,0:T(8,128)S(1)}, f32[8,32,128]{2,1,0:T(8,128)S(1)}, u32[]{:S(2)}, u32[]{:S(2)}) collective-permute-start(f32[8,32,128]{2,1,0:T(8,128)S(1)} %get-tuple-element.36), channel_id=1, source_target_pairs={{0,8},{1,9},{2,10},{3,11},{4,12},{5,13},{6,14},{7,15},{8,0},{9,1},... | collective-permute-start | bytes 393224 | tf_op jit(solution)/shard_map/ppermute | solution.py:224
  13.1 33.4 %collective-permute-start.1 = (f32[8,32,128]{2,1,0:T(8,128)S(1)}, f32[8,32,128]{2,1,0:T(8,128)S(1)}, u32[]{:S(2)}, u32[]{:S(2)}) collective-permute-start(f32[8,32,128]{2,1,0:T(8,128)S(1)} %get-tuple-element.37), channel_id=1, source_target_pairs={{0,16},{1,17},{2,18},{3,19},{4,20},{5,21},{6,22},{7,23},{8,24},{9,... | collective-permute-start | bytes 393224 | tf_op jit(solution)/shard_map/ppermute | solution.py:224
  15.5 31.0 %collective-permute-start.2 = (f32[8,32,128]{2,1,0:T(8,128)S(1)}, f32[8,32,128]{2,1,0:T(8,128)S(1)}, u32[]{:S(2)}, u32[]{:S(2)}) collective-permute-start(f32[8,32,128]{2,1,0:T(8,128)S(1)} %get-tuple-element.38), channel_id=1, source_target_pairs={{0,24},{1,25},{2,26},{3,27},{4,28},{5,29},{6,30},{7,31},{8,16},{9,... | collective-permute-start | bytes 393224 | tf_op jit(solution)/shard_map/ppermute | solution.py:224
  46.5 5.3 %collective-permute-start.3 = (f32[4,32,128]{2,1,0:T(8,128)S(1)}, f32[4,32,128]{2,1,0:T(8,128)S(1)}, u32[]{:S(2)}, u32[]{:S(2)}) collective-permute-start(f32[4,32,128]{2,1,0:T(8,128)S(1)} %get-tuple-element.40), channel_id=1, source_target_pairs={{0,1},{1,0},{2,3},{3,2},{4,5},{5,4},{6,7},{7,6},{8,9},{9,8},{10,11... | collective-permute-start | bytes 196616 | tf_op jit(solution)/shard_map/ppermute | solution.py:224
  48.0 4.3 %collective-permute-start.4 = (f32[4,32,128]{2,1,0:T(8,128)S(1)}, f32[4,32,128]{2,1,0:T(8,128)S(1)}, u32[]{:S(2)}, u32[]{:S(2)}) collective-permute-start(f32[4,32,128]{2,1,0:T(8,128)S(1)} %get-tuple-element.41), channel_id=1, source_target_pairs={{0,2},{1,3},{2,0},{3,1},{4,6},{5,7},{6,4},{7,5},{8,10},{9,11},{10,... | collective-permute-start | bytes 196616 | tf_op jit(solution)/shard_map/ppermute | solution.py:224
  48.1 5.9 %collective-permute-start.5 = (f32[4,32,128]{2,1,0:T(8,128)S(1)}, f32[4,32,128]{2,1,0:T(8,128)S(1)}, u32[]{:S(2)}, u32[]{:S(2)}) collective-permute-start(f32[4,32,128]{2,1,0:T(8,128)S(1)} %get-tuple-element.42), channel_id=1, source_target_pairs={{0,3},{1,2},{2,1},{3,0},{4,7},{5,6},{6,5},{7,4},{8,11},{9,10},{10,... | collective-permute-start | bytes 196616 | tf_op jit(solution)/shard_map/ppermute | solution.py:224
  48.9 5.2 %collective-permute-start.6 = (f32[4,32,128]{2,1,0:T(8,128)S(1)}, f32[4,32,128]{2,1,0:T(8,128)S(1)}, u32[]{:S(2)}, u32[]{:S(2)}) collective-permute-start(f32[4,32,128]{2,1,0:T(8,128)S(1)} %get-tuple-element.43), channel_id=1, source_target_pairs={{0,4},{1,5},{2,6},{3,7},{4,0},{5,1},{6,2},{7,3},{8,12},{9,13},{10,... | collective-permute-start | bytes 196616 | tf_op jit(solution)/shard_map/ppermute | solution.py:224
  50.4 5.4 %collective-permute-start.7 = (f32[4,32,128]{2,1,0:T(8,128)S(1)}, f32[4,32,128]{2,1,0:T(8,128)S(1)}, u32[]{:S(2)}, u32[]{:S(2)}) collective-permute-start(f32[4,32,128]{2,1,0:T(8,128)S(1)} %get-tuple-element.44), channel_id=1, source_target_pairs={{0,5},{1,4},{2,7},{3,6},{4,1},{5,0},{6,3},{7,2},{8,13},{9,12},{10,... | collective-permute-start | bytes 196616 | tf_op jit(solution)/shard_map/ppermute | solution.py:224
  51.8 4.4 %collective-permute-start.8 = (f32[4,32,128]{2,1,0:T(8,128)S(1)}, f32[4,32,128]{2,1,0:T(8,128)S(1)}, u32[]{:S(2)}, u32[]{:S(2)}) collective-permute-start(f32[4,32,128]{2,1,0:T(8,128)S(1)} %get-tuple-element.45), channel_id=1, source_target_pairs={{0,6},{1,7},{2,4},{3,5},{4,2},{5,3},{6,0},{7,1},{8,14},{9,15},{10,... | collective-permute-start | bytes 196616 | tf_op jit(solution)/shard_map/ppermute | solution.py:224
  52.3 5.5 %collective-permute-start.9 = (f32[4,32,128]{2,1,0:T(8,128)S(1)}, f32[4,32,128]{2,1,0:T(8,128)S(1)}, u32[]{:S(2)}, u32[]{:S(2)}) collective-permute-start(f32[4,32,128]{2,1,0:T(8,128)S(1)} %get-tuple-element.46), channel_id=1, source_target_pairs={{0,7},{1,6},{2,5},{3,4},{4,3},{5,2},{6,1},{7,0},{8,15},{9,14},{10,... | collective-permute-start | bytes 196616 | tf_op jit(solution)/shard_map/ppermute | solution.py:224
  59.8 40.2 %all-to-all-start.1 = ((f32[32,2,16,128]{3,2,1,0:T(8,128)}), f32[32,2,16,128]{3,2,1,0:T(8,128)S(1)}, u32[]{:S(2)}, u32[]{:S(2)}) async-start(f32[32,2,16,128]{3,2,1,0:T(8,128)} %shard_map.44), calls=%async_computation.1 | async-start | bytes 1048576 | tf_op jit(solution)/shard_map/all_to_all | solution.py:313
  64.5 12.7 %collective-permute-start.10 = (f32[8,2,16,128]{3,2,1,0:T(8,128)S(1)}, f32[8,2,16,128]{3,2,1,0:T(8,128)S(1)}, u32[]{:S(2)}, u32[]{:S(2)}) collective-permute-start(f32[8,2,16,128]{3,2,1,0:T(8,128)S(1)} %get-tuple-element.50), channel_id=1, source_target_pairs={{0,8},{1,9},{2,10},{3,11},{4,12},{5,13},{6,14},{7,15},{8,0},{9,1},... | collective-permute-start | bytes 393224 | tf_op jit(solution)/shard_map/ppermute | solution.py:224
  66.3 21.9 %collective-permute-start.11 = (f32[8,2,16,128]{3,2,1,0:T(8,128)S(1)}, f32[8,2,16,128]{3,2,1,0:T(8,128)S(1)}, u32[]{:S(2)}, u32[]{:S(2)}) collective-permute-start(f32[8,2,16,128]{3,2,1,0:T(8,128)S(1)} %get-tuple-element.51), channel_id=1, source_target_pairs={{0,16},{1,17},{2,18},{3,19},{4,20},{5,21},{6,22},{7,23},{8,24},{9,... | collective-permute-start | bytes 393224 | tf_op jit(solution)/shard_map/ppermute | solution.py:224
  68.7 19.5 %collective-permute-start.12 = (f32[8,2,16,128]{3,2,1,0:T(8,128)S(1)}, f32[8,2,16,128]{3,2,1,0:T(8,128)S(1)}, u32[]{:S(2)}, u32[]{:S(2)}) collective-permute-start(f32[8,2,16,128]{3,2,1,0:T(8,128)S(1)} %get-tuple-element.52), channel_id=1, source_target_pairs={{0,24},{1,25},{2,26},{3,27},{4,28},{5,29},{6,30},{7,31},{8,16},{9,... | collective-permute-start | bytes 393224 | tf_op jit(solution)/shard_map/ppermute | solution.py:224
  88.2 5.2 %collective-permute-start.13 = (f32[4,2,16,128]{3,2,1,0:T(8,128)S(1)}, f32[4,2,16,128]{3,2,1,0:T(8,128)S(1)}, u32[]{:S(2)}, u32[]{:S(2)}) collective-permute-start(f32[4,2,16,128]{3,2,1,0:T(8,128)S(1)} %get-tuple-element.54), channel_id=1, source_target_pairs={{0,1},{1,0},{2,3},{3,2},{4,5},{5,4},{6,7},{7,6},{8,9},{9,8},{10,11... | collective-permute-start | bytes 196616 | tf_op jit(solution)/shard_map/ppermute | solution.py:224
  89.8 4.1 %collective-permute-start.14 = (f32[4,2,16,128]{3,2,1,0:T(8,128)S(1)}, f32[4,2,16,128]{3,2,1,0:T(8,128)S(1)}, u32[]{:S(2)}, u32[]{:S(2)}) collective-permute-start(f32[4,2,16,128]{3,2,1,0:T(8,128)S(1)} %get-tuple-element.55), channel_id=1, source_target_pairs={{0,2},{1,3},{2,0},{3,1},{4,6},{5,7},{6,4},{7,5},{8,10},{9,11},{10,... | collective-permute-start | bytes 196616 | tf_op jit(solution)/shard_map/ppermute | solution.py:224
  89.8 6.1 %collective-permute-start.15 = (f32[4,2,16,128]{3,2,1,0:T(8,128)S(1)}, f32[4,2,16,128]{3,2,1,0:T(8,128)S(1)}, u32[]{:S(2)}, u32[]{:S(2)}) collective-permute-start(f32[4,2,16,128]{3,2,1,0:T(8,128)S(1)} %get-tuple-element.56), channel_id=1, source_target_pairs={{0,3},{1,2},{2,1},{3,0},{4,7},{5,6},{6,5},{7,4},{8,11},{9,10},{10,... | collective-permute-start | bytes 196616 | tf_op jit(solution)/shard_map/ppermute | solution.py:224
  90.4 5.5 %collective-permute-start.16 = (f32[4,2,16,128]{3,2,1,0:T(8,128)S(1)}, f32[4,2,16,128]{3,2,1,0:T(8,128)S(1)}, u32[]{:S(2)}, u32[]{:S(2)}) collective-permute-start(f32[4,2,16,128]{3,2,1,0:T(8,128)S(1)} %get-tuple-element.57), channel_id=1, source_target_pairs={{0,4},{1,5},{2,6},{3,7},{4,0},{5,1},{6,2},{7,3},{8,12},{9,13},{10,... | collective-permute-start | bytes 196616 | tf_op jit(solution)/shard_map/ppermute | solution.py:224
  91.9 5.2 %collective-permute-start.17 = (f32[4,2,16,128]{3,2,1,0:T(8,128)S(1)}, f32[4,2,16,128]{3,2,1,0:T(8,128)S(1)}, u32[]{:S(2)}, u32[]{:S(2)}) collective-permute-start(f32[4,2,16,128]{3,2,1,0:T(8,128)S(1)} %get-tuple-element.58), channel_id=1, source_target_pairs={{0,5},{1,4},{2,7},{3,6},{4,1},{5,0},{6,3},{7,2},{8,13},{9,12},{10,... | collective-permute-start | bytes 196616 | tf_op jit(solution)/shard_map/ppermute | solution.py:224
  93.4 4.4 %collective-permute-start.18 = (f32[4,2,16,128]{3,2,1,0:T(8,128)S(1)}, f32[4,2,16,128]{3,2,1,0:T(8,128)S(1)}, u32[]{:S(2)}, u32[]{:S(2)}) collective-permute-start(f32[4,2,16,128]{3,2,1,0:T(8,128)S(1)} %get-tuple-element.59), channel_id=1, source_target_pairs={{0,6},{1,7},{2,4},{3,5},{4,2},{5,3},{6,0},{7,1},{8,14},{9,15},{10,... | collective-permute-start | bytes 196616 | tf_op jit(solution)/shard_map/ppermute | solution.py:224
  93.9 5.5 %collective-permute-start.19 = (f32[4,2,16,128]{3,2,1,0:T(8,128)S(1)}, f32[4,2,16,128]{3,2,1,0:T(8,128)S(1)}, u32[]{:S(2)}, u32[]{:S(2)}) collective-permute-start(f32[4,2,16,128]{3,2,1,0:T(8,128)S(1)} %get-tuple-element.60), channel_id=1, source_target_pairs={{0,7},{1,6},{2,5},{3,4},{4,3},{5,2},{6,1},{7,0},{8,15},{9,14},{10,... | collective-permute-start | bytes 196616 | tf_op jit(solution)/shard_map/ppermute | solution.py:224

commit v6 on v5

--- a/solution.py
+++ b/solution.py
@@ -177,7 +177,7 @@
 
 def last_kernel(devices, part, few_ref, most_ref, out_ref, held, done, sems):
     tiles = part // 8
-    low = 4
+    low = 8
     high = devices // low
 
     start = few_ref.shape[2] // 8
@@ -238,7 +238,7 @@
 
 def device_order(devices, core):
     low, high = core.bit_length() - 1, devices.bit_length() - 1
-    bits = [high - 1, *range(low - 1, -1, -1), low + 1, *range(high - 2, low + 1, -1), low]
+    bits = [high - 1, low + 1, *range(low - 1, -1, -1), *range(high - 2, low + 1, -1), low]
     order = [sum((rank >> (high - 1 - i) & 1) << bit for i, bit in enumerate(bits)) for rank in range(devices)]
     return order, [order.index(d) for d in range(devices)]
 
@@ -324,7 +324,7 @@
     )(place, right, left_small, *map(near, few))
     out = kernel_call(
         functools.partial(last_kernel, devices, part), [WHOLE] * 2, flat(2, total, lanes),
-        [held_shape(2, devices // 4, part // 2, 8, lanes), held_shape(2, total, lanes), pltpu.SemaphoreType.DMA((devices // 2,))],
+        [held_shape(2, devices // 8, part * 8 // 8, 8, lanes), held_shape(2, total, lanes), pltpu.SemaphoreType.DMA((2 * devices // 8,))],
         FAR,
     )(near(few), near(most))
     return out.reshape(2, blocks, rows, lanes)

time: 102 us -> 102 us (level)
  no operation moved by 1% of the time
where the time goes in v6:
time: 102 us; the launch traced here: 101 us
  waiting for transfers between devices  56.4 us (55%)
  starting transfers between devices  35.9 us (35%)
  Pallas kernels  7.82 us (8%)
    ppermute x20, waiting for transfers between devices, swap(): return lax.ppermute(x, axes, [(i, i ^ mask) for i in range(devices)])  56.4 us
    ppermute x20, starting transfers between devices, swap(): return lax.ppermute(x, axes, [(i, i ^ mask) for i in range(devices)])  24.1 us
    all_to_all x1, starting transfers between devices, body_fast(): lax.all_to_all(sent, axes, 0, 0, tiled=True, axis_index_groups=[order])  7.33 us
    all_to_all x1, starting transfers between devices, body_fast(): most = lax.all_to_all(most, axes, 0, 0, tiled=True)  4.49 us
    pallas_call x1, Pallas kernels, body_fast(): kernel_call(functools.partial(first_kernel, slots, part, scale), [WHOLE]...  2.3 us
  transfers between devices with their start and end apart: 22, of which 10 were waited for; matrix products, arithmetic and copies ran while one was open for 1% of the time, Pallas kernels for 1%

profile of v6, /device:TPU:0, one launch (start us, length us, event | category | flops | bytes accessed | tf_op | source)
XLA Modules:
  0.0 101.2 jit_solution(3041273724496136564)
XLA Ops:
  0.1 1.5 %shard_map.37 = (f32[2,1024,128]{2,1,0:T(8,128)S(1)}, f32[32,32,128]{2,1,0:T(8,128)S(1)}, f32[2,128]{1,0:T(2,128)S(1)}, f32[8,32,128]{2,1,0:T(8,128)S(1)}, f32[8...) custom-call(s32[1]{0:T(128)} %bitcast.place_ref, f32[2,1024,128]{2,1,0:T(8,128)} %bitcast.8, f32[32,32,128]{2,1,0:T(8,128)} %bitcast.9, ...), custom_call_target="tpu_custom_call" | custom-call | tf_op jit(solution)/shard_map/pallas_call | solution.py:277
  1.6 2.3 %shard_map.38 = f32[32,2,32,128]{3,2,1,0:T(8,128)} custom-call(f32[2,1024,128]{2,1,0:T(8,128)S(1)} %get-tuple-element.33.wave_ref, f32[1024,128]{1,0:T(8,128)S(1)} %bitcast.7, f32[2,128]{1,0:T(2,128)S(1)} %get-tuple-element.35.angle_ref, bf16[256,128]{1,0:T(8,128)(2,1)S(1)} %pad_maximum_fusion.right_ref, bf16[128,256]{1,0:T(8,128)(2,1)S(1)} %pad_maximum_fusion.2.left_ref), custom_call_target="tpu_custom_call" | custom-call | tf_op jit(solution)/shard_map/pallas_call | solution.py:286
  3.9 7.3 %all-to-all-start = ((f32[32,2,32,128]{3,2,1,0:T(8,128)}), f32[32,2,32,128]{3,2,1,0:T(8,128)S(1)}, u32[]{:S(2)}, u32[]{:S(2)}) async-start(f32[32,2,32,128]{3,2,1,0:T(8,128)} %shard_map.38), calls=%async_computation | async-start | bytes 2097152 | tf_op jit(solution)/shard_map/all_to_all | solution.py:290
  11.3 1.8 %collective-permute-start = (f32[8,32,128]{2,1,0:T(8,128)S(1)}, f32[8,32,128]{2,1,0:T(8,128)S(1)}, u32[]{:S(2)}, u32[]{:S(2)}) collective-permute-start(f32[8,32,128]{2,1,0:T(8,128)S(1)} %get-tuple-element.36), channel_id=1, source_target_pairs={{0,8},{1,9},{2,10},{3,11},{4,12},{5,13},{6,14},{7,15},{8,0},{9,1},... | collective-permute-start | bytes 393224 | tf_op jit(solution)/shard_map/ppermute | solution.py:224
  13.1 2.4 %collective-permute-start.1 = (f32[8,32,128]{2,1,0:T(8,128)S(1)}, f32[8,32,128]{2,1,0:T(8,128)S(1)}, u32[]{:S(2)}, u32[]{:S(2)}) collective-permute-start(f32[8,32,128]{2,1,0:T(8,128)S(1)} %get-tuple-element.37), channel_id=1, source_target_pairs={{0,16},{1,17},{2,18},{3,19},{4,20},{5,21},{6,22},{7,23},{8,24},{9,... | collective-permute-start | bytes 393224 | tf_op jit(solution)/shard_map/ppermute | solution.py:224
  15.5 0.2 collective-permute-start.2
  15.8 0.1 tile.13
  15.9 0.5 tile.14
  16.4 15.6 %collective-permute-done.refs_1_ = f32[8,32,128]{2,1,0:T(8,128)S(1)} collective-permute-done((f32[8,32,128]{2,1,0:T(8,128)S(1)}, f32[8,32,128]{2,1,0:T(8,128)S(1)}, u32[]{:S(2)}, u32[]{:S(2)}) %collective-permute-start) | collective-permute-done | bytes 131104 | tf_op jit(solution)/shard_map/ppermute | solution.py:224
  32.0 14.5 %collective-permute-done.1.refs_2_ = f32[8,32,128]{2,1,0:T(8,128)S(1)} collective-permute-done((f32[8,32,128]{2,1,0:T(8,128)S(1)}, f32[8,32,128]{2,1,0:T(8,128)S(1)}, u32[]{:S(2)}, u32[]{:S(2)}) %collective-permute-start.1) | collective-permute-done | bytes 131104 | tf_op jit(solution)/shard_map/ppermute | solution.py:224
  46.5 1.6 %collective-permute-start.3 = (f32[4,32,128]{2,1,0:T(8,128)S(1)}, f32[4,32,128]{2,1,0:T(8,128)S(1)}, u32[]{:S(2)}, u32[]{:S(2)}) collective-permute-start(f32[4,32,128]{2,1,0:T(8,128)S(1)} %get-tuple-element.40), channel_id=1, source_target_pairs={{0,1},{1,0},{2,3},{3,2},{4,5},{5,4},{6,7},{7,6},{8,9},{9,8},{10,11... | collective-permute-start | bytes 196616 | tf_op jit(solution)/shard_map/ppermute | solution.py:224
  48.1 0.1 compare_select_fusion
  48.2 0.7 collective-permute-start.5
  48.9 1.5 %collective-permute-start.6 = (f32[4,32,128]{2,1,0:T(8,128)S(1)}, f32[4,32,128]{2,1,0:T(8,128)S(1)}, u32[]{:S(2)}, u32[]{:S(2)}) collective-permute-start(f32[4,32,128]{2,1,0:T(8,128)S(1)} %get-tuple-element.43), channel_id=1, source_target_pairs={{0,4},{1,5},{2,6},{3,7},{4,0},{5,1},{6,2},{7,3},{8,12},{9,13},{10,... | collective-permute-start | bytes 196616 | tf_op jit(solution)/shard_map/ppermute | solution.py:224
  50.3 1.5 %collective-permute-start.7 = (f32[4,32,128]{2,1,0:T(8,128)S(1)}, f32[4,32,128]{2,1,0:T(8,128)S(1)}, u32[]{:S(2)}, u32[]{:S(2)}) collective-permute-start(f32[4,32,128]{2,1,0:T(8,128)S(1)} %get-tuple-element.44), channel_id=1, source_target_pairs={{0,5},{1,4},{2,7},{3,6},{4,1},{5,0},{6,3},{7,2},{8,13},{9,12},{10,... | collective-permute-start | bytes 196616 | tf_op jit(solution)/shard_map/ppermute | solution.py:224
  51.9 0.5 collective-permute-start.8
  52.3 1.8 %collective-permute-start.9 = (f32[4,32,128]{2,1,0:T(8,128)S(1)}, f32[4,32,128]{2,1,0:T(8,128)S(1)}, u32[]{:S(2)}, u32[]{:S(2)}) collective-permute-start(f32[4,32,128]{2,1,0:T(8,128)S(1)} %get-tuple-element.46), channel_id=1, source_target_pairs={{0,7},{1,6},{2,5},{3,4},{4,3},{5,2},{6,1},{7,0},{8,15},{9,14},{10,... | collective-permute-start | bytes 196616 | tf_op jit(solution)/shard_map/ppermute | solution.py:224
  54.2 0.0 collective-permute-done.5.refs_3_
  54.2 0.0 collective-permute-done.6.refs_4_
  54.2 1.4 %collective-permute-done.7.refs_5_ = f32[4,32,128]{2,1,0:T(8,128)S(1)} collective-permute-done((f32[4,32,128]{2,1,0:T(8,128)S(1)}, f32[4,32,128]{2,1,0:T(8,128)S(1)}, u32[]{:S(2)}, u32[]{:S(2)}) %collective-permute-start.7) | collective-permute-done | bytes 65568 | tf_op jit(solution)/shard_map/ppermute | solution.py:224
  55.6 0.7 collective-permute-done.8.refs_6_
  56.3 1.5 %collective-permute-done.9.refs_7_ = f32[4,32,128]{2,1,0:T(8,128)S(1)} collective-permute-done((f32[4,32,128]{2,1,0:T(8,128)S(1)}, f32[4,32,128]{2,1,0:T(8,128)S(1)}, u32[]{:S(2)}, u32[]{:S(2)}) %collective-permute-start.9) | collective-permute-done | bytes 65568 | tf_op jit(solution)/shard_map/ppermute | solution.py:224
  57.7 0.5 shard_map.40
  58.2 0.0 all-to-all-done.seen_ref
  58.3 1.5 %shard_map.44 = f32[32,2,16,128]{3,2,1,0:T(8,128)} custom-call(f32[32,2,32,128]{3,2,1,0:T(8,128)S(1)} %all-to-all-done.seen_ref, f32[32,32,128]{2,1,0:T(8,128)S(1)} %get-tuple-element.47.cos_ref, f32[32,32,128]{2,1,0:T(8,128)S(1)} %get-tuple-element.48.sin_ref, bf16[256,128]{1,0:T(8,128)(2,1)S(1)} %pad_maximum_fusion.right_ref, ...), custom_call_target="tpu_custom_call" | custom-call | tf_op jit(solution)/shard_map/pallas_call | solution.py:309
  59.7 4.5 %all-to-all-start.1 = ((f32[32,2,16,128]{3,2,1,0:T(8,128)}), f32[32,2,16,128]{3,2,1,0:T(8,128)S(1)}, u32[]{:S(2)}, u32[]{:S(2)}) async-start(f32[32,2,16,128]{3,2,1,0:T(8,128)} %shard_map.44), calls=%async_computation.1 | async-start | bytes 1048576 | tf_op jit(solution)/shard_map/all_to_all | solution.py:313
  64.2 0.3 shard_map.41
  64.5 1.8 %collective-permute-start.10 = (f32[8,2,16,128]{3,2,1,0:T(8,128)S(1)}, f32[8,2,16,128]{3,2,1,0:T(8,128)S(1)}, u32[]{:S(2)}, u32[]{:S(2)}) collective-permute-start(f32[8,2,16,128]{3,2,1,0:T(8,128)S(1)} %get-tuple-element.50), channel_id=1, source_target_pairs={{0,8},{1,9},{2,10},{3,11},{4,12},{5,13},{6,14},{7,15},{8,0},{9,1},... | collective-permute-start | bytes 393224 | tf_op jit(solution)/shard_map/ppermute | solution.py:224
  66.3 2.4 %collective-permute-start.11 = (f32[8,2,16,128]{3,2,1,0:T(8,128)S(1)}, f32[8,2,16,128]{3,2,1,0:T(8,128)S(1)}, u32[]{:S(2)}, u32[]{:S(2)}) collective-permute-start(f32[8,2,16,128]{3,2,1,0:T(8,128)S(1)} %get-tuple-element.51), channel_id=1, source_target_pairs={{0,16},{1,17},{2,18},{3,19},{4,20},{5,21},{6,22},{7,23},{8,24},{9,... | collective-permute-start | bytes 393224 | tf_op jit(solution)/shard_map/ppermute | solution.py:224
  68.7 0.2 collective-permute-start.12
  68.9 8.3 %collective-permute-done.10.refs_1_ = f32[8,2,16,128]{3,2,1,0:T(8,128)S(1)} collective-permute-done((f32[8,2,16,128]{3,2,1,0:T(8,128)S(1)}, f32[8,2,16,128]{3,2,1,0:T(8,128)S(1)}, u32[]{:S(2)}, u32[]{:S(2)}) %collective-permute-start.10) | collective-permute-done | bytes 131104 | tf_op jit(solution)/shard_map/ppermute | solution.py:224
  77.2 11.0 %collective-permute-done.11.refs_2_ = f32[8,2,16,128]{3,2,1,0:T(8,128)S(1)} collective-permute-done((f32[8,2,16,128]{3,2,1,0:T(8,128)S(1)}, f32[8,2,16,128]{3,2,1,0:T(8,128)S(1)}, u32[]{:S(2)}, u32[]{:S(2)}) %collective-permute-start.11) | collective-permute-done | bytes 131104 | tf_op jit(solution)/shard_map/ppermute | solution.py:224
  88.2 0.0 collective-permute-done.12.refs_3_
  88.2 1.5 %collective-permute-start.13 = (f32[4,2,16,128]{3,2,1,0:T(8,128)S(1)}, f32[4,2,16,128]{3,2,1,0:T(8,128)S(1)}, u32[]{:S(2)}, u32[]{:S(2)}) collective-permute-start(f32[4,2,16,128]{3,2,1,0:T(8,128)S(1)} %get-tuple-element.54), channel_id=1, source_target_pairs={{0,1},{1,0},{2,3},{3,2},{4,5},{5,4},{6,7},{7,6},{8,9},{9,8},{10,11... | collective-permute-start | bytes 196616 | tf_op jit(solution)/shard_map/ppermute | solution.py:224
  89.8 0.0 collective-permute-start.14
  89.8 0.7 collective-permute-start.15
  90.4 1.5 %collective-permute-start.16 = (f32[4,2,16,128]{3,2,1,0:T(8,128)S(1)}, f32[4,2,16,128]{3,2,1,0:T(8,128)S(1)}, u32[]{:S(2)}, u32[]{:S(2)}) collective-permute-start(f32[4,2,16,128]{3,2,1,0:T(8,128)S(1)} %get-tuple-element.57), channel_id=1, source_target_pairs={{0,4},{1,5},{2,6},{3,7},{4,0},{5,1},{6,2},{7,3},{8,12},{9,13},{10,... | collective-permute-start | bytes 196616 | tf_op jit(solution)/shard_map/ppermute | solution.py:224
  91.9 1.5 %collective-permute-start.17 = (f32[4,2,16,128]{3,2,1,0:T(8,128)S(1)}, f32[4,2,16,128]{3,2,1,0:T(8,128)S(1)}, u32[]{:S(2)}, u32[]{:S(2)}) collective-permute-start(f32[4,2,16,128]{3,2,1,0:T(8,128)S(1)} %get-tuple-element.58), channel_id=1, source_target_pairs={{0,5},{1,4},{2,7},{3,6},{4,1},{5,0},{6,3},{7,2},{8,13},{9,12},{10,... | collective-permute-start | bytes 196616 | tf_op jit(solution)/shard_map/ppermute | solution.py:224
  93.4 0.0 collective-permute-done.13.refs_1_
  93.4 0.5 collective-permute-start.18
  93.9 2.0 %collective-permute-start.19 = (f32[4,2,16,128]{3,2,1,0:T(8,128)S(1)}, f32[4,2,16,128]{3,2,1,0:T(8,128)S(1)}, u32[]{:S(2)}, u32[]{:S(2)}) collective-permute-start(f32[4,2,16,128]{3,2,1,0:T(8,128)S(1)} %get-tuple-element.60), channel_id=1, source_target_pairs={{0,7},{1,6},{2,5},{3,4},{4,3},{5,2},{6,1},{7,0},{8,15},{9,14},{10,... | collective-permute-start | bytes 196616 | tf_op jit(solution)/shard_map/ppermute | solution.py:224
  95.9 0.0 collective-permute-done.15.refs_3_
  95.9 0.0 collective-permute-done.16.refs_4_
  95.9 1.2 %collective-permute-done.17.refs_5_ = f32[4,2,16,128]{3,2,1,0:T(8,128)S(1)} collective-permute-done((f32[4,2,16,128]{3,2,1,0:T(8,128)S(1)}, f32[4,2,16,128]{3,2,1,0:T(8,128)S(1)}, u32[]{:S(2)}, u32[]{:S(2)}) %collective-permute-start.17) | collective-permute-done | bytes 65568 | tf_op jit(solution)/shard_map/ppermute | solution.py:224
  97.1 0.7 collective-permute-done.18.refs_6_
  97.7 1.7 %collective-permute-done.19.refs_7_ = f32[4,2,16,128]{3,2,1,0:T(8,128)S(1)} collective-permute-done((f32[4,2,16,128]{3,2,1,0:T(8,128)S(1)}, f32[4,2,16,128]{3,2,1,0:T(8,128)S(1)}, u32[]{:S(2)}, u32[]{:S(2)}) %collective-permute-start.19) | collective-permute-done | bytes 65568 | tf_op jit(solution)/shard_map/ppermute | solution.py:224
  99.4 0.6 shard_map.43.few_ref
  100.0 1.1 %shard_map.45 = f32[2,1024,128]{2,1,0:T(8,128)} custom-call(f32[32,2,16,128]{3,2,1,0:T(8,128)S(1)} %shard_map.43.few_ref, f32[32,2,16,128]{3,2,1,0:T(8,128)S(1)} %all-to-all-done.1.most_ref), custom_call_target="tpu_custom_call" | custom-call | tf_op jit(solution)/shard_map/pallas_call | solution.py:325
  (15 shorter events, 0.2 us)
Async XLA Ops:
  3.9 54.3 %all-to-all-start = ((f32[32,2,32,128]{3,2,1,0:T(8,128)}), f32[32,2,32,128]{3,2,1,0:T(8,128)S(1)}, u32[]{:S(2)}, u32[]{:S(2)}) async-start(f32[32,2,32,128]{3,2,1,0:T(8,128)} %shard_map.38), calls=%async_computation | async-start | bytes 2097152 | tf_op jit(solution)/shard_map/all_to_all | solution.py:290
  11.3 20.7 %collective-permute-start = (f32[8,32,128]{2,1,0:T(8,128)S(1)}, f32[8,32,128]{2,1,0:T(8,128)S(1)}, u32[]{:S(2)}, u32[]{:S(2)}) collective-permute-start(f32[8,32,128]{2,1,0:T(8,128)S(1)} %get-tuple-element.36), channel_id=1, source_target_pairs={{0,8},{1,9},{2,10},{3,11},{4,12},{5,13},{6,14},{7,15},{8,0},{9,1},... | collective-permute-start | bytes 393224 | tf_op jit(solution)/shard_map/ppermute | solution.py:224
  13.1 33.4 %collective-permute-start.1 = (f32[8,32,128]{2,1,0:T(8,128)S(1)}, f32[8,32,128]{2,1,0:T(8,128)S(1)}, u32[]{:S(2)}, u32[]{:S(2)}) collective-permute-start(f32[8,32,128]{2,1,0:T(8,128)S(1)} %get-tuple-element.37), channel_id=1, source_target_pairs={{0,16},{1,17},{2,18},{3,19},{4,20},{5,21},{6,22},{7,23},{8,24},{9,... | collective-permute-start | bytes 393224 | tf_op jit(solution)/shard_map/ppermute | solution.py:224
  15.5 31.0 %collective-permute-start.2 = (f32[8,32,128]{2,1,0:T(8,128)S(1)}, f32[8,32,128]{2,1,0:T(8,128)S(1)}, u32[]{:S(2)}, u32[]{:S(2)}) collective-permute-start(f32[8,32,128]{2,1,0:T(8,128)S(1)} %get-tuple-element.38), channel_id=1, source_target_pairs={{0,24},{1,25},{2,26},{3,27},{4,28},{5,29},{6,30},{7,31},{8,16},{9,... | collective-permute-start | bytes 393224 | tf_op jit(solution)/shard_map/ppermute | solution.py:224
  46.5 5.4 %collective-permute-start.3 = (f32[4,32,128]{2,1,0:T(8,128)S(1)}, f32[4,32,128]{2,1,0:T(8,128)S(1)}, u32[]{:S(2)}, u32[]{:S(2)}) collective-permute-start(f32[4,32,128]{2,1,0:T(8,128)S(1)} %get-tuple-element.40), channel_id=1, source_target_pairs={{0,1},{1,0},{2,3},{3,2},{4,5},{5,4},{6,7},{7,6},{8,9},{9,8},{10,11... | collective-permute-start | bytes 196616 | tf_op jit(solution)/shard_map/ppermute | solution.py:224
  48.1 4.2 %collective-permute-start.4 = (f32[4,32,128]{2,1,0:T(8,128)S(1)}, f32[4,32,128]{2,1,0:T(8,128)S(1)}, u32[]{:S(2)}, u32[]{:S(2)}) collective-permute-start(f32[4,32,128]{2,1,0:T(8,128)S(1)} %get-tuple-element.41), channel_id=1, source_target_pairs={{0,2},{1,3},{2,0},{3,1},{4,6},{5,7},{6,4},{7,5},{8,10},{9,11},{10,... | collective-permute-start | bytes 196616 | tf_op jit(solution)/shard_map/ppermute | solution.py:224
  48.2 6.0 %collective-permute-start.5 = (f32[4,32,128]{2,1,0:T(8,128)S(1)}, f32[4,32,128]{2,1,0:T(8,128)S(1)}, u32[]{:S(2)}, u32[]{:S(2)}) collective-permute-start(f32[4,32,128]{2,1,0:T(8,128)S(1)} %get-tuple-element.42), channel_id=1, source_target_pairs={{0,3},{1,2},{2,1},{3,0},{4,7},{5,6},{6,5},{7,4},{8,11},{9,10},{10,... | collective-permute-start | bytes 196616 | tf_op jit(solution)/shard_map/ppermute | solution.py:224
  48.9 5.3 %collective-permute-start.6 = (f32[4,32,128]{2,1,0:T(8,128)S(1)}, f32[4,32,128]{2,1,0:T(8,128)S(1)}, u32[]{:S(2)}, u32[]{:S(2)}) collective-permute-start(f32[4,32,128]{2,1,0:T(8,128)S(1)} %get-tuple-element.43), channel_id=1, source_target_pairs={{0,4},{1,5},{2,6},{3,7},{4,0},{5,1},{6,2},{7,3},{8,12},{9,13},{10,... | collective-permute-start | bytes 196616 | tf_op jit(solution)/shard_map/ppermute | solution.py:224
  50.3 5.3 %collective-permute-start.7 = (f32[4,32,128]{2,1,0:T(8,128)S(1)}, f32[4,32,128]{2,1,0:T(8,128)S(1)}, u32[]{:S(2)}, u32[]{:S(2)}) collective-permute-start(f32[4,32,128]{2,1,0:T(8,128)S(1)} %get-tuple-element.44), channel_id=1, source_target_pairs={{0,5},{1,4},{2,7},{3,6},{4,1},{5,0},{6,3},{7,2},{8,13},{9,12},{10,... | collective-permute-start | bytes 196616 | tf_op jit(solution)/shard_map/ppermute | solution.py:224
  51.9 4.4 %collective-permute-start.8 = (f32[4,32,128]{2,1,0:T(8,128)S(1)}, f32[4,32,128]{2,1,0:T(8,128)S(1)}, u32[]{:S(2)}, u32[]{:S(2)}) collective-permute-start(f32[4,32,128]{2,1,0:T(8,128)S(1)} %get-tuple-element.45), channel_id=1, source_target_pairs={{0,6},{1,7},{2,4},{3,5},{4,2},{5,3},{6,0},{7,1},{8,14},{9,15},{10,... | collective-permute-start | bytes 196616 | tf_op jit(solution)/shard_map/ppermute | solution.py:224
  52.3 5.4 %collective-permute-start.9 = (f32[4,32,128]{2,1,0:T(8,128)S(1)}, f32[4,32,128]{2,1,0:T(8,128)S(1)}, u32[]{:S(2)}, u32[]{:S(2)}) collective-permute-start(f32[4,32,128]{2,1,0:T(8,128)S(1)} %get-tuple-element.46), channel_id=1, source_target_pairs={{0,7},{1,6},{2,5},{3,4},{4,3},{5,2},{6,1},{7,0},{8,15},{9,14},{10,... | collective-permute-start | bytes 196616 | tf_op jit(solution)/shard_map/ppermute | solution.py:224
  59.7 40.3 %all-to-all-start.1 = ((f32[32,2,16,128]{3,2,1,0:T(8,128)}), f32[32,2,16,128]{3,2,1,0:T(8,128)S(1)}, u32[]{:S(2)}, u32[]{:S(2)}) async-start(f32[32,2,16,128]{3,2,1,0:T(8,128)} %shard_map.44), calls=%async_computation.1 | async-start | bytes 1048576 | tf_op jit(solution)/shard_map/all_to_all | solution.py:313
  64.5 12.7 %collective-permute-start.10 = (f32[8,2,16,128]{3,2,1,0:T(8,128)S(1)}, f32[8,2,16,128]{3,2,1,0:T(8,128)S(1)}, u32[]{:S(2)}, u32[]{:S(2)}) collective-permute-start(f32[8,2,16,128]{3,2,1,0:T(8,128)S(1)} %get-tuple-element.50), channel_id=1, source_target_pairs={{0,8},{1,9},{2,10},{3,11},{4,12},{5,13},{6,14},{7,15},{8,0},{9,1},... | collective-permute-start | bytes 393224 | tf_op jit(solution)/shard_map/ppermute | solution.py:224
  66.3 21.9 %collective-permute-start.11 = (f32[8,2,16,128]{3,2,1,0:T(8,128)S(1)}, f32[8,2,16,128]{3,2,1,0:T(8,128)S(1)}, u32[]{:S(2)}, u32[]{:S(2)}) collective-permute-start(f32[8,2,16,128]{3,2,1,0:T(8,128)S(1)} %get-tuple-element.51), channel_id=1, source_target_pairs={{0,16},{1,17},{2,18},{3,19},{4,20},{5,21},{6,22},{7,23},{8,24},{9,... | collective-permute-start | bytes 393224 | tf_op jit(solution)/shard_map/ppermute | solution.py:224
  68.7 19.5 %collective-permute-start.12 = (f32[8,2,16,128]{3,2,1,0:T(8,128)S(1)}, f32[8,2,16,128]{3,2,1,0:T(8,128)S(1)}, u32[]{:S(2)}, u32[]{:S(2)}) collective-permute-start(f32[8,2,16,128]{3,2,1,0:T(8,128)S(1)} %get-tuple-element.52), channel_id=1, source_target_pairs={{0,24},{1,25},{2,26},{3,27},{4,28},{5,29},{6,30},{7,31},{8,16},{9,... | collective-permute-start | bytes 393224 | tf_op jit(solution)/shard_map/ppermute | solution.py:224
  88.2 5.2 %collective-permute-start.13 = (f32[4,2,16,128]{3,2,1,0:T(8,128)S(1)}, f32[4,2,16,128]{3,2,1,0:T(8,128)S(1)}, u32[]{:S(2)}, u32[]{:S(2)}) collective-permute-start(f32[4,2,16,128]{3,2,1,0:T(8,128)S(1)} %get-tuple-element.54), channel_id=1, source_target_pairs={{0,1},{1,0},{2,3},{3,2},{4,5},{5,4},{6,7},{7,6},{8,9},{9,8},{10,11... | collective-permute-start | bytes 196616 | tf_op jit(solution)/shard_map/ppermute | solution.py:224
  89.8 4.1 %collective-permute-start.14 = (f32[4,2,16,128]{3,2,1,0:T(8,128)S(1)}, f32[4,2,16,128]{3,2,1,0:T(8,128)S(1)}, u32[]{:S(2)}, u32[]{:S(2)}) collective-permute-start(f32[4,2,16,128]{3,2,1,0:T(8,128)S(1)} %get-tuple-element.55), channel_id=1, source_target_pairs={{0,2},{1,3},{2,0},{3,1},{4,6},{5,7},{6,4},{7,5},{8,10},{9,11},{10,... | collective-permute-start | bytes 196616 | tf_op jit(solution)/shard_map/ppermute | solution.py:224
  89.8 6.1 %collective-permute-start.15 = (f32[4,2,16,128]{3,2,1,0:T(8,128)S(1)}, f32[4,2,16,128]{3,2,1,0:T(8,128)S(1)}, u32[]{:S(2)}, u32[]{:S(2)}) collective-permute-start(f32[4,2,16,128]{3,2,1,0:T(8,128)S(1)} %get-tuple-element.56), channel_id=1, source_target_pairs={{0,3},{1,2},{2,1},{3,0},{4,7},{5,6},{6,5},{7,4},{8,11},{9,10},{10,... | collective-permute-start | bytes 196616 | tf_op jit(solution)/shard_map/ppermute | solution.py:224
  90.4 5.5 %collective-permute-start.16 = (f32[4,2,16,128]{3,2,1,0:T(8,128)S(1)}, f32[4,2,16,128]{3,2,1,0:T(8,128)S(1)}, u32[]{:S(2)}, u32[]{:S(2)}) collective-permute-start(f32[4,2,16,128]{3,2,1,0:T(8,128)S(1)} %get-tuple-element.57), channel_id=1, source_target_pairs={{0,4},{1,5},{2,6},{3,7},{4,0},{5,1},{6,2},{7,3},{8,12},{9,13},{10,... | collective-permute-start | bytes 196616 | tf_op jit(solution)/shard_map/ppermute | solution.py:224
  91.9 5.2 %collective-permute-start.17 = (f32[4,2,16,128]{3,2,1,0:T(8,128)S(1)}, f32[4,2,16,128]{3,2,1,0:T(8,128)S(1)}, u32[]{:S(2)}, u32[]{:S(2)}) collective-permute-start(f32[4,2,16,128]{3,2,1,0:T(8,128)S(1)} %get-tuple-element.58), channel_id=1, source_target_pairs={{0,5},{1,4},{2,7},{3,6},{4,1},{5,0},{6,3},{7,2},{8,13},{9,12},{10,... | collective-permute-start | bytes 196616 | tf_op jit(solution)/shard_map/ppermute | solution.py:224
  93.4 4.4 %collective-permute-start.18 = (f32[4,2,16,128]{3,2,1,0:T(8,128)S(1)}, f32[4,2,16,128]{3,2,1,0:T(8,128)S(1)}, u32[]{:S(2)}, u32[]{:S(2)}) collective-permute-start(f32[4,2,16,128]{3,2,1,0:T(8,128)S(1)} %get-tuple-element.59), channel_id=1, source_target_pairs={{0,6},{1,7},{2,4},{3,5},{4,2},{5,3},{6,0},{7,1},{8,14},{9,15},{10,... | collective-permute-start | bytes 196616 | tf_op jit(solution)/shard_map/ppermute | solution.py:224
  93.9 5.5 %collective-permute-start.19 = (f32[4,2,16,128]{3,2,1,0:T(8,128)S(1)}, f32[4,2,16,128]{3,2,1,0:T(8,128)S(1)}, u32[]{:S(2)}, u32[]{:S(2)}) collective-permute-start(f32[4,2,16,128]{3,2,1,0:T(8,128)S(1)} %get-tuple-element.60), channel_id=1, source_target_pairs={{0,7},{1,6},{2,5},{3,4},{4,3},{5,2},{6,1},{7,0},{8,15},{9,14},{10,... | collective-permute-start | bytes 196616 | tf_op jit(solution)/shard_map/ppermute | solution.py:224

commit v7 on v6

--- a/solution.py
+++ b/solution.py
@@ -75,7 +75,7 @@
         copy.wait()
 
 
-def first_kernel(slots, part, scale, wave_ref, level_ref, angle_ref, right_ref, left_ref, out_ref, held):
+def first_kernel(slots, part, scale, wave_ref, level_ref, angle_ref, right_ref, left_ref, out_ref, held, done, sems):
     lanes = wave_ref.shape[2]
     block = left_ref.shape[0]
     groups, per = len(slots) * part // block, block // part
@@ -84,14 +84,21 @@
     for g in range(groups):
         rows = slice(g * block, (g + 1) * block)
         c, s = trig(angle * level_ref[rows, :], scale)
-        for p, x in enumerate(rotate(wave_ref[0, rows, :], wave_ref[1, rows, :], c, s)):
-            held[p, rows, :] = tile_turn(x, right, left)
+        held[0, rows, :], held[1, rows, :] = rotate(wave_ref[0, rows, :], wave_ref[1, rows, :], c, s)
+    copies = []
     for p in range(2):
+        for g in range(groups):
+            rows = slice(g * block, (g + 1) * block)
+            held[p, rows, :] = tile_turn(held[p, rows, :], right, left)
         for tile in range(block // 8):
             values = butterflies([held[p, g * block + tile * 8:g * block + tile * 8 + 8, :] for g in range(groups)])
             k, row = tile * 8 // part, tile * 8 % part
             for g, value in enumerate(values):
-                out_ref[slots[g * per + k], p, row:row + 8, :] = value
+                done[slots[g * per + k], p, row:row + 8, :] = value
+        copies.append(pltpu.make_async_copy(done.at[:, p], out_ref.at[:, p], sems.at[p]))
+        copies[-1].start()
+    for copy in copies:
+        copy.wait()
 
 
 def deal_kernel(slabs, size, place_ref, *refs):
@@ -285,14 +292,17 @@
         mine.append(swap(picked[m - 1], axes, devices, m * size))
     sent = kernel_call(
         functools.partial(first_kernel, slots, part, scale), [WHOLE] * 5,
-        flat(devices, 2, part, lanes), [held_shape(2, total, lanes)],
+        flat(devices, 2, part, lanes),
+        [held_shape(2, total, lanes), held_shape(devices, 2, part, lanes), pltpu.SemaphoreType.DMA((2,))], FAR,
     )(near(wave), near(levels.reshape(total, lanes)), near(angles), right, left)
     seen = lax.all_to_all(sent, axes, 0, 0, tiled=True, axis_index_groups=[order])
     dealt = kernel_call(
         functools.partial(deal_kernel, slabs, size), [SCALAR] + [WHOLE] * slabs,
         [held_shape(slabs, part, lanes)] * size,
     )(place, *map(near, mine))
-    dealt = [dealt[0]] + [swap(dealt[k], axes, devices, k) for k in range(1, size)]
+    dealt = list(dealt)
+    for k in low_masks(size, core)[::-1]:
+        dealt[k] = swap(dealt[k], axes, devices, k)
     cos, sin = kernel_call(
         functools.partial(trig_kernel, slabs, size, scale), [SCALAR] + [WHOLE] * (1 + size),
         [held_shape(devices, part, lanes)] * 2,

time: 102 us -> 102 us (level)
  no operation moved by 1% of the time
where the time goes in v7:
time: 102 us; the launch traced here: 101 us
  waiting for transfers between devices  56.4 us (55%)
  starting transfers between devices  36 us (35%)
  Pallas kernels  7.67 us (8%)
    ppermute x20, waiting for transfers between devices, swap(): return lax.ppermute(x, axes, [(i, i ^ mask) for i in range(devices)])  56.4 us
    ppermute x20, starting transfers between devices, swap(): return lax.ppermute(x, axes, [(i, i ^ mask) for i in range(devices)])  24.1 us
    all_to_all x1, starting transfers between devices, body_fast(): lax.all_to_all(sent, axes, 0, 0, tiled=True, axis_index_groups=[order])  7.33 us
    all_to_all x1, starting transfers between devices, body_fast(): most = lax.all_to_all(most, axes, 0, 0, tiled=True)  4.49 us
    pallas_call x1, Pallas kernels, body_fast(): kernel_call(functools.partial(first_kernel, slots, part, scale), [WHOLE]...  2.15 us
  transfers between devices with their start and end apart: 22, of which 10 were waited for; matrix products, arithmetic and copies ran while one was open for 1% of the time, Pallas kernels for 1%

profile of v7, /device:TPU:0, one launch (start us, length us, event | category | flops | bytes accessed | tf_op | source)
XLA Modules:
  0.0 101.0 jit_solution(2009735781068177996)
XLA Ops:
  0.1 1.5 %shard_map.37 = (f32[2,1024,128]{2,1,0:T(8,128)S(1)}, f32[32,32,128]{2,1,0:T(8,128)S(1)}, f32[2,128]{1,0:T(2,128)S(1)}, f32[8,32,128]{2,1,0:T(8,128)S(1)}, f32[8...) custom-call(s32[1]{0:T(128)} %bitcast.place_ref, f32[2,1024,128]{2,1,0:T(8,128)} %bitcast.8, f32[32,32,128]{2,1,0:T(8,128)} %bitcast.9, ...), custom_call_target="tpu_custom_call" | custom-call | tf_op jit(solution)/shard_map/pallas_call | solution.py:284
  1.6 2.1 %shard_map.38 = f32[32,2,32,128]{3,2,1,0:T(8,128)} custom-call(f32[2,1024,128]{2,1,0:T(8,128)S(1)} %get-tuple-element.33.wave_ref, f32[1024,128]{1,0:T(8,128)S(1)} %bitcast.7, f32[2,128]{1,0:T(2,128)S(1)} %get-tuple-element.35.angle_ref, bf16[256,128]{1,0:T(8,128)(2,1)S(1)} %pad_maximum_fusion.right_ref, bf16[128,256]{1,0:T(8,128)(2,1)S(1)} %pad_maximum_fusion.2.left_ref), custom_call_target="tpu_custom_call" | custom-call | tf_op jit(solution)/shard_map/pallas_call | solution.py:293
  3.8 7.3 %all-to-all-start = ((f32[32,2,32,128]{3,2,1,0:T(8,128)}), f32[32,2,32,128]{3,2,1,0:T(8,128)S(1)}, u32[]{:S(2)}, u32[]{:S(2)}) async-start(f32[32,2,32,128]{3,2,1,0:T(8,128)} %shard_map.38), calls=%async_computation | async-start | bytes 2097152 | tf_op jit(solution)/shard_map/all_to_all | solution.py:298
  11.1 1.8 %collective-permute-start = (f32[8,32,128]{2,1,0:T(8,128)S(1)}, f32[8,32,128]{2,1,0:T(8,128)S(1)}, u32[]{:S(2)}, u32[]{:S(2)}) collective-permute-start(f32[8,32,128]{2,1,0:T(8,128)S(1)} %get-tuple-element.36), channel_id=1, source_target_pairs={{0,8},{1,9},{2,10},{3,11},{4,12},{5,13},{6,14},{7,15},{8,0},{9,1},... | collective-permute-start | bytes 393224 | tf_op jit(solution)/shard_map/ppermute | solution.py:231
  13.0 2.4 %collective-permute-start.1 = (f32[8,32,128]{2,1,0:T(8,128)S(1)}, f32[8,32,128]{2,1,0:T(8,128)S(1)}, u32[]{:S(2)}, u32[]{:S(2)}) collective-permute-start(f32[8,32,128]{2,1,0:T(8,128)S(1)} %get-tuple-element.37), channel_id=1, source_target_pairs={{0,16},{1,17},{2,18},{3,19},{4,20},{5,21},{6,22},{7,23},{8,24},{9,... | collective-permute-start | bytes 393224 | tf_op jit(solution)/shard_map/ppermute | solution.py:231
  15.4 0.2 collective-permute-start.2
  15.6 0.1 tile.13
  15.7 0.5 tile.14
  16.2 15.6 %collective-permute-done.refs_1_ = f32[8,32,128]{2,1,0:T(8,128)S(1)} collective-permute-done((f32[8,32,128]{2,1,0:T(8,128)S(1)}, f32[8,32,128]{2,1,0:T(8,128)S(1)}, u32[]{:S(2)}, u32[]{:S(2)}) %collective-permute-start) | collective-permute-done | bytes 131104 | tf_op jit(solution)/shard_map/ppermute | solution.py:231
  31.8 14.5 %collective-permute-done.1.refs_2_ = f32[8,32,128]{2,1,0:T(8,128)S(1)} collective-permute-done((f32[8,32,128]{2,1,0:T(8,128)S(1)}, f32[8,32,128]{2,1,0:T(8,128)S(1)}, u32[]{:S(2)}, u32[]{:S(2)}) %collective-permute-start.1) | collective-permute-done | bytes 131104 | tf_op jit(solution)/shard_map/ppermute | solution.py:231
  46.3 0.0 collective-permute-done.2.refs_3_
  46.4 1.6 %collective-permute-start.3 = (f32[4,32,128]{2,1,0:T(8,128)S(1)}, f32[4,32,128]{2,1,0:T(8,128)S(1)}, u32[]{:S(2)}, u32[]{:S(2)}) collective-permute-start(f32[4,32,128]{2,1,0:T(8,128)S(1)} %get-tuple-element.40), channel_id=1, source_target_pairs={{0,1},{1,0},{2,3},{3,2},{4,5},{5,4},{6,7},{7,6},{8,9},{9,8},{10,11... | collective-permute-start | bytes 196616 | tf_op jit(solution)/shard_map/ppermute | solution.py:231
  48.0 0.0 collective-permute-start.4
  48.0 0.1 compare_select_fusion
  48.1 0.7 collective-permute-start.5
  48.7 1.5 %collective-permute-start.6 = (f32[4,32,128]{2,1,0:T(8,128)S(1)}, f32[4,32,128]{2,1,0:T(8,128)S(1)}, u32[]{:S(2)}, u32[]{:S(2)}) collective-permute-start(f32[4,32,128]{2,1,0:T(8,128)S(1)} %get-tuple-element.43), channel_id=1, source_target_pairs={{0,4},{1,5},{2,6},{3,7},{4,0},{5,1},{6,2},{7,3},{8,12},{9,13},{10,... | collective-permute-start | bytes 196616 | tf_op jit(solution)/shard_map/ppermute | solution.py:231
  50.2 1.5 %collective-permute-start.7 = (f32[4,32,128]{2,1,0:T(8,128)S(1)}, f32[4,32,128]{2,1,0:T(8,128)S(1)}, u32[]{:S(2)}, u32[]{:S(2)}) collective-permute-start(f32[4,32,128]{2,1,0:T(8,128)S(1)} %get-tuple-element.44), channel_id=1, source_target_pairs={{0,5},{1,4},{2,7},{3,6},{4,1},{5,0},{6,3},{7,2},{8,13},{9,12},{10,... | collective-permute-start | bytes 196616 | tf_op jit(solution)/shard_map/ppermute | solution.py:231
  51.7 0.5 collective-permute-start.8
  52.2 1.8 %collective-permute-start.9 = (f32[4,32,128]{2,1,0:T(8,128)S(1)}, f32[4,32,128]{2,1,0:T(8,128)S(1)}, u32[]{:S(2)}, u32[]{:S(2)}) collective-permute-start(f32[4,32,128]{2,1,0:T(8,128)S(1)} %get-tuple-element.46), channel_id=1, source_target_pairs={{0,7},{1,6},{2,5},{3,4},{4,3},{5,2},{6,1},{7,0},{8,15},{9,14},{10,... | collective-permute-start | bytes 196616 | tf_op jit(solution)/shard_map/ppermute | solution.py:231
  54.0 0.0 collective-permute-done.5.refs_3_
  54.1 1.4 %collective-permute-done.7.refs_5_ = f32[4,32,128]{2,1,0:T(8,128)S(1)} collective-permute-done((f32[4,32,128]{2,1,0:T(8,128)S(1)}, f32[4,32,128]{2,1,0:T(8,128)S(1)}, u32[]{:S(2)}, u32[]{:S(2)}) %collective-permute-start.7) | collective-permute-done | bytes 65568 | tf_op jit(solution)/shard_map/ppermute | solution.py:231
  55.5 0.7 collective-permute-done.8.refs_6_
  56.1 1.5 %collective-permute-done.9.refs_7_ = f32[4,32,128]{2,1,0:T(8,128)S(1)} collective-permute-done((f32[4,32,128]{2,1,0:T(8,128)S(1)}, f32[4,32,128]{2,1,0:T(8,128)S(1)}, u32[]{:S(2)}, u32[]{:S(2)}) %collective-permute-start.9) | collective-permute-done | bytes 65568 | tf_op jit(solution)/shard_map/ppermute | solution.py:231
  57.6 0.5 shard_map.40
  58.1 0.0 all-to-all-done.seen_ref
  58.1 1.5 %shard_map.44 = f32[32,2,16,128]{3,2,1,0:T(8,128)} custom-call(f32[32,2,32,128]{3,2,1,0:T(8,128)S(1)} %all-to-all-done.seen_ref, f32[32,32,128]{2,1,0:T(8,128)S(1)} %get-tuple-element.47.cos_ref, f32[32,32,128]{2,1,0:T(8,128)S(1)} %get-tuple-element.48.sin_ref, bf16[256,128]{1,0:T(8,128)(2,1)S(1)} %pad_maximum_fusion.right_ref, ...), custom_call_target="tpu_custom_call" | custom-call | tf_op jit(solution)/shard_map/pallas_call | solution.py:319
  59.6 4.5 %all-to-all-start.1 = ((f32[32,2,16,128]{3,2,1,0:T(8,128)}), f32[32,2,16,128]{3,2,1,0:T(8,128)S(1)}, u32[]{:S(2)}, u32[]{:S(2)}) async-start(f32[32,2,16,128]{3,2,1,0:T(8,128)} %shard_map.44), calls=%async_computation.1 | async-start | bytes 1048576 | tf_op jit(solution)/shard_map/all_to_all | solution.py:323
  64.1 0.3 shard_map.41
  64.4 1.8 %collective-permute-start.10 = (f32[8,2,16,128]{3,2,1,0:T(8,128)S(1)}, f32[8,2,16,128]{3,2,1,0:T(8,128)S(1)}, u32[]{:S(2)}, u32[]{:S(2)}) collective-permute-start(f32[8,2,16,128]{3,2,1,0:T(8,128)S(1)} %get-tuple-element.50), channel_id=1, source_target_pairs={{0,8},{1,9},{2,10},{3,11},{4,12},{5,13},{6,14},{7,15},{8,0},{9,1},... | collective-permute-start | bytes 393224 | tf_op jit(solution)/shard_map/ppermute | solution.py:231
  66.2 2.4 %collective-permute-start.11 = (f32[8,2,16,128]{3,2,1,0:T(8,128)S(1)}, f32[8,2,16,128]{3,2,1,0:T(8,128)S(1)}, u32[]{:S(2)}, u32[]{:S(2)}) collective-permute-start(f32[8,2,16,128]{3,2,1,0:T(8,128)S(1)} %get-tuple-element.51), channel_id=1, source_target_pairs={{0,16},{1,17},{2,18},{3,19},{4,20},{5,21},{6,22},{7,23},{8,24},{9,... | collective-permute-start | bytes 393224 | tf_op jit(solution)/shard_map/ppermute | solution.py:231
  68.6 0.2 collective-permute-start.12
  68.8 8.3 %collective-permute-done.10.refs_1_ = f32[8,2,16,128]{3,2,1,0:T(8,128)S(1)} collective-permute-done((f32[8,2,16,128]{3,2,1,0:T(8,128)S(1)}, f32[8,2,16,128]{3,2,1,0:T(8,128)S(1)}, u32[]{:S(2)}, u32[]{:S(2)}) %collective-permute-start.10) | collective-permute-done | bytes 131104 | tf_op jit(solution)/shard_map/ppermute | solution.py:231
  77.1 11.0 %collective-permute-done.11.refs_2_ = f32[8,2,16,128]{3,2,1,0:T(8,128)S(1)} collective-permute-done((f32[8,2,16,128]{3,2,1,0:T(8,128)S(1)}, f32[8,2,16,128]{3,2,1,0:T(8,128)S(1)}, u32[]{:S(2)}, u32[]{:S(2)}) %collective-permute-start.11) | collective-permute-done | bytes 131104 | tf_op jit(solution)/shard_map/ppermute | solution.py:231
  88.1 1.5 %collective-permute-start.13 = (f32[4,2,16,128]{3,2,1,0:T(8,128)S(1)}, f32[4,2,16,128]{3,2,1,0:T(8,128)S(1)}, u32[]{:S(2)}, u32[]{:S(2)}) collective-permute-start(f32[4,2,16,128]{3,2,1,0:T(8,128)S(1)} %get-tuple-element.54), channel_id=1, source_target_pairs={{0,1},{1,0},{2,3},{3,2},{4,5},{5,4},{6,7},{7,6},{8,9},{9,8},{10,11... | collective-permute-start | bytes 196616 | tf_op jit(solution)/shard_map/ppermute | solution.py:231
  89.6 0.7 collective-permute-start.15
  90.3 1.5 %collective-permute-start.16 = (f32[4,2,16,128]{3,2,1,0:T(8,128)S(1)}, f32[4,2,16,128]{3,2,1,0:T(8,128)S(1)}, u32[]{:S(2)}, u32[]{:S(2)}) collective-permute-start(f32[4,2,16,128]{3,2,1,0:T(8,128)S(1)} %get-tuple-element.57), channel_id=1, source_target_pairs={{0,4},{1,5},{2,6},{3,7},{4,0},{5,1},{6,2},{7,3},{8,12},{9,13},{10,... | collective-permute-start | bytes 196616 | tf_op jit(solution)/shard_map/ppermute | solution.py:231
  91.8 1.5 %collective-permute-start.17 = (f32[4,2,16,128]{3,2,1,0:T(8,128)S(1)}, f32[4,2,16,128]{3,2,1,0:T(8,128)S(1)}, u32[]{:S(2)}, u32[]{:S(2)}) collective-permute-start(f32[4,2,16,128]{3,2,1,0:T(8,128)S(1)} %get-tuple-element.58), channel_id=1, source_target_pairs={{0,5},{1,4},{2,7},{3,6},{4,1},{5,0},{6,3},{7,2},{8,13},{9,12},{10,... | collective-permute-start | bytes 196616 | tf_op jit(solution)/shard_map/ppermute | solution.py:231
  93.2 0.0 collective-permute-done.13.refs_1_
  93.2 0.5 collective-permute-start.18
  93.8 0.0 collective-permute-done.14.refs_2_
  93.8 2.0 %collective-permute-start.19 = (f32[4,2,16,128]{3,2,1,0:T(8,128)S(1)}, f32[4,2,16,128]{3,2,1,0:T(8,128)S(1)}, u32[]{:S(2)}, u32[]{:S(2)}) collective-permute-start(f32[4,2,16,128]{3,2,1,0:T(8,128)S(1)} %get-tuple-element.60), channel_id=1, source_target_pairs={{0,7},{1,6},{2,5},{3,4},{4,3},{5,2},{6,1},{7,0},{8,15},{9,14},{10,... | collective-permute-start | bytes 196616 | tf_op jit(solution)/shard_map/ppermute | solution.py:231
  95.8 0.0 collective-permute-done.16.refs_4_
  95.8 1.2 %collective-permute-done.17.refs_5_ = f32[4,2,16,128]{3,2,1,0:T(8,128)S(1)} collective-permute-done((f32[4,2,16,128]{3,2,1,0:T(8,128)S(1)}, f32[4,2,16,128]{3,2,1,0:T(8,128)S(1)}, u32[]{:S(2)}, u32[]{:S(2)}) %collective-permute-start.17) | collective-permute-done | bytes 65568 | tf_op jit(solution)/shard_map/ppermute | solution.py:231
  96.9 0.7 collective-permute-done.18.refs_6_
  97.6 1.7 %collective-permute-done.19.refs_7_ = f32[4,2,16,128]{3,2,1,0:T(8,128)S(1)} collective-permute-done((f32[4,2,16,128]{3,2,1,0:T(8,128)S(1)}, f32[4,2,16,128]{3,2,1,0:T(8,128)S(1)}, u32[]{:S(2)}, u32[]{:S(2)}) %collective-permute-start.19) | collective-permute-done | bytes 65568 | tf_op jit(solution)/shard_map/ppermute | solution.py:231
  99.3 0.6 shard_map.43.few_ref
  99.9 0.0 all-to-all-done.1.most_ref
  99.9 1.1 %shard_map.45 = f32[2,1024,128]{2,1,0:T(8,128)} custom-call(f32[32,2,16,128]{3,2,1,0:T(8,128)S(1)} %shard_map.43.few_ref, f32[32,2,16,128]{3,2,1,0:T(8,128)S(1)} %all-to-all-done.1.most_ref), custom_call_target="tpu_custom_call" | custom-call | tf_op jit(solution)/shard_map/pallas_call | solution.py:335
  (15 shorter events, 0.2 us)
Async XLA Ops:
  3.8 54.3 %all-to-all-start = ((f32[32,2,32,128]{3,2,1,0:T(8,128)}), f32[32,2,32,128]{3,2,1,0:T(8,128)S(1)}, u32[]{:S(2)}, u32[]{:S(2)}) async-start(f32[32,2,32,128]{3,2,1,0:T(8,128)} %shard_map.38), calls=%async_computation | async-start | bytes 2097152 | tf_op jit(solution)/shard_map/all_to_all | solution.py:298
  11.1 20.7 %collective-permute-start = (f32[8,32,128]{2,1,0:T(8,128)S(1)}, f32[8,32,128]{2,1,0:T(8,128)S(1)}, u32[]{:S(2)}, u32[]{:S(2)}) collective-permute-start(f32[8,32,128]{2,1,0:T(8,128)S(1)} %get-tuple-element.36), channel_id=1, source_target_pairs={{0,8},{1,9},{2,10},{3,11},{4,12},{5,13},{6,14},{7,15},{8,0},{9,1},... | collective-permute-start | bytes 393224 | tf_op jit(solution)/shard_map/ppermute | solution.py:231
  13.0 33.4 %collective-permute-start.1 = (f32[8,32,128]{2,1,0:T(8,128)S(1)}, f32[8,32,128]{2,1,0:T(8,128)S(1)}, u32[]{:S(2)}, u32[]{:S(2)}) collective-permute-start(f32[8,32,128]{2,1,0:T(8,128)S(1)} %get-tuple-element.37), channel_id=1, source_target_pairs={{0,16},{1,17},{2,18},{3,19},{4,20},{5,21},{6,22},{7,23},{8,24},{9,... | collective-permute-start | bytes 393224 | tf_op jit(solution)/shard_map/ppermute | solution.py:231
  15.4 31.0 %collective-permute-start.2 = (f32[8,32,128]{2,1,0:T(8,128)S(1)}, f32[8,32,128]{2,1,0:T(8,128)S(1)}, u32[]{:S(2)}, u32[]{:S(2)}) collective-permute-start(f32[8,32,128]{2,1,0:T(8,128)S(1)} %get-tuple-element.38), channel_id=1, source_target_pairs={{0,24},{1,25},{2,26},{3,27},{4,28},{5,29},{6,30},{7,31},{8,16},{9,... | collective-permute-start | bytes 393224 | tf_op jit(solution)/shard_map/ppermute | solution.py:231
  46.4 5.4 %collective-permute-start.3 = (f32[4,32,128]{2,1,0:T(8,128)S(1)}, f32[4,32,128]{2,1,0:T(8,128)S(1)}, u32[]{:S(2)}, u32[]{:S(2)}) collective-permute-start(f32[4,32,128]{2,1,0:T(8,128)S(1)} %get-tuple-element.40), channel_id=1, source_target_pairs={{0,1},{1,0},{2,3},{3,2},{4,5},{5,4},{6,7},{7,6},{8,9},{9,8},{10,11... | collective-permute-start | bytes 196616 | tf_op jit(solution)/shard_map/ppermute | solution.py:231
  48.0 4.2 %collective-permute-start.4 = (f32[4,32,128]{2,1,0:T(8,128)S(1)}, f32[4,32,128]{2,1,0:T(8,128)S(1)}, u32[]{:S(2)}, u32[]{:S(2)}) collective-permute-start(f32[4,32,128]{2,1,0:T(8,128)S(1)} %get-tuple-element.41), channel_id=1, source_target_pairs={{0,2},{1,3},{2,0},{3,1},{4,6},{5,7},{6,4},{7,5},{8,10},{9,11},{10,... | collective-permute-start | bytes 196616 | tf_op jit(solution)/shard_map/ppermute | solution.py:231
  48.1 6.0 %collective-permute-start.5 = (f32[4,32,128]{2,1,0:T(8,128)S(1)}, f32[4,32,128]{2,1,0:T(8,128)S(1)}, u32[]{:S(2)}, u32[]{:S(2)}) collective-permute-start(f32[4,32,128]{2,1,0:T(8,128)S(1)} %get-tuple-element.42), channel_id=1, source_target_pairs={{0,3},{1,2},{2,1},{3,0},{4,7},{5,6},{6,5},{7,4},{8,11},{9,10},{10,... | collective-permute-start | bytes 196616 | tf_op jit(solution)/shard_map/ppermute | solution.py:231
  48.7 5.3 %collective-permute-start.6 = (f32[4,32,128]{2,1,0:T(8,128)S(1)}, f32[4,32,128]{2,1,0:T(8,128)S(1)}, u32[]{:S(2)}, u32[]{:S(2)}) collective-permute-start(f32[4,32,128]{2,1,0:T(8,128)S(1)} %get-tuple-element.43), channel_id=1, source_target_pairs={{0,4},{1,5},{2,6},{3,7},{4,0},{5,1},{6,2},{7,3},{8,12},{9,13},{10,... | collective-permute-start | bytes 196616 | tf_op jit(solution)/shard_map/ppermute | solution.py:231
  50.2 5.3 %collective-permute-start.7 = (f32[4,32,128]{2,1,0:T(8,128)S(1)}, f32[4,32,128]{2,1,0:T(8,128)S(1)}, u32[]{:S(2)}, u32[]{:S(2)}) collective-permute-start(f32[4,32,128]{2,1,0:T(8,128)S(1)} %get-tuple-element.44), channel_id=1, source_target_pairs={{0,5},{1,4},{2,7},{3,6},{4,1},{5,0},{6,3},{7,2},{8,13},{9,12},{10,... | collective-permute-start | bytes 196616 | tf_op jit(solution)/shard_map/ppermute | solution.py:231
  51.7 4.4 %collective-permute-start.8 = (f32[4,32,128]{2,1,0:T(8,128)S(1)}, f32[4,32,128]{2,1,0:T(8,128)S(1)}, u32[]{:S(2)}, u32[]{:S(2)}) collective-permute-start(f32[4,32,128]{2,1,0:T(8,128)S(1)} %get-tuple-element.45), channel_id=1, source_target_pairs={{0,6},{1,7},{2,4},{3,5},{4,2},{5,3},{6,0},{7,1},{8,14},{9,15},{10,... | collective-permute-start | bytes 196616 | tf_op jit(solution)/shard_map/ppermute | solution.py:231
  52.2 5.4 %collective-permute-start.9 = (f32[4,32,128]{2,1,0:T(8,128)S(1)}, f32[4,32,128]{2,1,0:T(8,128)S(1)}, u32[]{:S(2)}, u32[]{:S(2)}) collective-permute-start(f32[4,32,128]{2,1,0:T(8,128)S(1)} %get-tuple-element.46), channel_id=1, source_target_pairs={{0,7},{1,6},{2,5},{3,4},{4,3},{5,2},{6,1},{7,0},{8,15},{9,14},{10,... | collective-permute-start | bytes 196616 | tf_op jit(solution)/shard_map/ppermute | solution.py:231
  59.6 40.3 %all-to-all-start.1 = ((f32[32,2,16,128]{3,2,1,0:T(8,128)}), f32[32,2,16,128]{3,2,1,0:T(8,128)S(1)}, u32[]{:S(2)}, u32[]{:S(2)}) async-start(f32[32,2,16,128]{3,2,1,0:T(8,128)} %shard_map.44), calls=%async_computation.1 | async-start | bytes 1048576 | tf_op jit(solution)/shard_map/all_to_all | solution.py:323
  64.4 12.7 %collective-permute-start.10 = (f32[8,2,16,128]{3,2,1,0:T(8,128)S(1)}, f32[8,2,16,128]{3,2,1,0:T(8,128)S(1)}, u32[]{:S(2)}, u32[]{:S(2)}) collective-permute-start(f32[8,2,16,128]{3,2,1,0:T(8,128)S(1)} %get-tuple-element.50), channel_id=1, source_target_pairs={{0,8},{1,9},{2,10},{3,11},{4,12},{5,13},{6,14},{7,15},{8,0},{9,1},... | collective-permute-start | bytes 393224 | tf_op jit(solution)/shard_map/ppermute | solution.py:231
  66.2 21.9 %collective-permute-start.11 = (f32[8,2,16,128]{3,2,1,0:T(8,128)S(1)}, f32[8,2,16,128]{3,2,1,0:T(8,128)S(1)}, u32[]{:S(2)}, u32[]{:S(2)}) collective-permute-start(f32[8,2,16,128]{3,2,1,0:T(8,128)S(1)} %get-tuple-element.51), channel_id=1, source_target_pairs={{0,16},{1,17},{2,18},{3,19},{4,20},{5,21},{6,22},{7,23},{8,24},{9,... | collective-permute-start | bytes 393224 | tf_op jit(solution)/shard_map/ppermute | solution.py:231
  68.6 19.5 %collective-permute-start.12 = (f32[8,2,16,128]{3,2,1,0:T(8,128)S(1)}, f32[8,2,16,128]{3,2,1,0:T(8,128)S(1)}, u32[]{:S(2)}, u32[]{:S(2)}) collective-permute-start(f32[8,2,16,128]{3,2,1,0:T(8,128)S(1)} %get-tuple-element.52), channel_id=1, source_target_pairs={{0,24},{1,25},{2,26},{3,27},{4,28},{5,29},{6,30},{7,31},{8,16},{9,... | collective-permute-start | bytes 393224 | tf_op jit(solution)/shard_map/ppermute | solution.py:231
  88.1 5.2 %collective-permute-start.13 = (f32[4,2,16,128]{3,2,1,0:T(8,128)S(1)}, f32[4,2,16,128]{3,2,1,0:T(8,128)S(1)}, u32[]{:S(2)}, u32[]{:S(2)}) collective-permute-start(f32[4,2,16,128]{3,2,1,0:T(8,128)S(1)} %get-tuple-element.54), channel_id=1, source_target_pairs={{0,1},{1,0},{2,3},{3,2},{4,5},{5,4},{6,7},{7,6},{8,9},{9,8},{10,11... | collective-permute-start | bytes 196616 | tf_op jit(solution)/shard_map/ppermute | solution.py:231
  89.6 4.1 %collective-permute-start.14 = (f32[4,2,16,128]{3,2,1,0:T(8,128)S(1)}, f32[4,2,16,128]{3,2,1,0:T(8,128)S(1)}, u32[]{:S(2)}, u32[]{:S(2)}) collective-permute-start(f32[4,2,16,128]{3,2,1,0:T(8,128)S(1)} %get-tuple-element.55), channel_id=1, source_target_pairs={{0,2},{1,3},{2,0},{3,1},{4,6},{5,7},{6,4},{7,5},{8,10},{9,11},{10,... | collective-permute-start | bytes 196616 | tf_op jit(solution)/shard_map/ppermute | solution.py:231
  89.6 6.1 %collective-permute-start.15 = (f32[4,2,16,128]{3,2,1,0:T(8,128)S(1)}, f32[4,2,16,128]{3,2,1,0:T(8,128)S(1)}, u32[]{:S(2)}, u32[]{:S(2)}) collective-permute-start(f32[4,2,16,128]{3,2,1,0:T(8,128)S(1)} %get-tuple-element.56), channel_id=1, source_target_pairs={{0,3},{1,2},{2,1},{3,0},{4,7},{5,6},{6,5},{7,4},{8,11},{9,10},{10,... | collective-permute-start | bytes 196616 | tf_op jit(solution)/shard_map/ppermute | solution.py:231
  90.3 5.5 %collective-permute-start.16 = (f32[4,2,16,128]{3,2,1,0:T(8,128)S(1)}, f32[4,2,16,128]{3,2,1,0:T(8,128)S(1)}, u32[]{:S(2)}, u32[]{:S(2)}) collective-permute-start(f32[4,2,16,128]{3,2,1,0:T(8,128)S(1)} %get-tuple-element.57), channel_id=1, source_target_pairs={{0,4},{1,5},{2,6},{3,7},{4,0},{5,1},{6,2},{7,3},{8,12},{9,13},{10,... | collective-permute-start | bytes 196616 | tf_op jit(solution)/shard_map/ppermute | solution.py:231
  91.8 5.2 %collective-permute-start.17 = (f32[4,2,16,128]{3,2,1,0:T(8,128)S(1)}, f32[4,2,16,128]{3,2,1,0:T(8,128)S(1)}, u32[]{:S(2)}, u32[]{:S(2)}) collective-permute-start(f32[4,2,16,128]{3,2,1,0:T(8,128)S(1)} %get-tuple-element.58), channel_id=1, source_target_pairs={{0,5},{1,4},{2,7},{3,6},{4,1},{5,0},{6,3},{7,2},{8,13},{9,12},{10,... | collective-permute-start | bytes 196616 | tf_op jit(solution)/shard_map/ppermute | solution.py:231
  93.2 4.4 %collective-permute-start.18 = (f32[4,2,16,128]{3,2,1,0:T(8,128)S(1)}, f32[4,2,16,128]{3,2,1,0:T(8,128)S(1)}, u32[]{:S(2)}, u32[]{:S(2)}) collective-permute-start(f32[4,2,16,128]{3,2,1,0:T(8,128)S(1)} %get-tuple-element.59), channel_id=1, source_target_pairs={{0,6},{1,7},{2,4},{3,5},{4,2},{5,3},{6,0},{7,1},{8,14},{9,15},{10,... | collective-permute-start | bytes 196616 | tf_op jit(solution)/shard_map/ppermute | solution.py:231
  93.8 5.5 %collective-permute-start.19 = (f32[4,2,16,128]{3,2,1,0:T(8,128)S(1)}, f32[4,2,16,128]{3,2,1,0:T(8,128)S(1)}, u32[]{:S(2)}, u32[]{:S(2)}) collective-permute-start(f32[4,2,16,128]{3,2,1,0:T(8,128)S(1)} %get-tuple-element.60), channel_id=1, source_target_pairs={{0,7},{1,6},{2,5},{3,4},{4,3},{5,2},{6,1},{7,0},{8,15},{9,14},{10,... | collective-permute-start | bytes 196616 | tf_op jit(solution)/shard_map/ppermute | solution.py:231

commit v8 on v7

--- a/solution.py
+++ b/solution.py
@@ -168,18 +168,18 @@
                 out_ref[d:d + step, p, (tile - start) * 8:(tile - start) * 8 + 8, :] = tile_turn(x, right, left).reshape(step, 8, lanes)
 
 
-def gather_kernel(slabs, size, place_ref, right_ref, left_ref, *refs):
-    parts, out_ref, held = refs[:size], refs[size], refs[size + 1]
-    for k in range(size):
-        for m in range(slabs):
-            held[place_ref[0] ^ (m * size + k)] = parts[k][m]
+def gather_kernel(slabs, size, kinds, place_ref, right_ref, left_ref, *refs):
+    parts, out_ref = refs[:len(kinds)], refs[-1]
     right, left = right_ref[...], left_ref[...]
-    step = left.shape[0] // 8
+    count, lanes = out_ref.shape[2:]
+    step = left.shape[0] // (slabs * count)
     for p in range(2):
-        for d in range(0, slabs * size, step):
-            for row in range(0, held.shape[2], 8):
-                x = held[d:d + step, p, row:row + 8, :].reshape(step * 8, held.shape[3])
-                out_ref[d:d + step, p, row:row + 8, :] = tile_turn(x, right, left).reshape(step, 8, held.shape[3])
+        for i in range(0, len(kinds), step):
+            x = jnp.concatenate([part[:, p].reshape(slabs * count, lanes) for part in parts[i:i + step]], axis=0)
+            y = tile_turn(x, right, left).reshape(step, slabs, count, lanes)
+            for j in range(step):
+                for m in range(slabs):
+                    out_ref[place_ref[0] ^ (m * size + kinds[i + j]), p] = y[j, m]
 
 
 def last_kernel(devices, part, few_ref, most_ref, out_ref, held, done, sems):
@@ -328,10 +328,16 @@
     few = list(few)
     for k in low_masks(size, core):
         few[k] = swap(few[k], axes, devices, k)
-    few = kernel_call(
-        functools.partial(gather_kernel, slabs, size), [SCALAR] + [WHOLE] * (2 + size),
-        held_shape(devices, 2, count, lanes), [held_shape(devices, 2, count, lanes)],
-    )(place, right, left_small, *map(near, few))
+    kinds = [0, *low_masks(size, core)]
+    done = []
+    for some in (kinds[:size // 2], kinds[size // 2:]):
+        specs = [SCALAR] + [WHOLE] * (2 + len(some) + len(done))
+        done = [pl.pallas_call(
+            functools.partial(gather_kernel, slabs, size, some), in_specs=specs, out_specs=WHOLE,
+            out_shape=held_shape(devices, 2, count, lanes), compiler_params=PARAMS,
+            input_output_aliases={len(specs) - 1: 0} if done else {},
+        )(place, right, left_small, *(near(few[k]) for k in some), *map(near, done))]
+    few = done[0]
     out = kernel_call(
         functools.partial(last_kernel, devices, part), [WHOLE] * 2, flat(2, total, lanes),
         [held_shape(2, devices // 8, part * 8 // 8, 8, lanes), held_shape(2, total, lanes), pltpu.SemaphoreType.DMA((2 * devices // 8,))],

time: 102 us -> 101 us (level)
  transfers between devices with their start and end apart: 22 -> 22, of which waited for: 10 -> 9; matrix products, arithmetic and copies ran while one was open for 1% -> 1% of each run, Pallas kernels for 1% -> 2%
where the time goes in v8:
time: 101 us; the launch traced here: 100 us
  waiting for transfers between devices  56.3 us (56%)
  starting transfers between devices  35.3 us (35%)
  Pallas kernels  7.92 us (8%)
    ppermute x20, waiting for transfers between devices, swap(): return lax.ppermute(x, axes, [(i, i ^ mask) for i in range(devices)])  56.3 us
    ppermute x20, starting transfers between devices, swap(): return lax.ppermute(x, axes, [(i, i ^ mask) for i in range(devices)])  23.5 us
    all_to_all x1, starting transfers between devices, body_fast(): lax.all_to_all(sent, axes, 0, 0, tiled=True, axis_index_groups=[order])  7.33 us
    all_to_all x1, starting transfers between devices, body_fast(): most = lax.all_to_all(most, axes, 0, 0, tiled=True)  4.49 us
    pallas_call x1, Pallas kernels, body_fast(): kernel_call(functools.partial(first_kernel, slots, part, scale), [WHOLE]...  2.15 us
  transfers between devices with their start and end apart: 22, of which 9 were waited for; matrix products, arithmetic and copies ran while one was open for 1% of the time, Pallas kernels for 2%

profile of v8, /device:TPU:0, one launch (start us, length us, event | category | flops | bytes accessed | tf_op | source)
XLA Modules:
  0.0 100.5 jit_solution(7851592162076637174)
XLA Ops:
  0.1 1.5 %shard_map.37 = (f32[2,1024,128]{2,1,0:T(8,128)S(1)}, f32[32,32,128]{2,1,0:T(8,128)S(1)}, f32[2,128]{1,0:T(2,128)S(1)}, f32[8,32,128]{2,1,0:T(8,128)S(1)}, f32[8...) custom-call(s32[1]{0:T(128)} %bitcast.place_ref, f32[2,1024,128]{2,1,0:T(8,128)} %bitcast.8, f32[32,32,128]{2,1,0:T(8,128)} %bitcast.9, ...), custom_call_target="tpu_custom_call" | custom-call | tf_op jit(solution)/shard_map/pallas_call | solution.py:284
  1.6 2.1 %shard_map.38 = f32[32,2,32,128]{3,2,1,0:T(8,128)} custom-call(f32[2,1024,128]{2,1,0:T(8,128)S(1)} %get-tuple-element.33.wave_ref, f32[1024,128]{1,0:T(8,128)S(1)} %bitcast.7, f32[2,128]{1,0:T(2,128)S(1)} %get-tuple-element.35.angle_ref, bf16[256,128]{1,0:T(8,128)(2,1)S(1)} %pad_maximum_fusion.right_ref, bf16[128,256]{1,0:T(8,128)(2,1)S(1)} %pad_maximum_fusion.2.left_ref), custom_call_target="tpu_custom_call" | custom-call | tf_op jit(solution)/shard_map/pallas_call | solution.py:293
  3.8 7.3 %all-to-all-start = ((f32[32,2,32,128]{3,2,1,0:T(8,128)}), f32[32,2,32,128]{3,2,1,0:T(8,128)S(1)}, u32[]{:S(2)}, u32[]{:S(2)}) async-start(f32[32,2,32,128]{3,2,1,0:T(8,128)} %shard_map.38), calls=%async_computation | async-start | bytes 2097152 | tf_op jit(solution)/shard_map/all_to_all | solution.py:298
  11.1 1.8 %collective-permute-start = (f32[8,32,128]{2,1,0:T(8,128)S(1)}, f32[8,32,128]{2,1,0:T(8,128)S(1)}, u32[]{:S(2)}, u32[]{:S(2)}) collective-permute-start(f32[8,32,128]{2,1,0:T(8,128)S(1)} %get-tuple-element.36), channel_id=1, source_target_pairs={{0,8},{1,9},{2,10},{3,11},{4,12},{5,13},{6,14},{7,15},{8,0},{9,1},... | collective-permute-start | bytes 393224 | tf_op jit(solution)/shard_map/ppermute | solution.py:231
  13.0 2.4 %collective-permute-start.1 = (f32[8,32,128]{2,1,0:T(8,128)S(1)}, f32[8,32,128]{2,1,0:T(8,128)S(1)}, u32[]{:S(2)}, u32[]{:S(2)}) collective-permute-start(f32[8,32,128]{2,1,0:T(8,128)S(1)} %get-tuple-element.37), channel_id=1, source_target_pairs={{0,16},{1,17},{2,18},{3,19},{4,20},{5,21},{6,22},{7,23},{8,24},{9,... | collective-permute-start | bytes 393224 | tf_op jit(solution)/shard_map/ppermute | solution.py:231
  15.4 0.2 collective-permute-start.2
  15.6 0.1 tile.13
  15.7 0.5 tile.14
  16.2 15.6 %collective-permute-done.refs_1_ = f32[8,32,128]{2,1,0:T(8,128)S(1)} collective-permute-done((f32[8,32,128]{2,1,0:T(8,128)S(1)}, f32[8,32,128]{2,1,0:T(8,128)S(1)}, u32[]{:S(2)}, u32[]{:S(2)}) %collective-permute-start) | collective-permute-done | bytes 131104 | tf_op jit(solution)/shard_map/ppermute | solution.py:231
  31.8 14.5 %collective-permute-done.1.refs_2_ = f32[8,32,128]{2,1,0:T(8,128)S(1)} collective-permute-done((f32[8,32,128]{2,1,0:T(8,128)S(1)}, f32[8,32,128]{2,1,0:T(8,128)S(1)}, u32[]{:S(2)}, u32[]{:S(2)}) %collective-permute-start.1) | collective-permute-done | bytes 131104 | tf_op jit(solution)/shard_map/ppermute | solution.py:231
  46.3 0.0 collective-permute-done.2.refs_3_
  46.4 1.6 %collective-permute-start.3 = (f32[4,32,128]{2,1,0:T(8,128)S(1)}, f32[4,32,128]{2,1,0:T(8,128)S(1)}, u32[]{:S(2)}, u32[]{:S(2)}) collective-permute-start(f32[4,32,128]{2,1,0:T(8,128)S(1)} %get-tuple-element.40), channel_id=1, source_target_pairs={{0,1},{1,0},{2,3},{3,2},{4,5},{5,4},{6,7},{7,6},{8,9},{9,8},{10,11... | collective-permute-start | bytes 196616 | tf_op jit(solution)/shard_map/ppermute | solution.py:231
  48.0 0.0 collective-permute-start.4
  48.0 0.1 compare_select_fusion
  48.1 0.7 collective-permute-start.5
  48.7 1.5 %collective-permute-start.6 = (f32[4,32,128]{2,1,0:T(8,128)S(1)}, f32[4,32,128]{2,1,0:T(8,128)S(1)}, u32[]{:S(2)}, u32[]{:S(2)}) collective-permute-start(f32[4,32,128]{2,1,0:T(8,128)S(1)} %get-tuple-element.43), channel_id=1, source_target_pairs={{0,4},{1,5},{2,6},{3,7},{4,0},{5,1},{6,2},{7,3},{8,12},{9,13},{10,... | collective-permute-start | bytes 196616 | tf_op jit(solution)/shard_map/ppermute | solution.py:231
  50.2 1.5 %collective-permute-start.7 = (f32[4,32,128]{2,1,0:T(8,128)S(1)}, f32[4,32,128]{2,1,0:T(8,128)S(1)}, u32[]{:S(2)}, u32[]{:S(2)}) collective-permute-start(f32[4,32,128]{2,1,0:T(8,128)S(1)} %get-tuple-element.44), channel_id=1, source_target_pairs={{0,5},{1,4},{2,7},{3,6},{4,1},{5,0},{6,3},{7,2},{8,13},{9,12},{10,... | collective-permute-start | bytes 196616 | tf_op jit(solution)/shard_map/ppermute | solution.py:231
  51.7 0.0 collective-permute-done.3.refs_1_
  51.7 0.5 collective-permute-start.8
  52.2 1.8 %collective-permute-start.9 = (f32[4,32,128]{2,1,0:T(8,128)S(1)}, f32[4,32,128]{2,1,0:T(8,128)S(1)}, u32[]{:S(2)}, u32[]{:S(2)}) collective-permute-start(f32[4,32,128]{2,1,0:T(8,128)S(1)} %get-tuple-element.46), channel_id=1, source_target_pairs={{0,7},{1,6},{2,5},{3,4},{4,3},{5,2},{6,1},{7,0},{8,15},{9,14},{10,... | collective-permute-start | bytes 196616 | tf_op jit(solution)/shard_map/ppermute | solution.py:231
  54.0 0.0 collective-permute-done.5.refs_3_
  54.1 1.4 %collective-permute-done.7.refs_5_ = f32[4,32,128]{2,1,0:T(8,128)S(1)} collective-permute-done((f32[4,32,128]{2,1,0:T(8,128)S(1)}, f32[4,32,128]{2,1,0:T(8,128)S(1)}, u32[]{:S(2)}, u32[]{:S(2)}) %collective-permute-start.7) | collective-permute-done | bytes 65568 | tf_op jit(solution)/shard_map/ppermute | solution.py:231
  55.5 0.7 collective-permute-done.8.refs_6_
  56.1 1.5 %collective-permute-done.9.refs_7_ = f32[4,32,128]{2,1,0:T(8,128)S(1)} collective-permute-done((f32[4,32,128]{2,1,0:T(8,128)S(1)}, f32[4,32,128]{2,1,0:T(8,128)S(1)}, u32[]{:S(2)}, u32[]{:S(2)}) %collective-permute-start.9) | collective-permute-done | bytes 65568 | tf_op jit(solution)/shard_map/ppermute | solution.py:231
  57.6 0.5 shard_map.40
  58.1 0.0 all-to-all-done.seen_ref
  58.1 1.5 %shard_map.45 = f32[32,2,16,128]{3,2,1,0:T(8,128)} custom-call(f32[32,2,32,128]{3,2,1,0:T(8,128)S(1)} %all-to-all-done.seen_ref, f32[32,32,128]{2,1,0:T(8,128)S(1)} %get-tuple-element.47.cos_ref, f32[32,32,128]{2,1,0:T(8,128)S(1)} %get-tuple-element.48.sin_ref, bf16[256,128]{1,0:T(8,128)(2,1)S(1)} %pad_maximum_fusion.right_ref, ...), custom_call_target="tpu_custom_call" | custom-call | tf_op jit(solution)/shard_map/pallas_call | solution.py:319
  59.6 4.5 %all-to-all-start.1 = ((f32[32,2,16,128]{3,2,1,0:T(8,128)}), f32[32,2,16,128]{3,2,1,0:T(8,128)S(1)}, u32[]{:S(2)}, u32[]{:S(2)}) async-start(f32[32,2,16,128]{3,2,1,0:T(8,128)} %shard_map.45), calls=%async_computation.1 | async-start | bytes 1048576 | tf_op jit(solution)/shard_map/all_to_all | solution.py:323
  64.1 0.3 shard_map.41
  64.4 1.8 %collective-permute-start.10 = (f32[8,2,16,128]{3,2,1,0:T(8,128)S(1)}, f32[8,2,16,128]{3,2,1,0:T(8,128)S(1)}, u32[]{:S(2)}, u32[]{:S(2)}) collective-permute-start(f32[8,2,16,128]{3,2,1,0:T(8,128)S(1)} %get-tuple-element.50), channel_id=1, source_target_pairs={{0,8},{1,9},{2,10},{3,11},{4,12},{5,13},{6,14},{7,15},{8,0},{9,1},... | collective-permute-start | bytes 393224 | tf_op jit(solution)/shard_map/ppermute | solution.py:231
  66.2 2.4 %collective-permute-start.11 = (f32[8,2,16,128]{3,2,1,0:T(8,128)S(1)}, f32[8,2,16,128]{3,2,1,0:T(8,128)S(1)}, u32[]{:S(2)}, u32[]{:S(2)}) collective-permute-start(f32[8,2,16,128]{3,2,1,0:T(8,128)S(1)} %get-tuple-element.51), channel_id=1, source_target_pairs={{0,16},{1,17},{2,18},{3,19},{4,20},{5,21},{6,22},{7,23},{8,24},{9,... | collective-permute-start | bytes 393224 | tf_op jit(solution)/shard_map/ppermute | solution.py:231
  68.6 0.2 collective-permute-start.12
  68.8 8.3 %collective-permute-done.10.refs_1_ = f32[8,2,16,128]{3,2,1,0:T(8,128)S(1)} collective-permute-done((f32[8,2,16,128]{3,2,1,0:T(8,128)S(1)}, f32[8,2,16,128]{3,2,1,0:T(8,128)S(1)}, u32[]{:S(2)}, u32[]{:S(2)}) %collective-permute-start.10) | collective-permute-done | bytes 131104 | tf_op jit(solution)/shard_map/ppermute | solution.py:231
  77.1 11.0 %collective-permute-done.11.refs_2_ = f32[8,2,16,128]{3,2,1,0:T(8,128)S(1)} collective-permute-done((f32[8,2,16,128]{3,2,1,0:T(8,128)S(1)}, f32[8,2,16,128]{3,2,1,0:T(8,128)S(1)}, u32[]{:S(2)}, u32[]{:S(2)}) %collective-permute-start.11) | collective-permute-done | bytes 131104 | tf_op jit(solution)/shard_map/ppermute | solution.py:231
  88.1 1.5 %collective-permute-start.17 = (f32[4,2,16,128]{3,2,1,0:T(8,128)S(1)}, f32[4,2,16,128]{3,2,1,0:T(8,128)S(1)}, u32[]{:S(2)}, u32[]{:S(2)}) collective-permute-start(f32[4,2,16,128]{3,2,1,0:T(8,128)S(1)} %get-tuple-element.58), channel_id=1, source_target_pairs={{0,4},{1,5},{2,6},{3,7},{4,0},{5,1},{6,2},{7,3},{8,12},{9,13},{10,... | collective-permute-start | bytes 196616 | tf_op jit(solution)/shard_map/ppermute | solution.py:231
  89.6 1.5 %collective-permute-start.18 = (f32[4,2,16,128]{3,2,1,0:T(8,128)S(1)}, f32[4,2,16,128]{3,2,1,0:T(8,128)S(1)}, u32[]{:S(2)}, u32[]{:S(2)}) collective-permute-start(f32[4,2,16,128]{3,2,1,0:T(8,128)S(1)} %get-tuple-element.59), channel_id=1, source_target_pairs={{0,1},{1,0},{2,3},{3,2},{4,5},{5,4},{6,7},{7,6},{8,9},{9,8},{10,11... | collective-permute-start | bytes 196616 | tf_op jit(solution)/shard_map/ppermute | solution.py:231
  91.1 0.0 collective-permute-start.13
  91.1 0.8 collective-permute-start.14
  91.9 2.4 %collective-permute-start.19 = (f32[4,2,16,128]{3,2,1,0:T(8,128)S(1)}, f32[4,2,16,128]{3,2,1,0:T(8,128)S(1)}, u32[]{:S(2)}, u32[]{:S(2)}) collective-permute-start(f32[4,2,16,128]{3,2,1,0:T(8,128)S(1)} %get-tuple-element.60), channel_id=1, source_target_pairs={{0,5},{1,4},{2,7},{3,6},{4,1},{5,0},{6,3},{7,2},{8,13},{9,12},{10,... | collective-permute-start | bytes 196616 | tf_op jit(solution)/shard_map/ppermute | solution.py:231
  94.3 0.8 collective-permute-start.16
  95.1 2.0 %collective-permute-done.19.refs_3_ = f32[4,2,16,128]{3,2,1,0:T(8,128)S(1)} collective-permute-done((f32[4,2,16,128]{3,2,1,0:T(8,128)S(1)}, f32[4,2,16,128]{3,2,1,0:T(8,128)S(1)}, u32[]{:S(2)}, u32[]{:S(2)}) %collective-permute-start.19) | collective-permute-done | bytes 65568 | tf_op jit(solution)/shard_map/ppermute | solution.py:231
  97.1 0.4 shard_map.43.refs_4_
  97.5 0.0 collective-permute-done.13.refs_0_
  97.5 1.4 %collective-permute-done.15.refs_2_ = f32[4,2,16,128]{3,2,1,0:T(8,128)S(1)} collective-permute-done((f32[4,2,16,128]{3,2,1,0:T(8,128)S(1)}, f32[4,2,16,128]{3,2,1,0:T(8,128)S(1)}, u32[]{:S(2)}, u32[]{:S(2)}) %collective-permute-start.15) | collective-permute-done | bytes 65568 | tf_op jit(solution)/shard_map/ppermute | solution.py:231
  98.9 0.0 collective-permute-done.16.refs_3_
  98.9 0.4 shard_map.44.few_ref
  99.4 0.0 all-to-all-done.1.most_ref
  99.4 1.1 %shard_map.46 = f32[2,1024,128]{2,1,0:T(8,128)} custom-call(f32[32,2,16,128]{3,2,1,0:T(8,128)S(1)} %shard_map.44.few_ref, f32[32,2,16,128]{3,2,1,0:T(8,128)S(1)} %all-to-all-done.1.most_ref), custom_call_target="tpu_custom_call" | custom-call | tf_op jit(solution)/shard_map/pallas_call | solution.py:341
  (16 shorter events, 0.2 us)
Async XLA Ops:
  3.8 54.3 %all-to-all-start = ((f32[32,2,32,128]{3,2,1,0:T(8,128)}), f32[32,2,32,128]{3,2,1,0:T(8,128)S(1)}, u32[]{:S(2)}, u32[]{:S(2)}) async-start(f32[32,2,32,128]{3,2,1,0:T(8,128)} %shard_map.38), calls=%async_computation | async-start | bytes 2097152 | tf_op jit(solution)/shard_map/all_to_all | solution.py:298
  11.1 20.7 %collective-permute-start = (f32[8,32,128]{2,1,0:T(8,128)S(1)}, f32[8,32,128]{2,1,0:T(8,128)S(1)}, u32[]{:S(2)}, u32[]{:S(2)}) collective-permute-start(f32[8,32,128]{2,1,0:T(8,128)S(1)} %get-tuple-element.36), channel_id=1, source_target_pairs={{0,8},{1,9},{2,10},{3,11},{4,12},{5,13},{6,14},{7,15},{8,0},{9,1},... | collective-permute-start | bytes 393224 | tf_op jit(solution)/shard_map/ppermute | solution.py:231
  13.0 33.4 %collective-permute-start.1 = (f32[8,32,128]{2,1,0:T(8,128)S(1)}, f32[8,32,128]{2,1,0:T(8,128)S(1)}, u32[]{:S(2)}, u32[]{:S(2)}) collective-permute-start(f32[8,32,128]{2,1,0:T(8,128)S(1)} %get-tuple-element.37), channel_id=1, source_target_pairs={{0,16},{1,17},{2,18},{3,19},{4,20},{5,21},{6,22},{7,23},{8,24},{9,... | collective-permute-start | bytes 393224 | tf_op jit(solution)/shard_map/ppermute | solution.py:231
  15.4 31.0 %collective-permute-start.2 = (f32[8,32,128]{2,1,0:T(8,128)S(1)}, f32[8,32,128]{2,1,0:T(8,128)S(1)}, u32[]{:S(2)}, u32[]{:S(2)}) collective-permute-start(f32[8,32,128]{2,1,0:T(8,128)S(1)} %get-tuple-element.38), channel_id=1, source_target_pairs={{0,24},{1,25},{2,26},{3,27},{4,28},{5,29},{6,30},{7,31},{8,16},{9,... | collective-permute-start | bytes 393224 | tf_op jit(solution)/shard_map/ppermute | solution.py:231
  46.4 5.4 %collective-permute-start.3 = (f32[4,32,128]{2,1,0:T(8,128)S(1)}, f32[4,32,128]{2,1,0:T(8,128)S(1)}, u32[]{:S(2)}, u32[]{:S(2)}) collective-permute-start(f32[4,32,128]{2,1,0:T(8,128)S(1)} %get-tuple-element.40), channel_id=1, source_target_pairs={{0,1},{1,0},{2,3},{3,2},{4,5},{5,4},{6,7},{7,6},{8,9},{9,8},{10,11... | collective-permute-start | bytes 196616 | tf_op jit(solution)/shard_map/ppermute | solution.py:231
  48.0 4.2 %collective-permute-start.4 = (f32[4,32,128]{2,1,0:T(8,128)S(1)}, f32[4,32,128]{2,1,0:T(8,128)S(1)}, u32[]{:S(2)}, u32[]{:S(2)}) collective-permute-start(f32[4,32,128]{2,1,0:T(8,128)S(1)} %get-tuple-element.41), channel_id=1, source_target_pairs={{0,2},{1,3},{2,0},{3,1},{4,6},{5,7},{6,4},{7,5},{8,10},{9,11},{10,... | collective-permute-start | bytes 196616 | tf_op jit(solution)/shard_map/ppermute | solution.py:231
  48.1 6.0 %collective-permute-start.5 = (f32[4,32,128]{2,1,0:T(8,128)S(1)}, f32[4,32,128]{2,1,0:T(8,128)S(1)}, u32[]{:S(2)}, u32[]{:S(2)}) collective-permute-start(f32[4,32,128]{2,1,0:T(8,128)S(1)} %get-tuple-element.42), channel_id=1, source_target_pairs={{0,3},{1,2},{2,1},{3,0},{4,7},{5,6},{6,5},{7,4},{8,11},{9,10},{10,... | collective-permute-start | bytes 196616 | tf_op jit(solution)/shard_map/ppermute | solution.py:231
  48.7 5.3 %collective-permute-start.6 = (f32[4,32,128]{2,1,0:T(8,128)S(1)}, f32[4,32,128]{2,1,0:T(8,128)S(1)}, u32[]{:S(2)}, u32[]{:S(2)}) collective-permute-start(f32[4,32,128]{2,1,0:T(8,128)S(1)} %get-tuple-element.43), channel_id=1, source_target_pairs={{0,4},{1,5},{2,6},{3,7},{4,0},{5,1},{6,2},{7,3},{8,12},{9,13},{10,... | collective-permute-start | bytes 196616 | tf_op jit(solution)/shard_map/ppermute | solution.py:231
  50.2 5.3 %collective-permute-start.7 = (f32[4,32,128]{2,1,0:T(8,128)S(1)}, f32[4,32,128]{2,1,0:T(8,128)S(1)}, u32[]{:S(2)}, u32[]{:S(2)}) collective-permute-start(f32[4,32,128]{2,1,0:T(8,128)S(1)} %get-tuple-element.44), channel_id=1, source_target_pairs={{0,5},{1,4},{2,7},{3,6},{4,1},{5,0},{6,3},{7,2},{8,13},{9,12},{10,... | collective-permute-start | bytes 196616 | tf_op jit(solution)/shard_map/ppermute | solution.py:231
  51.7 4.4 %collective-permute-start.8 = (f32[4,32,128]{2,1,0:T(8,128)S(1)}, f32[4,32,128]{2,1,0:T(8,128)S(1)}, u32[]{:S(2)}, u32[]{:S(2)}) collective-permute-start(f32[4,32,128]{2,1,0:T(8,128)S(1)} %get-tuple-element.45), channel_id=1, source_target_pairs={{0,6},{1,7},{2,4},{3,5},{4,2},{5,3},{6,0},{7,1},{8,14},{9,15},{10,... | collective-permute-start | bytes 196616 | tf_op jit(solution)/shard_map/ppermute | solution.py:231
  52.2 5.4 %collective-permute-start.9 = (f32[4,32,128]{2,1,0:T(8,128)S(1)}, f32[4,32,128]{2,1,0:T(8,128)S(1)}, u32[]{:S(2)}, u32[]{:S(2)}) collective-permute-start(f32[4,32,128]{2,1,0:T(8,128)S(1)} %get-tuple-element.46), channel_id=1, source_target_pairs={{0,7},{1,6},{2,5},{3,4},{4,3},{5,2},{6,1},{7,0},{8,15},{9,14},{10,... | collective-permute-start | bytes 196616 | tf_op jit(solution)/shard_map/ppermute | solution.py:231
  59.6 39.8 %all-to-all-start.1 = ((f32[32,2,16,128]{3,2,1,0:T(8,128)}), f32[32,2,16,128]{3,2,1,0:T(8,128)S(1)}, u32[]{:S(2)}, u32[]{:S(2)}) async-start(f32[32,2,16,128]{3,2,1,0:T(8,128)} %shard_map.45), calls=%async_computation.1 | async-start | bytes 1048576 | tf_op jit(solution)/shard_map/all_to_all | solution.py:323
  64.4 12.7 %collective-permute-start.10 = (f32[8,2,16,128]{3,2,1,0:T(8,128)S(1)}, f32[8,2,16,128]{3,2,1,0:T(8,128)S(1)}, u32[]{:S(2)}, u32[]{:S(2)}) collective-permute-start(f32[8,2,16,128]{3,2,1,0:T(8,128)S(1)} %get-tuple-element.50), channel_id=1, source_target_pairs={{0,8},{1,9},{2,10},{3,11},{4,12},{5,13},{6,14},{7,15},{8,0},{9,1},... | collective-permute-start | bytes 393224 | tf_op jit(solution)/shard_map/ppermute | solution.py:231
  66.2 21.9 %collective-permute-start.11 = (f32[8,2,16,128]{3,2,1,0:T(8,128)S(1)}, f32[8,2,16,128]{3,2,1,0:T(8,128)S(1)}, u32[]{:S(2)}, u32[]{:S(2)}) collective-permute-start(f32[8,2,16,128]{3,2,1,0:T(8,128)S(1)} %get-tuple-element.51), channel_id=1, source_target_pairs={{0,16},{1,17},{2,18},{3,19},{4,20},{5,21},{6,22},{7,23},{8,24},{9,... | collective-permute-start | bytes 393224 | tf_op jit(solution)/shard_map/ppermute | solution.py:231
  68.6 19.5 %collective-permute-start.12 = (f32[8,2,16,128]{3,2,1,0:T(8,128)S(1)}, f32[8,2,16,128]{3,2,1,0:T(8,128)S(1)}, u32[]{:S(2)}, u32[]{:S(2)}) collective-permute-start(f32[8,2,16,128]{3,2,1,0:T(8,128)S(1)} %get-tuple-element.52), channel_id=1, source_target_pairs={{0,24},{1,25},{2,26},{3,27},{4,28},{5,29},{6,30},{7,31},{8,16},{9,... | collective-permute-start | bytes 393224 | tf_op jit(solution)/shard_map/ppermute | solution.py:231
  88.1 6.2 %collective-permute-start.17 = (f32[4,2,16,128]{3,2,1,0:T(8,128)S(1)}, f32[4,2,16,128]{3,2,1,0:T(8,128)S(1)}, u32[]{:S(2)}, u32[]{:S(2)}) collective-permute-start(f32[4,2,16,128]{3,2,1,0:T(8,128)S(1)} %get-tuple-element.58), channel_id=1, source_target_pairs={{0,4},{1,5},{2,6},{3,7},{4,0},{5,1},{6,2},{7,3},{8,12},{9,13},{10,... | collective-permute-start | bytes 196616 | tf_op jit(solution)/shard_map/ppermute | solution.py:231
  89.6 4.7 %collective-permute-start.18 = (f32[4,2,16,128]{3,2,1,0:T(8,128)S(1)}, f32[4,2,16,128]{3,2,1,0:T(8,128)S(1)}, u32[]{:S(2)}, u32[]{:S(2)}) collective-permute-start(f32[4,2,16,128]{3,2,1,0:T(8,128)S(1)} %get-tuple-element.59), channel_id=1, source_target_pairs={{0,1},{1,0},{2,3},{3,2},{4,5},{5,4},{6,7},{7,6},{8,9},{9,8},{10,11... | collective-permute-start | bytes 196616 | tf_op jit(solution)/shard_map/ppermute | solution.py:231
  91.1 6.4 %collective-permute-start.13 = (f32[4,2,16,128]{3,2,1,0:T(8,128)S(1)}, f32[4,2,16,128]{3,2,1,0:T(8,128)S(1)}, u32[]{:S(2)}, u32[]{:S(2)}) collective-permute-start(f32[4,2,16,128]{3,2,1,0:T(8,128)S(1)} %get-tuple-element.53), channel_id=1, source_target_pairs={{0,6},{1,7},{2,4},{3,5},{4,2},{5,3},{6,0},{7,1},{8,14},{9,15},{10,... | collective-permute-start | bytes 196616 | tf_op jit(solution)/shard_map/ppermute | solution.py:231
  91.1 6.4 %collective-permute-start.14 = (f32[4,2,16,128]{3,2,1,0:T(8,128)S(1)}, f32[4,2,16,128]{3,2,1,0:T(8,128)S(1)}, u32[]{:S(2)}, u32[]{:S(2)}) collective-permute-start(f32[4,2,16,128]{3,2,1,0:T(8,128)S(1)} %get-tuple-element.54), channel_id=1, source_target_pairs={{0,3},{1,2},{2,1},{3,0},{4,7},{5,6},{6,5},{7,4},{8,11},{9,10},{10,... | collective-permute-start | bytes 196616 | tf_op jit(solution)/shard_map/ppermute | solution.py:231
  91.9 5.2 %collective-permute-start.19 = (f32[4,2,16,128]{3,2,1,0:T(8,128)S(1)}, f32[4,2,16,128]{3,2,1,0:T(8,128)S(1)}, u32[]{:S(2)}, u32[]{:S(2)}) collective-permute-start(f32[4,2,16,128]{3,2,1,0:T(8,128)S(1)} %get-tuple-element.60), channel_id=1, source_target_pairs={{0,5},{1,4},{2,7},{3,6},{4,1},{5,0},{6,3},{7,2},{8,13},{9,12},{10,... | collective-permute-start | bytes 196616 | tf_op jit(solution)/shard_map/ppermute | solution.py:231
  94.3 4.6 %collective-permute-start.15 = (f32[4,2,16,128]{3,2,1,0:T(8,128)S(1)}, f32[4,2,16,128]{3,2,1,0:T(8,128)S(1)}, u32[]{:S(2)}, u32[]{:S(2)}) collective-permute-start(f32[4,2,16,128]{3,2,1,0:T(8,128)S(1)} %get-tuple-element.55), channel_id=1, source_target_pairs={{0,7},{1,6},{2,5},{3,4},{4,3},{5,2},{6,1},{7,0},{8,15},{9,14},{10,... | collective-permute-start | bytes 196616 | tf_op jit(solution)/shard_map/ppermute | solution.py:231
  94.3 4.6 %collective-permute-start.16 = (f32[4,2,16,128]{3,2,1,0:T(8,128)S(1)}, f32[4,2,16,128]{3,2,1,0:T(8,128)S(1)}, u32[]{:S(2)}, u32[]{:S(2)}) collective-permute-start(f32[4,2,16,128]{3,2,1,0:T(8,128)S(1)} %get-tuple-element.56), channel_id=1, source_target_pairs={{0,2},{1,3},{2,0},{3,1},{4,6},{5,7},{6,4},{7,5},{8,10},{9,11},{10,... | collective-permute-start | bytes 196616 | tf_op jit(solution)/shard_map/ppermute | solution.py:231
